TPU v7x, 256 devices: a whole 4x4x8 slice. The times are simulated.
256 devices in a mesh: rows: 16 (over y, x_lo, core), cols: 4 (over z_1, x_hi), slabs: 2 (over z_0), trial: 2 (over z_2).
Axes of the slice: x: 4 (x_hi: 2, x_lo: 2; x = x_hi * 2 + x_lo), y: 4, z: 8 (z_0: 2, z_1: 2, z_2: 2; z = z_0 * 4 + z_1 * 2 + z_2), core: 2. Of those that a mesh axis runs over, the one named last changes fastest.
Arguments:
- field_values: float32 [256, 64, 128, 128], P(('trial', 'rows'), 'cols', 'slabs'), parts along dimension 0, may hold values from 0.2 to 1.8
- crowding: float32 [256, 64, 128, 128], P(('trial', 'rows'), 'cols', 'slabs'), parts along dimension 0, may hold values from 0.5 to 2
Outputs:
- potential: float32 [256, 64, 128, 128], P(('trial', 'rows'), 'cols', 'slabs'), parts along dimension 0
- field_values_end: float32 [256, 64, 128, 128], P(('trial', 'rows'), 'cols', 'slabs'), parts along dimension 0
There are 2 independent parts, one for each index of `trial`. A program takes and returns all parts, laid end to end along the dimension named above; each array names one. Nothing has to cross between parts.
All inputs are finite; a program needn't handle non-finite values.
Results may differ from a plain program's by a relative error of at most 0.00002.
Values sent between devices are 32-bit elements; how exact they have to be, the bound alone decides.
No kernel may reach another device: no remote copies, remote signals or barrier semaphores. Data moves between devices by JAX's collectives and lax.ppermute only.
A program may use at most 64 MiB of HBM per device.

v0:
```python
import jax
import jax.numpy as jnp
from jax import lax
from jax.sharding import PartitionSpec as P

STEPS = 3


def with_halo(shard, sides, width):
    edges = {}
    for axis, dim in sides:
        devices, length = (lax.axis_size(axis), shard.shape[dim])
        up = [(i, (i + 1) % devices) for i in range(devices - 1)]
        last = lax.slice_in_dim(shard, length - width, length, axis=dim)
        initial = lax.slice_in_dim(shard, 0, width, axis=dim)
        edges[dim] = (
            lax.ppermute(last, axis, up),
            lax.ppermute(initial, axis, [(b, a) for a, b in up]),
        )
    done = []
    for _, dim in sides:
        low, high = edges[dim]
        around = [(width, width) if d in done else (0, 0) for d in range(shard.ndim)]
        shard = jnp.concatenate([jnp.pad(low, around), shard, jnp.pad(high, around)], axis=dim)
        done.append(dim)
    return shard


def entering(part, axis, combine, identity):
    place = lax.axis_index(axis)
    gathered = lax.all_gather(part, axis)
    state = jnp.zeros_like(part) + jnp.asarray(identity, part.dtype)

    def one(lap, state):
        return combine(state, lax.dynamic_index_in_dim(gathered, lap, 0, False))

    return lax.fori_loop(0, place, one, state)


def without_rim(values, dims):
    for dim in dims:
        values = lax.slice_in_dim(values, 1, values.shape[dim] - 1, axis=dim)
    return values


def shifted_cells(values, dim, start, dims):
    others = [other for other in dims if other != dim]
    values = without_rim(values, others)
    return lax.slice_in_dim(values, start, start + values.shape[dim] - 2, axis=dim)


def march_step(padded, crowding):
    middle = without_rim(padded, (0, 1, 2))
    lower = [shifted_cells(padded, dim, 0, (0, 1, 2)) for dim in (0, 1, 2)]
    upper = [shifted_cells(padded, dim, 2, (0, 1, 2)) for dim in (0, 1, 2)]
    spread = lower[0] + upper[0] + lower[1] + upper[1] + lower[2] + upper[2] - 6.0 * middle
    return middle + 0.1 * spread + 0.2 * middle * (1.0 - middle * crowding)


def on_device(field_values, crowding):
    for step in range(STEPS):
        padded = with_halo(field_values, (("rows", 0), ("cols", 1), ("slabs", 2)), 1)
        field_values = march_step(padded, crowding)
    here = jnp.cumsum(field_values, axis=0)
    total = lax.slice_in_dim(here, here.shape[0] - 1, here.shape[0], axis=0)

    def add_pair(earlier_total, later_total):
        return earlier_total + later_total

    below = entering(total, "rows", add_pair, jnp.zeros_like(total))
    potential = (here + below) / (field_values.shape[0] * lax.axis_size("rows"))
    return (potential, field_values)


def solution(mesh):
    in_specs = (
        P(("trial", "rows"), "cols", "slabs", None),
        P(("trial", "rows"), "cols", "slabs", None),
    )
    out_specs = (
        P(("trial", "rows"), "cols", "slabs", None),
        P(("trial", "rows"), "cols", "slabs", None),
    )
    return jax.shard_map(
        on_device, mesh=mesh, in_specs=in_specs, out_specs=out_specs, check_vma=False
    )
```

profile of v0, /device:TPU:27, one launch (start us, length us, event | category | flops | bytes accessed | tf_op | source)
XLA Modules:
  0.0 234.8 jit_solution(14719574178035145743)
XLA Ops:
  7.2 0.0 all-gather.3.cloned.1.call-start
  7.2 0.0 copy-start.1
  7.2 1.4 fusion.41
  8.6 1.4 collective-permute-start
  10.1 1.1 fusion.40
  11.2 3.8 %collective-permute-start.2 = (f32[8,1,64,128]{3,2,1,0:T(8,128)S(1)}, f32[8,1,64,128]{3,2,1,0:T(8,128)S(1)}, u32[]{:S(2)}, u32[]{:S(2)}) collective-permute-start(f32[8,1,64,128]{3,2,1,0:T(8,128)S(1)} %get-tuple-element.56), channel_id=1, source_target_pairs={{0,4},{4,8},{8,12},{1,5},{5,9},{9,13},{2,6},{6,10},{10,14},{3,7},{... | collective-permute-start | bytes 786440 | tf_op jit(solution)/shard_map/ppermute | solution.py:17
  14.9 1.3 collective-permute-start.3
  16.2 3.5 %collective-permute-start.1 = (f32[1,16,64,128]{3,2,1,0:T(8,128)S(1)}, f32[1,16,64,128]{3,2,1,0:T(8,128)S(1)}, u32[]{:S(2)}, u32[]{:S(2)}) collective-permute-start(f32[1,16,64,128]{3,2,1,0:T(8,128)S(1)} %get-tuple-element.58), channel_id=1, source_target_pairs={{16,0},{32,16},{48,32},{64,48},{80,64},{96,80},{112,96},{128,112},... | collective-permute-start | bytes 1572872 | tf_op jit(solution)/shard_map/ppermute | solution.py:18
  19.8 1.3 fusion.39
  21.1 8.8 %collective-permute-start.4 = (f32[8,16,1,128]{3,2,1,0:T(1,128)S(1)}, f32[8,16,1,128]{3,2,1,0:T(1,128)S(1)}, u32[]{:S(2)}, u32[]{:S(2)}) collective-permute-start(f32[8,16,1,128]{3,2,1,0:T(1,128)S(1)} %get-tuple-element.54), channel_id=1, source_target_pairs={{0,2},{1,3},{4,6},{5,7},{8,10},{9,11},{12,14},{13,15},{16,18},{17,... | collective-permute-start | bytes 196616 | tf_op jit(solution)/shard_map/ppermute | solution.py:17
  29.9 0.0 collective-permute-done.2
  29.9 1.3 collective-permute-start.5
  31.3 0.0 copy-start
  31.4 0.6 constant_dynamic-update-slice_fusion.1
  32.0 2.4 %copy-done.4 = f32[10,16,64,128]{3,2,1,0:T(8,128)} copy-done((f32[10,16,64,128]{3,2,1,0:T(8,128)}, f32[10,16,64,128]{3,2,1,0:T(8,128)S(1)}, u32[]{:S(2)}) %copy-start.4) | copy-done | bytes 5242904
  34.5 4.4 %collective-permute-done.5 = f32[8,16,1,128]{3,2,1,0:T(1,128)S(1)} collective-permute-done((f32[8,16,1,128]{3,2,1,0:T(1,128)S(1)}, f32[8,16,1,128]{3,2,1,0:T(1,128)S(1)}, u32[]{:S(2)}, u32[]{:S(2)}) %collective-permute-start.5) | collective-permute-done | bytes 65568 | tf_op jit(solution)/shard_map/ppermute | solution.py:18
  38.8 12.1 %fusion.27 = f32[8,16,64,128]{3,2,1,0:T(8,128)S(1)} fusion(f32[8,16,64,128]{3,2,1,0:T(8,128)S(1)} %copy-done.1, f32[8,16,1,128]{3,2,1,0:T(1,128)S(1)} %collective-permute-done.5, f32[10,1,64,128]{3,2,1,0:T(8,128)S(1)} %pad.39, f32[10,16,64,128]{3,2,1,0:T(8,128)} %copy-done.4, f32[10,1,64,128]{3,2,1,0:T(8,128)S(1)} %pad.38, ...), kind=kLoop, calls=%fused_computation.65 | loop fusion | flops 31457280 | bytes 19660800 | tf_op jit(solution)/shard_map/add | solution.py:57
  50.9 0.1 fusion.37
  51.0 1.3 collective-permute-start.6
  52.3 6.4 %collective-permute-start.7 = (f32[1,16,64,128]{3,2,1,0:T(8,128)S(1)}, f32[1,16,64,128]{3,2,1,0:T(8,128)S(1)}, u32[]{:S(2)}, u32[]{:S(2)}) collective-permute-start(f32[1,16,64,128]{3,2,1,0:T(8,128)S(1)} %get-tuple-element.51), channel_id=1, source_target_pairs={{16,0},{32,16},{48,32},{64,48},{80,64},{96,80},{112,96},{128,112},... | collective-permute-start | bytes 1572872 | tf_op jit(solution)/shard_map/ppermute | solution.py:18
  58.7 4.6 %collective-permute-start.8 = (f32[8,1,64,128]{3,2,1,0:T(8,128)S(1)}, f32[8,1,64,128]{3,2,1,0:T(8,128)S(1)}, u32[]{:S(2)}, u32[]{:S(2)}) collective-permute-start(f32[8,1,64,128]{3,2,1,0:T(8,128)S(1)} %get-tuple-element.52), channel_id=1, source_target_pairs={{0,4},{4,8},{8,12},{1,5},{5,9},{9,13},{2,6},{6,10},{10,14},{3,7},{... | collective-permute-start | bytes 786440 | tf_op jit(solution)/shard_map/ppermute | solution.py:17
  63.3 1.3 collective-permute-start.9
  64.6 0.1 fusion.36
  64.7 4.0 %collective-permute-start.10 = (f32[8,16,1,128]{3,2,1,0:T(1,128)S(1)}, f32[8,16,1,128]{3,2,1,0:T(1,128)S(1)}, u32[]{:S(2)}, u32[]{:S(2)}) collective-permute-start(f32[8,16,1,128]{3,2,1,0:T(1,128)S(1)} %get-tuple-element.48), channel_id=1, source_target_pairs={{0,2},{1,3},{4,6},{5,7},{8,10},{9,11},{12,14},{13,15},{16,18},{17,... | collective-permute-start | bytes 196616 | tf_op jit(solution)/shard_map/ppermute | solution.py:17
  68.7 0.7 collective-permute-done.8
  69.4 1.3 collective-permute-start.11
  70.7 3.0 %collective-permute-done.9 = f32[8,1,64,128]{3,2,1,0:T(8,128)S(1)} collective-permute-done((f32[8,1,64,128]{3,2,1,0:T(8,128)S(1)}, f32[8,1,64,128]{3,2,1,0:T(8,128)S(1)}, u32[]{:S(2)}, u32[]{:S(2)}) %collective-permute-start.9) | collective-permute-done | bytes 262176 | tf_op jit(solution)/shard_map/ppermute | solution.py:18
  73.7 4.6 %collective-permute-done.11 = f32[8,16,1,128]{3,2,1,0:T(1,128)S(1)} collective-permute-done((f32[8,16,1,128]{3,2,1,0:T(1,128)S(1)}, f32[8,16,1,128]{3,2,1,0:T(1,128)S(1)}, u32[]{:S(2)}, u32[]{:S(2)}) %collective-permute-start.11) | collective-permute-done | bytes 65568 | tf_op jit(solution)/shard_map/ppermute | solution.py:18
  78.3 8.2 %fusion.16 = f32[8,16,64,128]{3,2,1,0:T(8,128)S(1)} fusion(f32[8,16,64,128]{3,2,1,0:T(8,128)S(1)} %fusion.27, f32[8,16,1,128]{3,2,1,0:T(1,128)S(1)} %collective-permute-done.11, f32[10,1,64,128]{3,2,1,0:T(8,128)S(1)} %pad.43, f32[10,1,64,128]{3,2,1,0:T(8,128)S(1)} %pad.42, f32[1,16,64,128]{3,2,1,0:T(8,128)S(1)} %collective-permute-done.7, ...), kind=kLoop, calls=%fused_computation.36 | loop fusion | flops 39845888 | bytes 14417920 | tf_op jit(solution)/shard_map/add | solution.py:57
  86.5 0.1 fusion.34
  86.6 1.3 collective-permute-start.12
  87.9 7.6 %collective-permute-start.13 = (f32[1,16,64,128]{3,2,1,0:T(8,128)S(1)}, f32[1,16,64,128]{3,2,1,0:T(8,128)S(1)}, u32[]{:S(2)}, u32[]{:S(2)}) collective-permute-start(f32[1,16,64,128]{3,2,1,0:T(8,128)S(1)} %get-tuple-element.45), channel_id=1, source_target_pairs={{16,0},{32,16},{48,32},{64,48},{80,64},{96,80},{112,96},{128,112},... | collective-permute-start | bytes 1572872 | tf_op jit(solution)/shard_map/ppermute | solution.py:18
  95.5 7.5 %collective-permute-start.14 = (f32[8,1,64,128]{3,2,1,0:T(8,128)S(1)}, f32[8,1,64,128]{3,2,1,0:T(8,128)S(1)}, u32[]{:S(2)}, u32[]{:S(2)}) collective-permute-start(f32[8,1,64,128]{3,2,1,0:T(8,128)S(1)} %get-tuple-element.46), channel_id=1, source_target_pairs={{0,4},{4,8},{8,12},{1,5},{5,9},{9,13},{2,6},{6,10},{10,14},{3,7},{... | collective-permute-start | bytes 786440 | tf_op jit(solution)/shard_map/ppermute | solution.py:17
  103.0 1.3 collective-permute-start.15
  104.3 0.1 fusion.33
  104.4 2.5 %collective-permute-start.16 = (f32[8,16,1,128]{3,2,1,0:T(1,128)S(1)}, f32[8,16,1,128]{3,2,1,0:T(1,128)S(1)}, u32[]{:S(2)}, u32[]{:S(2)}) collective-permute-start(f32[8,16,1,128]{3,2,1,0:T(1,128)S(1)} %get-tuple-element.42), channel_id=1, source_target_pairs={{0,2},{1,3},{4,6},{5,7},{8,10},{9,11},{12,14},{13,15},{16,18},{17,... | collective-permute-start | bytes 196616 | tf_op jit(solution)/shard_map/ppermute | solution.py:17
  106.9 1.3 collective-permute-start.17
  108.3 5.3 %collective-permute-done.15 = f32[8,1,64,128]{3,2,1,0:T(8,128)S(1)} collective-permute-done((f32[8,1,64,128]{3,2,1,0:T(8,128)S(1)}, f32[8,1,64,128]{3,2,1,0:T(8,128)S(1)}, u32[]{:S(2)}, u32[]{:S(2)}) %collective-permute-start.15) | collective-permute-done | bytes 262176 | tf_op jit(solution)/shard_map/ppermute | solution.py:18
  113.6 2.3 collective-permute-done.17
  115.9 8.1 %fusion.5 = f32[8,16,64,128]{3,2,1,0:T(8,128)S(1)} fusion(f32[8,16,64,128]{3,2,1,0:T(8,128)S(1)} %fusion.16, f32[8,16,1,128]{3,2,1,0:T(1,128)S(1)} %collective-permute-done.17, f32[10,1,64,128]{3,2,1,0:T(8,128)S(1)} %pad.47, f32[10,1,64,128]{3,2,1,0:T(8,128)S(1)} %pad.46, f32[1,16,64,128]{3,2,1,0:T(8,128)S(1)} %collective-permute-done.13, ...), kind=kLoop, calls=%fused_computation.7 | loop fusion | flops 39845888 | bytes 14417920 | tf_op jit(solution)/shard_map/add | solution.py:57
  124.0 0.0 copy-start.3
  124.0 5.4 %fusion.42 = f32[8,16,64,128]{3,2,1,0:T(8,128)S(1)} fusion(f32[8,16,64,128]{3,2,1,0:T(8,128)S(1)} %fusion.5), kind=kOutput, calls=%fused_computation.95 | output fusion | flops 7340032 | bytes 8388608 | tf_op jit(solution)/shard_map/jit(cumsum)/reduce_window_sum | solution.py:64
  129.4 0.0 copy-start.2
  129.5 2.0 copy-done.2
  131.5 0.9 slice.277
  132.3 0.0 all-gather.3.cloned.1.call-update
  132.4 72.4 %all-gather.3.cloned.1.call-done = f32[16,16,64,128]{3,2,1,0:T(8,128)} async-done(((f32[1,16,64,128]{3,2,1,0:T(8,128)}), f32[16,16,64,128]{3,2,1,0:T(8,128)}) %all-gather.3.cloned.1.call-update) | async-done | bytes 8388624 | tf_op jit(solution)/shard_map/all_gather | solution.py:31
  204.8 18.0 %while.10 = (s32[]{:T(128)}, f32[1,16,64,128]{3,2,1,0:T(8,128)S(1)}, s32[]{:T(128)}, f32[16,1,16,64,128]{4,3,2,1,0:T(8,128)}, s32[]{:T(128)}, /*index=5*/s32[]{:T(128)}, s32[]{:T(128)}) while((s32[]{:T(128)}, f32[1,16,64,128]{3,2,1,0:T(8,128)S(1)}, s32[]{:T(128)}, f32[16,1,16,64,128]{4,3,2,1,0:T(8,128)}, s32[]{:T(128)}, /*index=5*/s32[]{:T(128)}, ...), condition=%wide.region_2.3_spmd, body=%wide.region_1.2_spmd.sunk | while | flops 131077 | bytes 1572987 | solution.py:37
  204.8 1.2 bitcast_add_fusion.2
  206.0 1.2 bitcast_add_fusion.2
  207.2 1.2 bitcast_add_fusion.2
  208.4 1.2 bitcast_add_fusion.2
  209.6 1.2 bitcast_add_fusion.2
  210.8 1.2 bitcast_add_fusion.2
  212.0 1.2 bitcast_add_fusion.2
  213.2 1.2 bitcast_add_fusion.2
  214.4 1.2 bitcast_add_fusion.2
  215.6 1.2 bitcast_add_fusion.2
  216.8 1.2 bitcast_add_fusion.2
  218.0 1.2 bitcast_add_fusion.2
  219.2 1.2 bitcast_add_fusion.2
  220.4 1.2 bitcast_add_fusion.2
  221.6 1.2 bitcast_add_fusion.2
  222.8 5.1 %add_multiply_fusion = f32[8,16,64,128]{3,2,1,0:T(8,128)} fusion(f32[8,16,64,128]{3,2,1,0:T(8,128)} %copy-done.2, f32[16,64,128]{2,1,0:T(8,128)S(1)} %bitcast.9), kind=kLoop, calls=%fused_computation.82 | loop fusion | flops 2097152 | bytes 8912896 | tf_op jit(solution)/shard_map/div | solution.py:71
  (26 shorter events, 0.4 us)
Async XLA Ops:
  7.2 197.6 %all-gather.3.cloned.1.call-start = ((), (), s32[]{:S(2)}) async-start(), calls=%async_computation | async-start | bytes 8912896 | tf_op jit(solution)/shard_map/all_gather | solution.py:31
  7.2 24.1 %copy-start.1 = (f32[8,16,64,128]{3,2,1,0:T(8,128)S(1)}, f32[8,16,64,128]{3,2,1,0:T(8,128)}, u32[]{:S(2)}) copy-start(f32[8,16,64,128]{3,2,1,0:T(8,128)} %param.4) | copy-start | bytes 12582916
  8.6 22.6 %collective-permute-start = (f32[1,16,64,128]{3,2,1,0:T(8,128)S(1)}, f32[1,16,64,128]{3,2,1,0:T(8,128)S(1)}, u32[]{:S(2)}, u32[]{:S(2)}) collective-permute-start(f32[1,16,64,128]{3,2,1,0:T(8,128)S(1)} %get-tuple-element.59), channel_id=1, source_target_pairs={{0,16},{16,32},{32,48},{48,64},{64,80},{80,96},{96,112},{112,128},... | collective-permute-start | bytes 1572872 | tf_op jit(solution)/shard_map/ppermute | solution.py:17
  11.2 18.7 %collective-permute-start.2 = (f32[8,1,64,128]{3,2,1,0:T(8,128)S(1)}, f32[8,1,64,128]{3,2,1,0:T(8,128)S(1)}, u32[]{:S(2)}, u32[]{:S(2)}) collective-permute-start(f32[8,1,64,128]{3,2,1,0:T(8,128)S(1)} %get-tuple-element.56), channel_id=1, source_target_pairs={{0,4},{4,8},{8,12},{1,5},{5,9},{9,13},{2,6},{6,10},{10,14},{3,7},{... | collective-permute-start | bytes 786440 | tf_op jit(solution)/shard_map/ppermute | solution.py:17
  14.9 16.3 %collective-permute-start.3 = (f32[8,1,64,128]{3,2,1,0:T(8,128)S(1)}, f32[8,1,64,128]{3,2,1,0:T(8,128)S(1)}, u32[]{:S(2)}, u32[]{:S(2)}) collective-permute-start(f32[8,1,64,128]{3,2,1,0:T(8,128)S(1)} %get-tuple-element.57), channel_id=1, source_target_pairs={{4,0},{8,4},{12,8},{5,1},{9,5},{13,9},{6,2},{10,6},{14,10},{7,3},{... | collective-permute-start | bytes 786440 | tf_op jit(solution)/shard_map/ppermute | solution.py:18
  16.2 15.7 %collective-permute-start.1 = (f32[1,16,64,128]{3,2,1,0:T(8,128)S(1)}, f32[1,16,64,128]{3,2,1,0:T(8,128)S(1)}, u32[]{:S(2)}, u32[]{:S(2)}) collective-permute-start(f32[1,16,64,128]{3,2,1,0:T(8,128)S(1)} %get-tuple-element.58), channel_id=1, source_target_pairs={{16,0},{32,16},{48,32},{64,48},{80,64},{96,80},{112,96},{128,112},... | collective-permute-start | bytes 1572872 | tf_op jit(solution)/shard_map/ppermute | solution.py:18
  21.1 10.9 %collective-permute-start.4 = (f32[8,16,1,128]{3,2,1,0:T(1,128)S(1)}, f32[8,16,1,128]{3,2,1,0:T(1,128)S(1)}, u32[]{:S(2)}, u32[]{:S(2)}) collective-permute-start(f32[8,16,1,128]{3,2,1,0:T(1,128)S(1)} %get-tuple-element.54), channel_id=1, source_target_pairs={{0,2},{1,3},{4,6},{5,7},{8,10},{9,11},{12,14},{13,15},{16,18},{17,... | collective-permute-start | bytes 196616 | tf_op jit(solution)/shard_map/ppermute | solution.py:17
  29.9 8.9 %collective-permute-start.5 = (f32[8,16,1,128]{3,2,1,0:T(1,128)S(1)}, f32[8,16,1,128]{3,2,1,0:T(1,128)S(1)}, u32[]{:S(2)}, u32[]{:S(2)}) collective-permute-start(f32[8,16,1,128]{3,2,1,0:T(1,128)S(1)} %get-tuple-element.55), channel_id=1, source_target_pairs={{2,0},{3,1},{6,4},{7,5},{10,8},{11,9},{14,12},{15,13},{18,16},{19,... | collective-permute-start | bytes 196616 | tf_op jit(solution)/shard_map/ppermute | solution.py:18
  31.3 7.5 %copy-start = (f32[8,16,64,128]{3,2,1,0:T(8,128)S(1)}, f32[8,16,64,128]{3,2,1,0:T(8,128)}, u32[]{:S(2)}) copy-start(f32[8,16,64,128]{3,2,1,0:T(8,128)} %param.5) | copy-start | bytes 12582916
  32.0 2.5 %copy-start.4 = (f32[10,16,64,128]{3,2,1,0:T(8,128)}, f32[10,16,64,128]{3,2,1,0:T(8,128)S(1)}, u32[]{:S(2)}) copy-start(f32[10,16,64,128]{3,2,1,0:T(8,128)S(1)} %constant_dynamic-update-slice_fusion) | copy-start | bytes 15728644
  51.0 27.3 %collective-permute-start.6 = (f32[1,16,64,128]{3,2,1,0:T(8,128)S(1)}, f32[1,16,64,128]{3,2,1,0:T(8,128)S(1)}, u32[]{:S(2)}, u32[]{:S(2)}) collective-permute-start(f32[1,16,64,128]{3,2,1,0:T(8,128)S(1)} %get-tuple-element.50), channel_id=1, source_target_pairs={{0,16},{16,32},{32,48},{48,64},{64,80},{80,96},{96,112},{112,128},... | collective-permute-start | bytes 1572872 | tf_op jit(solution)/shard_map/ppermute | solution.py:17
  52.3 26.0 %collective-permute-start.7 = (f32[1,16,64,128]{3,2,1,0:T(8,128)S(1)}, f32[1,16,64,128]{3,2,1,0:T(8,128)S(1)}, u32[]{:S(2)}, u32[]{:S(2)}) collective-permute-start(f32[1,16,64,128]{3,2,1,0:T(8,128)S(1)} %get-tuple-element.51), channel_id=1, source_target_pairs={{16,0},{32,16},{48,32},{64,48},{80,64},{96,80},{112,96},{128,112},... | collective-permute-start | bytes 1572872 | tf_op jit(solution)/shard_map/ppermute | solution.py:18
  58.7 10.7 %collective-permute-start.8 = (f32[8,1,64,128]{3,2,1,0:T(8,128)S(1)}, f32[8,1,64,128]{3,2,1,0:T(8,128)S(1)}, u32[]{:S(2)}, u32[]{:S(2)}) collective-permute-start(f32[8,1,64,128]{3,2,1,0:T(8,128)S(1)} %get-tuple-element.52), channel_id=1, source_target_pairs={{0,4},{4,8},{8,12},{1,5},{5,9},{9,13},{2,6},{6,10},{10,14},{3,7},{... | collective-permute-start | bytes 786440 | tf_op jit(solution)/shard_map/ppermute | solution.py:17
  63.3 10.4 %collective-permute-start.9 = (f32[8,1,64,128]{3,2,1,0:T(8,128)S(1)}, f32[8,1,64,128]{3,2,1,0:T(8,128)S(1)}, u32[]{:S(2)}, u32[]{:S(2)}) collective-permute-start(f32[8,1,64,128]{3,2,1,0:T(8,128)S(1)} %get-tuple-element.53), channel_id=1, source_target_pairs={{4,0},{8,4},{12,8},{5,1},{9,5},{13,9},{6,2},{10,6},{14,10},{7,3},{... | collective-permute-start | bytes 786440 | tf_op jit(solution)/shard_map/ppermute | solution.py:18
  64.7 9.0 %collective-permute-start.10 = (f32[8,16,1,128]{3,2,1,0:T(1,128)S(1)}, f32[8,16,1,128]{3,2,1,0:T(1,128)S(1)}, u32[]{:S(2)}, u32[]{:S(2)}) collective-permute-start(f32[8,16,1,128]{3,2,1,0:T(1,128)S(1)} %get-tuple-element.48), channel_id=1, source_target_pairs={{0,2},{1,3},{4,6},{5,7},{8,10},{9,11},{12,14},{13,15},{16,18},{17,... | collective-permute-start | bytes 196616 | tf_op jit(solution)/shard_map/ppermute | solution.py:17
  69.4 8.9 %collective-permute-start.11 = (f32[8,16,1,128]{3,2,1,0:T(1,128)S(1)}, f32[8,16,1,128]{3,2,1,0:T(1,128)S(1)}, u32[]{:S(2)}, u32[]{:S(2)}) collective-permute-start(f32[8,16,1,128]{3,2,1,0:T(1,128)S(1)} %get-tuple-element.49), channel_id=1, source_target_pairs={{2,0},{3,1},{6,4},{7,5},{10,8},{11,9},{14,12},{15,13},{18,16},{19,... | collective-permute-start | bytes 196616 | tf_op jit(solution)/shard_map/ppermute | solution.py:18
  86.6 29.3 %collective-permute-start.12 = (f32[1,16,64,128]{3,2,1,0:T(8,128)S(1)}, f32[1,16,64,128]{3,2,1,0:T(8,128)S(1)}, u32[]{:S(2)}, u32[]{:S(2)}) collective-permute-start(f32[1,16,64,128]{3,2,1,0:T(8,128)S(1)} %get-tuple-element.44), channel_id=1, source_target_pairs={{0,16},{16,32},{32,48},{48,64},{64,80},{80,96},{96,112},{112,128},... | collective-permute-start | bytes 1572872 | tf_op jit(solution)/shard_map/ppermute | solution.py:17
  87.9 28.0 %collective-permute-start.13 = (f32[1,16,64,128]{3,2,1,0:T(8,128)S(1)}, f32[1,16,64,128]{3,2,1,0:T(8,128)S(1)}, u32[]{:S(2)}, u32[]{:S(2)}) collective-permute-start(f32[1,16,64,128]{3,2,1,0:T(8,128)S(1)} %get-tuple-element.45), channel_id=1, source_target_pairs={{16,0},{32,16},{48,32},{64,48},{80,64},{96,80},{112,96},{128,112},... | collective-permute-start | bytes 1572872 | tf_op jit(solution)/shard_map/ppermute | solution.py:18
  95.5 11.5 %collective-permute-start.14 = (f32[8,1,64,128]{3,2,1,0:T(8,128)S(1)}, f32[8,1,64,128]{3,2,1,0:T(8,128)S(1)}, u32[]{:S(2)}, u32[]{:S(2)}) collective-permute-start(f32[8,1,64,128]{3,2,1,0:T(8,128)S(1)} %get-tuple-element.46), channel_id=1, source_target_pairs={{0,4},{4,8},{8,12},{1,5},{5,9},{9,13},{2,6},{6,10},{10,14},{3,7},{... | collective-permute-start | bytes 786440 | tf_op jit(solution)/shard_map/ppermute | solution.py:17
  103.0 10.6 %collective-permute-start.15 = (f32[8,1,64,128]{3,2,1,0:T(8,128)S(1)}, f32[8,1,64,128]{3,2,1,0:T(8,128)S(1)}, u32[]{:S(2)}, u32[]{:S(2)}) collective-permute-start(f32[8,1,64,128]{3,2,1,0:T(8,128)S(1)} %get-tuple-element.47), channel_id=1, source_target_pairs={{4,0},{8,4},{12,8},{5,1},{9,5},{13,9},{6,2},{10,6},{14,10},{7,3},{... | collective-permute-start | bytes 786440 | tf_op jit(solution)/shard_map/ppermute | solution.py:18
  104.4 9.2 %collective-permute-start.16 = (f32[8,16,1,128]{3,2,1,0:T(1,128)S(1)}, f32[8,16,1,128]{3,2,1,0:T(1,128)S(1)}, u32[]{:S(2)}, u32[]{:S(2)}) collective-permute-start(f32[8,16,1,128]{3,2,1,0:T(1,128)S(1)} %get-tuple-element.42), channel_id=1, source_target_pairs={{0,2},{1,3},{4,6},{5,7},{8,10},{9,11},{12,14},{13,15},{16,18},{17,... | collective-permute-start | bytes 196616 | tf_op jit(solution)/shard_map/ppermute | solution.py:17
  106.9 8.9 %collective-permute-start.17 = (f32[8,16,1,128]{3,2,1,0:T(1,128)S(1)}, f32[8,16,1,128]{3,2,1,0:T(1,128)S(1)}, u32[]{:S(2)}, u32[]{:S(2)}) collective-permute-start(f32[8,16,1,128]{3,2,1,0:T(1,128)S(1)} %get-tuple-element.43), channel_id=1, source_target_pairs={{2,0},{3,1},{6,4},{7,5},{10,8},{11,9},{14,12},{15,13},{18,16},{19,... | collective-permute-start | bytes 196616 | tf_op jit(solution)/shard_map/ppermute | solution.py:18
  124.0 5.4 %copy-start.3 = (f32[8,16,64,128]{3,2,1,0:T(8,128)}, f32[8,16,64,128]{3,2,1,0:T(8,128)S(1)}, u32[]{:S(2)}) copy-start(f32[8,16,64,128]{3,2,1,0:T(8,128)S(1)} %fusion.5) | copy-start | bytes 12582916
  129.4 2.0 copy-start.2
Sparse Core Ops, SparseCore 0:
  132.5 72.2 all-gather.2
where the time goes:
time: 236 us; the launch traced here: 235 us
  waiting for transfers between devices  92.6 us (39%)
  starting transfers between devices  60.4 us (26%)
  other arithmetic  56.6 us (24%)
  between operations  14.5 us (6%)
  local copies, waits for them, and re-layouts  10.4 us (4%)
    all_gather x1, waiting for transfers between devices, entering(): gathered = lax.all_gather(part, axis)  72.4 us
    ppermute x9, starting transfers between devices, with_halo(): lax.ppermute(last, axis, up)  35.2 us
    add x3, other arithmetic, march_step(): return middle + 0.1 * spread + 0.2 * middle * (1.0 - middle * crowding)  28.4 us
    ppermute x9, starting transfers between devices, with_halo(): lax.ppermute(initial, axis, [(b, a) for a, b in up])  25.2 us
    ppermute x9, waiting for transfers between devices, with_halo(): lax.ppermute(initial, axis, [(b, a) for a, b in up])  19.5 us
    add x15, other arithmetic, add_pair(): return earlier_total + later_total  17.7 us
    another operation x1, other arithmetic, on_device(): here = jnp.cumsum(field_values, axis=0)  5.41 us
    div x1, other arithmetic, on_device(): potential = (here + below) / (field_values.shape[0] * lax.axis_size('rows'))  5.13 us
  transfers between devices with their start and end apart: 19, of which 7 were waited for; matrix products, arithmetic and copies ran while one was open for 1% of the time, Pallas kernels for 0%

commit v1 on v0

v1 whole, which is shorter than its diff:
```python
import functools

import jax
import jax.numpy as jnp
from jax import lax
from jax.experimental import pallas as pl
from jax.experimental.pallas import tpu as pltpu
from jax.sharding import PartitionSpec as P


STEPS = 3
HALF = 64
TILE = 8
VMEM = pl.BlockSpec(memory_space=pltpu.MemorySpace.VMEM)
SMEM = pl.BlockSpec(memory_space=pltpu.MemorySpace.SMEM)


def call(body, outs, args, scratch=(), limit=16, **more):
    return pl.pallas_call(
        body,
        out_shape=[jax.ShapeDtypeStruct(s, jnp.float32) for s in outs],
        scratch_shapes=[pltpu.VMEM(s, jnp.float32) for s in scratch],
        compiler_params=pltpu.CompilerParams(vmem_limit_bytes=limit * 1024 * 1024),
        **more,
    )(*args)


def left(shape=(TILE, 128)):
    return lax.broadcasted_iota(jnp.int32, shape, len(shape) - 1) < HALF


def swap(v):
    return pltpu.roll(v, HALF, v.ndim - 1)


def pack_tiles(ref, j, i, t, nk):
    a = ref[j, i, pl.ds(t * TILE, TILE), :]
    b = ref[j, i, pl.ds(nk // 2 + t * TILE, TILE), :]
    m = left()
    return jnp.where(m, a, swap(b)), jnp.where(m, swap(a), b)


def write_faces(place, out, s_c0, s_c1, s_k):
    nj, ni, nk = out.shape[:3]
    for j in range(nj):
        first, last = out[j, 0], out[j, ni - 1]
        s_c0[j] = jnp.where(place[1] == 0, last, first)
        s_c1[j] = jnp.where(place[1] == 0, first, last)
        s_k[j] = jnp.where(place[2] == 0, out[j, :, nk - 1, :], out[j, :, 0, :])


def pack_field(place, f, fa, fb, *faces):
    nj, ni, nk = f.shape[:3]
    sa, sb = faces[:5], faces[5:]

    def at(i, _):
        for t in range(nk // 2 // TILE):
            ends = {}
            for j in range(nj):
                a, b = pack_tiles(f, j, i, t, nk)
                fa[j, i, pl.ds(t * TILE, TILE), :] = a
                fb[j, i, pl.ds(t * TILE, TILE), :] = b
                if j in (0, nj - 1):
                    ends[j] = (a, b)
            for n, s in ((0, sa), (1, sb)):
                first, last = ends[0][n], ends[nj - 1][n]
                s[0][i, pl.ds(t * TILE, TILE), :] = jnp.where(place[0] == 0, last, first)
                s[1][i, pl.ds(t * TILE, TILE), :] = jnp.where(place[0] == 0, first, last)
        return 0

    lax.fori_loop(0, ni, at, 0)
    write_faces(place, fa, *sa[2:])
    write_faces(place, fb, *sb[2:])


def pack_crowding(c, ca, cb):
    nj, ni, nk = c.shape[:3]

    def at(i, _):
        for j in range(nj):
            for t in range(nk // 2 // TILE):
                a, b = pack_tiles(c, j, i, t, nk)
                ca[j, i, pl.ds(t * TILE, TILE), :] = 0.2 * a
                cb[j, i, pl.ds(t * TILE, TILE), :] = 0.2 * b
        return 0

    lax.fori_loop(0, ni, at, 0)


def step_body(last, with_total, place, f, c, r0, r1, c0, c1, ks, *rest):
    rest = list(rest)
    earlier = rest.pop(0) if with_total else None
    out = rest.pop(0)
    if last:
        total = rest.pop(0)
    else:
        s_r0, s_r1, s_c0, s_c1, s_k = rest[:5]
        rest = rest[5:]
    kl, kh = rest
    nj, ni, nk = f.shape[:3]
    tiles = nk // TILE
    wide = left((ni, 128))
    for j in range(nj):
        x = swap(ks[j])
        low_side = jnp.where(place[2] == 1, x, 0.0)
        high_side = jnp.where(place[2] == 0, x, 0.0)
        kl[j] = jnp.where(wide, low_side, swap(f[j, :, nk - 1, :]))
        kh[j] = jnp.where(wide, swap(f[j, :, 0, :]), high_side)
    row = lax.broadcasted_iota(jnp.int32, (TILE, 128), 0)
    top, bottom = row == 0, row == TILE - 1
    even_r, even_c = place[0] == 0, place[1] == 0

    def ds(t):
        return pl.ds(t * TILE, TILE)

    def at(i, below, above):
        down = [jnp.where(even_r, r1[i, ds(t), :], r0[i, ds(t), :]) for t in range(tiles)]
        mid = [f[0, i, ds(t), :] for t in range(tiles)]
        sums, first = [None] * tiles, [None] * tiles
        for j in range(nj):
            if j + 1 < nj:
                up = [f[j + 1, i, ds(t), :] for t in range(tiles)]
            else:
                up = [jnp.where(even_r, r0[i, ds(t), :], r1[i, ds(t), :]) for t in range(tiles)]
            fwd = [pltpu.roll(v, 1, 0) for v in mid]
            bwd = [pltpu.roll(v, TILE - 1, 0) for v in mid]
            low = jnp.broadcast_to(kl[j, pl.ds(i, 1), :], (TILE, 128))
            high = jnp.broadcast_to(kh[j, pl.ds(i, 1), :], (TILE, 128))
            for t in range(tiles):
                before = jnp.where(top, fwd[t - 1] if t else low, fwd[t])
                after = jnp.where(bottom, bwd[t + 1] if t + 1 < tiles else high, bwd[t])
                around = (down[t] + up[t]) + (below(j, t) + above(j, t)) + (before + after)
                v = mid[t] * (0.6 - c[j, i, ds(t), :] * mid[t]) + 0.1 * around
                out[j, i, ds(t), :] = v
                if last:
                    sums[t] = v if j == 0 else sums[t] + v
                elif j == 0:
                    first[t] = v
                elif j == nj - 1:
                    s_r0[i, ds(t), :] = jnp.where(even_r, v, first[t])
                    s_r1[i, ds(t), :] = jnp.where(even_r, first[t], v)
            down, mid = mid, up
        if last:
            base = nk if with_total else 0
            for t in range(tiles):
                total[i, pl.ds(base + t * TILE, TILE), :] = sums[t]
                if with_total:
                    total[i, ds(t), :] = earlier[i, ds(t), :]

    def inner(i, _):
        at(i, lambda j, t: f[j, i - 1, ds(t), :], lambda j, t: f[j, i + 1, ds(t), :])
        return 0

    at(0, lambda j, t: jnp.where(even_c, c1[j, ds(t), :], c0[j, ds(t), :]), lambda j, t: f[j, 1, ds(t), :])
    lax.fori_loop(1, ni - 1, inner, 0)
    at(ni - 1, lambda j, t: f[j, ni - 2, ds(t), :], lambda j, t: jnp.where(even_c, c0[j, ds(t), :], c1[j, ds(t), :]))
    if not last:
        write_faces(place, out, s_c0, s_c1, s_k)


def prefix_body(g, out):
    n = g.shape[0]
    state = jnp.zeros(g.shape[1:], jnp.float32)
    for d in range(n):
        out[d] = state
        if d + 1 < n:
            state = state + g[d]


def finish_body(scale, fa, fb, base, potential, field):
    nj, _, nk = fa.shape[:3]
    m = left()
    for t in range(nk // TILE):
        lo, hi = pl.ds(t * TILE, TILE), pl.ds(nk + t * TILE, TILE)

        def both(a, b):
            return jnp.where(m, a, swap(b)), jnp.where(m, swap(a), b)

        acc0, acc1 = both(base[0, lo, :], base[0, hi, :])
        for j in range(nj):
            v0, v1 = both(fa[j, 0, lo, :], fb[j, 0, lo, :])
            field[j, 0, lo, :] = v0
            field[j, 0, hi, :] = v1
            acc0, acc1 = acc0 + v0, acc1 + v1
            potential[j, 0, lo, :] = acc0 * scale
            potential[j, 0, hi, :] = acc1 * scale


def pairs(size, start):
    out = []
    for i in range(start, size - 1, 2):
        out += [(i, i + 1), (i + 1, i)]
    return out


KINDS = ("k", "c1", "c0", "r0", "r1")


def exchange(faces):
    r0, r1, c0, c1, k = faces
    rows, cols, slabs = lax.axis_size("rows"), lax.axis_size("cols"), lax.axis_size("slabs")
    sends = {
        "k": (k, "slabs", pairs(slabs, 0)),
        "c0": (c0, "cols", pairs(cols, 0)),
        "c1": (c1, "cols", pairs(cols, 1)),
        "r0": (r0, "rows", pairs(rows, 0)),
        "r1": (r1, "rows", pairs(rows, 1)),
    }
    got = {}
    for kind in KINDS:
        got[kind] = lax.ppermute(*sends[kind])
    return [got[kind] for kind in ("r0", "r1", "c0", "c1", "k")]


def on_device(field_values, crowding):
    nj, ni, nk, nl = field_values.shape
    half = (nj, ni, nk // 2, nl)
    faces = [(ni, nk // 2, nl)] * 2 + [(nj, nk // 2, nl)] * 2 + [(nj, ni, nl)]
    place = jnp.stack([lax.axis_index("rows") % 2, lax.axis_index("cols") % 2, lax.axis_index("slabs")])
    place = place.astype(jnp.int32)
    out = call(
        pack_field, [half, half] + faces + faces, (place, field_values), in_specs=[SMEM, VMEM]
    )
    f, sent = [out[0], out[1]], [out[2:7], out[7:12]]
    halos = [exchange(sent[0]), exchange(sent[1])]
    c = call(pack_crowding, [half, half], (crowding,))
    scratch = [(nj, ni, nl)] * 2
    total = None
    for step in range(STEPS):
        last = step == STEPS - 1
        for h in range(2):
            with_total = last and h == 1
            args = (place, f[h], c[h], *halos[h]) + ((total,) if with_total else ())
            if last:
                outs = [half, (ni, nk if with_total else nk // 2, nl)]
            else:
                outs = [half] + faces
            res = call(
                functools.partial(step_body, last, with_total),
                outs,
                args,
                scratch,
                in_specs=[SMEM] + [VMEM] * (len(args) - 1),
            )
            f[h] = res[0]
            if last:
                total = res[1]
            else:
                halos[h] = exchange(res[1:])
    rows = lax.axis_size("rows")
    gathered = lax.all_to_all(total.reshape(rows, ni * nk // rows, nl), "rows", 0, 0, tiled=True)
    before = call(prefix_body, [gathered.shape], (gathered,))[0]
    base = lax.all_to_all(before, "rows", 0, 0, tiled=True).reshape(ni, nk, nl)
    full = pl.BlockSpec((nj, 1, nk, nl), lambda i: (0, i, 0, 0))
    part = pl.BlockSpec((nj, 1, nk // 2, nl), lambda i: (0, i, 0, 0))
    potential, field = call(
        functools.partial(finish_body, 1.0 / (nj * rows)),
        [field_values.shape] * 2,
        (f[0], f[1], base),
        grid=(ni,),
        in_specs=[part, part, pl.BlockSpec((1, nk, nl), lambda i: (i, 0, 0))],
        out_specs=[full, full],
    )
    return potential, field


def solution(mesh):
    spec = P(("trial", "rows"), "cols", "slabs", None)
    return jax.shard_map(
        on_device, mesh=mesh, in_specs=(spec, spec), out_specs=(spec, spec), check_vma=False
    )
```

time: 236 us -> 152 us (0.64)
  the two profiles are of different devices: /device:TPU:27 before, /device:TPU:4 now
where the time goes in v1:
time: 152 us
  starting transfers between devices  59.8 us (39%)
  blocking collectives  34.6 us (23%)
  waiting for transfers between devices  30.5 us (20%)
  Pallas kernels  23.7 us (16%)
  local copies, waits for them, and re-layouts  2.19 us (1%)
    ppermute x30, starting transfers between devices, exchange(): got[kind] = lax.ppermute(*sends[kind])  59.8 us
    ppermute x30, waiting for transfers between devices, exchange(): got[kind] = lax.ppermute(*sends[kind])  30.5 us
    pallas_call x10, Pallas kernels, call(): pl.pallas_call(body, out_shape=[jax.ShapeDtypeStruct(s, jnp.float32) for...  23.7 us
    all_to_all x1, blocking collectives, on_device(): lax.all_to_all(total.reshape(rows, ni * nk // rows, nl), 'rows', 0, 0, ti...  21.2 us
    all_to_all x1, blocking collectives, on_device(): base = lax.all_to_all(before, 'rows', 0, 0, tiled=True).reshape(ni, nk, nl)  13.5 us
  transfers between devices with their start and end apart: 30, of which 10 were waited for; matrix products, arithmetic and copies ran while one was open for 0% of the time, Pallas kernels for 7%

profile of v1, /device:TPU:4, one launch (start us, length us, event | category | flops | bytes accessed | tf_op | source)
XLA Modules:
  0.0 151.7 jit_solution(9764026963043423486)
XLA Ops:
  0.6 0.1 pad_add_fusion.place
  0.7 2.2 %copy-done = f32[8,16,64,128]{3,2,1,0:T(8,128)S(1)} copy-done((f32[8,16,64,128]{3,2,1,0:T(8,128)S(1)}, f32[8,16,64,128]{3,2,1,0:T(8,128)}, u32[]{:S(2)}) %copy-start) | copy-done | bytes 4194328
  2.9 2.9 %shard_map.41 = (f32[8,16,32,128]{3,2,1,0:T(8,128)S(1)}, f32[8,16,32,128]{3,2,1,0:T(8,128)S(1)}, f32[16,32,128]{2,1,0:T(8,128)S(1)}, f32[16,32,128]{2,1,0:T(8,12...) custom-call(s32[3]{0:T(128)S(1)} %pad_add_fusion.place, ...), custom_call_target="tpu_custom_call" | custom-call | tf_op jit(solution)/shard_map/pallas_call | solution.py:19
  5.8 0.1 collective-permute-start
  5.9 0.7 collective-permute-start.1
  6.6 2.3 %collective-permute-start.2 = (f32[8,32,128]{2,1,0:T(8,128)S(1)}, f32[8,32,128]{2,1,0:T(8,128)S(1)}, u32[]{:S(2)}, u32[]{:S(2)}) collective-permute-start(f32[8,32,128]{2,1,0:T(8,128)S(1)} %get-tuple-element.48), channel_id=1, source_target_pairs={{0,4},{4,0},{8,12},{12,8},{1,5},{5,1},{9,13},{13,9},{2,6},{6,2},{1... | collective-permute-start | bytes 393224 | tf_op jit(solution)/shard_map/ppermute | solution.py:211
  8.9 5.5 %collective-permute-start.4 = (f32[8,16,128]{2,1,0:T(8,128)S(1)}, f32[8,16,128]{2,1,0:T(8,128)S(1)}, u32[]{:S(2)}, u32[]{:S(2)}) collective-permute-start(f32[8,16,128]{2,1,0:T(8,128)S(1)} %get-tuple-element.50), channel_id=1, source_target_pairs={{0,2},{2,0},{1,3},{3,1},{4,6},{6,4},{5,7},{7,5},{8,10},{10,8},{9,1... | collective-permute-start | bytes 196616 | tf_op jit(solution)/shard_map/ppermute | solution.py:211
  14.4 5.8 %collective-permute-start.3 = (f32[8,32,128]{2,1,0:T(8,128)S(1)}, f32[8,32,128]{2,1,0:T(8,128)S(1)}, u32[]{:S(2)}, u32[]{:S(2)}) collective-permute-start(f32[8,32,128]{2,1,0:T(8,128)S(1)} %get-tuple-element.49), channel_id=1, source_target_pairs={{4,8},{8,4},{5,9},{9,5},{6,10},{10,6},{7,11},{11,7},{20,24},{24,20... | collective-permute-start | bytes 393224 | tf_op jit(solution)/shard_map/ppermute | solution.py:211
  20.2 1.8 %collective-permute-start.15 = (f32[16,32,128]{2,1,0:T(8,128)S(1)}, f32[16,32,128]{2,1,0:T(8,128)S(1)}, u32[]{:S(2)}, u32[]{:S(2)}) collective-permute-start(f32[16,32,128]{2,1,0:T(8,128)S(1)} %get-tuple-element.66), channel_id=1, source_target_pairs={{0,16},{16,0},{32,48},{48,32},{64,80},{80,64},{96,112},{112,96},{1... | collective-permute-start | bytes 786440 | tf_op jit(solution)/shard_map/ppermute | solution.py:211
  22.0 0.7 collective-permute-start.16
  22.7 5.6 %collective-permute-done.3.c1 = f32[8,32,128]{2,1,0:T(8,128)S(1)} collective-permute-done((f32[8,32,128]{2,1,0:T(8,128)S(1)}, f32[8,32,128]{2,1,0:T(8,128)S(1)}, u32[]{:S(2)}, u32[]{:S(2)}) %collective-permute-start.3) | collective-permute-done | bytes 131104 | tf_op jit(solution)/shard_map/ppermute | solution.py:211
  28.3 0.0 collective-permute-done.r0
  28.3 2.6 %collective-permute-start.18 = (f32[8,32,128]{2,1,0:T(8,128)S(1)}, f32[8,32,128]{2,1,0:T(8,128)S(1)}, u32[]{:S(2)}, u32[]{:S(2)}) collective-permute-start(f32[8,32,128]{2,1,0:T(8,128)S(1)} %get-tuple-element.69), channel_id=1, source_target_pairs={{4,8},{8,4},{5,9},{9,5},{6,10},{10,6},{7,11},{11,7},{20,24},{24,20... | collective-permute-start | bytes 393224 | tf_op jit(solution)/shard_map/ppermute | solution.py:211
  30.9 0.0 collective-permute-done.1.r1
  30.9 1.8 %collective-permute-start.19 = (f32[8,16,128]{2,1,0:T(8,128)S(1)}, f32[8,16,128]{2,1,0:T(8,128)S(1)}, u32[]{:S(2)}, u32[]{:S(2)}) collective-permute-start(f32[8,16,128]{2,1,0:T(8,128)S(1)} %get-tuple-element.70), channel_id=1, source_target_pairs={{0,2},{2,0},{1,3},{3,1},{4,6},{6,4},{5,7},{7,5},{8,10},{10,8},{9,1... | collective-permute-start | bytes 196616 | tf_op jit(solution)/shard_map/ppermute | solution.py:211
  32.7 2.2 %shard_map.42 = (f32[8,16,32,128]{3,2,1,0:T(8,128)S(1)}, f32[8,16,32,128]{3,2,1,0:T(8,128)S(1)}) custom-call(f32[8,16,64,128]{3,2,1,0:T(8,128)S(1)} %copy-done.1), custom_call_target="tpu_custom_call" | custom-call | tf_op jit(solution)/shard_map/pallas_call | solution.py:19
  34.9 1.8 %shard_map.43 = (f32[8,16,32,128]{3,2,1,0:T(8,128)S(1)}, f32[16,32,128]{2,1,0:T(8,128)S(1)}, f32[16,32,128]{2,1,0:T(8,128)S(1)}, f32[8,32,128]{2,1,0:T(8,128)S(1...) custom-call(s32[3]{0:T(128)S(1)} %pad_add_fusion.place, f32[8,16,32,128]{3,2,1,0:T(8,128)S(1)} %get-tuple-element.44.f, ...), custom_call_target="tpu_custom_call" | custom-call | tf_op jit(solution)/shard_map/pallas_call | solution.py:19
  36.7 3.3 %collective-permute-done.19.ks = f32[8,16,128]{2,1,0:T(8,128)S(1)} collective-permute-done((f32[8,16,128]{2,1,0:T(8,128)S(1)}, f32[8,16,128]{2,1,0:T(8,128)S(1)}, u32[]{:S(2)}, u32[]{:S(2)}) %collective-permute-start.19) | collective-permute-done | bytes 65568 | tf_op jit(solution)/shard_map/ppermute | solution.py:211
  40.0 1.4 collective-permute-start.5
  41.4 0.7 collective-permute-start.6
  42.1 2.1 %collective-permute-done.18.c1 = f32[8,32,128]{2,1,0:T(8,128)S(1)} collective-permute-done((f32[8,32,128]{2,1,0:T(8,128)S(1)}, f32[8,32,128]{2,1,0:T(8,128)S(1)}, u32[]{:S(2)}, u32[]{:S(2)}) %collective-permute-start.18) | collective-permute-done | bytes 131104 | tf_op jit(solution)/shard_map/ppermute | solution.py:211
  44.2 0.0 collective-permute-start.7
  44.2 0.0 collective-permute-done.15.r0
  44.2 2.2 %collective-permute-start.9 = (f32[8,16,128]{2,1,0:T(8,128)S(1)}, f32[8,16,128]{2,1,0:T(8,128)S(1)}, u32[]{:S(2)}, u32[]{:S(2)}) collective-permute-start(f32[8,16,128]{2,1,0:T(8,128)S(1)} %get-tuple-element.56), channel_id=1, source_target_pairs={{0,2},{2,0},{1,3},{3,1},{4,6},{6,4},{5,7},{7,5},{8,10},{10,8},{9,1... | collective-permute-start | bytes 196616 | tf_op jit(solution)/shard_map/ppermute | solution.py:211
  46.5 2.9 %collective-permute-start.8 = (f32[8,32,128]{2,1,0:T(8,128)S(1)}, f32[8,32,128]{2,1,0:T(8,128)S(1)}, u32[]{:S(2)}, u32[]{:S(2)}) collective-permute-start(f32[8,32,128]{2,1,0:T(8,128)S(1)} %get-tuple-element.55), channel_id=1, source_target_pairs={{4,8},{8,4},{5,9},{9,5},{6,10},{10,6},{7,11},{11,7},{20,24},{24,20... | collective-permute-start | bytes 393224 | tf_op jit(solution)/shard_map/ppermute | solution.py:211
  49.4 1.8 %shard_map.46 = (f32[8,16,32,128]{3,2,1,0:T(8,128)S(1)}, f32[16,32,128]{2,1,0:T(8,128)S(1)}, f32[16,32,128]{2,1,0:T(8,128)S(1)}, f32[8,32,128]{2,1,0:T(8,128)S(1...) custom-call(s32[3]{0:T(128)S(1)} %pad_add_fusion.place, f32[8,16,32,128]{3,2,1,0:T(8,128)S(1)} %get-tuple-element.64.f, ...), custom_call_target="tpu_custom_call" | custom-call | tf_op jit(solution)/shard_map/pallas_call | solution.py:19
  51.2 1.2 collective-permute-done.9.ks
  52.4 3.7 %collective-permute-start.20 = (f32[16,32,128]{2,1,0:T(8,128)S(1)}, f32[16,32,128]{2,1,0:T(8,128)S(1)}, u32[]{:S(2)}, u32[]{:S(2)}) collective-permute-start(f32[16,32,128]{2,1,0:T(8,128)S(1)} %get-tuple-element.72), channel_id=1, source_target_pairs={{0,16},{16,0},{32,48},{48,32},{64,80},{80,64},{96,112},{112,96},{1... | collective-permute-start | bytes 786440 | tf_op jit(solution)/shard_map/ppermute | solution.py:211
  56.1 0.7 collective-permute-start.21
  56.8 3.8 %collective-permute-done.8.c1 = f32[8,32,128]{2,1,0:T(8,128)S(1)} collective-permute-done((f32[8,32,128]{2,1,0:T(8,128)S(1)}, f32[8,32,128]{2,1,0:T(8,128)S(1)}, u32[]{:S(2)}, u32[]{:S(2)}) %collective-permute-start.8) | collective-permute-done | bytes 131104 | tf_op jit(solution)/shard_map/ppermute | solution.py:211
  60.6 0.0 collective-permute-start.22
  60.6 0.0 collective-permute-done.5.r0
  60.6 2.1 %collective-permute-start.23 = (f32[8,32,128]{2,1,0:T(8,128)S(1)}, f32[8,32,128]{2,1,0:T(8,128)S(1)}, u32[]{:S(2)}, u32[]{:S(2)}) collective-permute-start(f32[8,32,128]{2,1,0:T(8,128)S(1)} %get-tuple-element.75), channel_id=1, source_target_pairs={{4,8},{8,4},{5,9},{9,5},{6,10},{10,6},{7,11},{11,7},{20,24},{24,20... | collective-permute-start | bytes 393224 | tf_op jit(solution)/shard_map/ppermute | solution.py:211
  62.7 0.0 collective-permute-done.6.r1
  62.7 3.8 %collective-permute-start.24 = (f32[8,16,128]{2,1,0:T(8,128)S(1)}, f32[8,16,128]{2,1,0:T(8,128)S(1)}, u32[]{:S(2)}, u32[]{:S(2)}) collective-permute-start(f32[8,16,128]{2,1,0:T(8,128)S(1)} %get-tuple-element.76), channel_id=1, source_target_pairs={{0,2},{2,0},{1,3},{3,1},{4,6},{6,4},{5,7},{7,5},{8,10},{10,8},{9,1... | collective-permute-start | bytes 196616 | tf_op jit(solution)/shard_map/ppermute | solution.py:211
  66.6 1.8 %shard_map.44 = (f32[8,16,32,128]{3,2,1,0:T(8,128)S(1)}, f32[16,32,128]{2,1,0:T(8,128)S(1)}, f32[16,32,128]{2,1,0:T(8,128)S(1)}, f32[8,32,128]{2,1,0:T(8,128)S(1...) custom-call(s32[3]{0:T(128)S(1)} %pad_add_fusion.place, f32[8,16,32,128]{3,2,1,0:T(8,128)S(1)} %get-tuple-element.51.f, ...), custom_call_target="tpu_custom_call" | custom-call | tf_op jit(solution)/shard_map/pallas_call | solution.py:19
  68.4 4.1 %collective-permute-done.24.ks = f32[8,16,128]{2,1,0:T(8,128)S(1)} collective-permute-done((f32[8,16,128]{2,1,0:T(8,128)S(1)}, f32[8,16,128]{2,1,0:T(8,128)S(1)}, u32[]{:S(2)}, u32[]{:S(2)}) %collective-permute-start.24) | collective-permute-done | bytes 65568 | tf_op jit(solution)/shard_map/ppermute | solution.py:211
  72.5 1.4 collective-permute-start.10
  73.9 0.0 collective-permute-done.22.c0
  73.9 0.0 collective-permute-start.12
  73.9 2.9 %collective-permute-done.23.c1 = f32[8,32,128]{2,1,0:T(8,128)S(1)} collective-permute-done((f32[8,32,128]{2,1,0:T(8,128)S(1)}, f32[8,32,128]{2,1,0:T(8,128)S(1)}, u32[]{:S(2)}, u32[]{:S(2)}) %collective-permute-start.23) | collective-permute-done | bytes 131104 | tf_op jit(solution)/shard_map/ppermute | solution.py:211
  76.8 0.7 collective-permute-start.11
  77.5 0.0 collective-permute-done.20.r0
  77.5 2.4 %collective-permute-start.14 = (f32[8,16,128]{2,1,0:T(8,128)S(1)}, f32[8,16,128]{2,1,0:T(8,128)S(1)}, u32[]{:S(2)}, u32[]{:S(2)}) collective-permute-start(f32[8,16,128]{2,1,0:T(8,128)S(1)} %get-tuple-element.62), channel_id=1, source_target_pairs={{0,2},{2,0},{1,3},{3,1},{4,6},{6,4},{5,7},{7,5},{8,10},{10,8},{9,1... | collective-permute-start | bytes 196616 | tf_op jit(solution)/shard_map/ppermute | solution.py:211
  79.9 0.0 collective-permute-done.21.r1
  79.9 3.0 %collective-permute-start.13 = (f32[8,32,128]{2,1,0:T(8,128)S(1)}, f32[8,32,128]{2,1,0:T(8,128)S(1)}, u32[]{:S(2)}, u32[]{:S(2)}) collective-permute-start(f32[8,32,128]{2,1,0:T(8,128)S(1)} %get-tuple-element.61), channel_id=1, source_target_pairs={{4,8},{8,4},{5,9},{9,5},{6,10},{10,6},{7,11},{11,7},{20,24},{24,20... | collective-permute-start | bytes 393224 | tf_op jit(solution)/shard_map/ppermute | solution.py:211
  83.0 1.8 %shard_map.47 = (f32[8,16,32,128]{3,2,1,0:T(8,128)S(1)}, f32[16,32,128]{2,1,0:T(8,128)S(1)}, f32[16,32,128]{2,1,0:T(8,128)S(1)}, f32[8,32,128]{2,1,0:T(8,128)S(1...) custom-call(s32[3]{0:T(128)S(1)} %pad_add_fusion.place, f32[8,16,32,128]{3,2,1,0:T(8,128)S(1)} %get-tuple-element.71.f, ...), custom_call_target="tpu_custom_call" | custom-call | tf_op jit(solution)/shard_map/pallas_call | solution.py:19
  84.8 1.0 collective-permute-done.14.ks
  85.7 4.1 %collective-permute-start.25 = (f32[16,32,128]{2,1,0:T(8,128)S(1)}, f32[16,32,128]{2,1,0:T(8,128)S(1)}, u32[]{:S(2)}, u32[]{:S(2)}) collective-permute-start(f32[16,32,128]{2,1,0:T(8,128)S(1)} %get-tuple-element.78), channel_id=1, source_target_pairs={{0,16},{16,0},{32,48},{48,32},{64,80},{80,64},{96,112},{112,96},{1... | collective-permute-start | bytes 786440 | tf_op jit(solution)/shard_map/ppermute | solution.py:211
  89.8 0.0 collective-permute-done.12.c0
  89.8 0.7 collective-permute-start.26
  90.5 0.7 collective-permute-done.13.c1
  91.2 0.0 collective-permute-start.27
  91.2 0.0 collective-permute-done.10.r0
  91.2 7.3 %collective-permute-start.28 = (f32[8,32,128]{2,1,0:T(8,128)S(1)}, f32[8,32,128]{2,1,0:T(8,128)S(1)}, u32[]{:S(2)}, u32[]{:S(2)}) collective-permute-start(f32[8,32,128]{2,1,0:T(8,128)S(1)} %get-tuple-element.81), channel_id=1, source_target_pairs={{4,8},{8,4},{5,9},{9,5},{6,10},{10,6},{7,11},{11,7},{20,24},{24,20... | collective-permute-start | bytes 393224 | tf_op jit(solution)/shard_map/ppermute | solution.py:211
  98.5 0.0 collective-permute-done.11.r1
  98.5 1.4 collective-permute-start.29
  100.0 1.8 %shard_map.45 = (f32[8,16,32,128]{3,2,1,0:T(8,128)S(1)}, f32[16,32,128]{2,1,0:T(8,128)S(1)}) custom-call(s32[3]{0:T(128)S(1)} %pad_add_fusion.place, f32[8,16,32,128]{3,2,1,0:T(8,128)S(1)} %get-tuple-element.57.f, f32[8,16,32,128]{3,2,1,0:T(8,128)S(1)} %get-tuple-element.45.c, f32[16,32,128]{2,1,0:T(8,128)S(1)} %collective-permute-done.10.r0, ...), custom_call_target="tpu_custom_call" | custom-call | tf_op jit(solution)/shard_map/pallas_call | solution.py:19
  101.8 5.7 %collective-permute-done.29.ks = f32[8,16,128]{2,1,0:T(8,128)S(1)} collective-permute-done((f32[8,16,128]{2,1,0:T(8,128)S(1)}, f32[8,16,128]{2,1,0:T(8,128)S(1)}, u32[]{:S(2)}, u32[]{:S(2)}) %collective-permute-start.29) | collective-permute-done | bytes 65568 | tf_op jit(solution)/shard_map/ppermute | solution.py:211
  107.4 0.0 collective-permute-done.27.c0
  107.5 1.8 %shard_map.48 = (f32[8,16,32,128]{3,2,1,0:T(8,128)S(1)}, f32[16,64,128]{2,1,0:T(8,128)S(1)}) custom-call(s32[3]{0:T(128)S(1)} %pad_add_fusion.place, f32[8,16,32,128]{3,2,1,0:T(8,128)S(1)} %get-tuple-element.77.f, f32[8,16,32,128]{3,2,1,0:T(8,128)S(1)} %get-tuple-element.65.c, f32[16,32,128]{2,1,0:T(8,128)S(1)} %collective-permute-done.25.r0, ...), custom_call_target="tpu_custom_call" | custom-call | tf_op jit(solution)/shard_map/pallas_call | solution.py:19
  109.2 21.2 %all_to_all.10.g = f32[16,64,128]{2,1,0:T(8,128)S(1)} all-to-all(f32[16,64,128]{2,1,0:T(8,128)S(1)} %get-tuple-element.85), channel_id=1, replica_groups=mesh['rows'=16,'cols'=4,'slabs'=2,'trial'=2] {'rows'}, dimensions={0} | all-to-all | bytes 1048576 | tf_op jit(solution)/shard_map/all_to_all | solution.py:251
  130.5 13.5 %all_to_all.11.base = f32[16,64,128]{2,1,0:T(8,128)S(1)} all-to-all(f32[16,64,128]{2,1,0:T(8,128)S(1)} %shard_map.49), channel_id=1, replica_groups=mesh['rows'=16,'cols'=4,'slabs'=2,'trial'=2] {'rows'}, dimensions={0} | all-to-all | bytes 1048576 | tf_op jit(solution)/shard_map/all_to_all | solution.py:253
  143.9 7.8 %shard_map.50 = (f32[8,16,64,128]{3,2,1,0:T(8,128)}, f32[8,16,64,128]{3,2,1,0:T(8,128)}) custom-call(f32[8,16,32,128]{3,2,1,0:T(8,128)S(1)} %get-tuple-element.63.fa, f32[8,16,32,128]{3,2,1,0:T(8,128)S(1)} %get-tuple-element.84.fb, f32[16,64,128]{2,1,0:T(8,128)S(1)} %all_to_all.11.base), custom_call_target="tpu_custom_call" | custom-call | tf_op jit(solution)/shard_map/pallas_call | solution.py:19
  (13 shorter events, 0.1 us)
Async XLA Ops:
  0.7 2.2 %copy-start = (f32[8,16,64,128]{3,2,1,0:T(8,128)S(1)}, f32[8,16,64,128]{3,2,1,0:T(8,128)}, u32[]{:S(2)}) copy-start(f32[8,16,64,128]{3,2,1,0:T(8,128)} %f.1) | copy-start | bytes 12582916
  2.9 29.8 %copy-start.1 = (f32[8,16,64,128]{3,2,1,0:T(8,128)S(1)}, f32[8,16,64,128]{3,2,1,0:T(8,128)}, u32[]{:S(2)}) copy-start(f32[8,16,64,128]{3,2,1,0:T(8,128)} %c.1) | copy-start | bytes 12582916
  5.8 22.5 %collective-permute-start = (f32[16,32,128]{2,1,0:T(8,128)S(1)}, f32[16,32,128]{2,1,0:T(8,128)S(1)}, u32[]{:S(2)}, u32[]{:S(2)}) collective-permute-start(f32[16,32,128]{2,1,0:T(8,128)S(1)} %get-tuple-element.46), channel_id=1, source_target_pairs={{0,16},{16,0},{32,48},{48,32},{64,80},{80,64},{96,112},{112,96},{1... | collective-permute-start | bytes 786440 | tf_op jit(solution)/shard_map/ppermute | solution.py:211
  5.9 25.0 %collective-permute-start.1 = (f32[16,32,128]{2,1,0:T(8,128)S(1)}, f32[16,32,128]{2,1,0:T(8,128)S(1)}, u32[]{:S(2)}, u32[]{:S(2)}) collective-permute-start(f32[16,32,128]{2,1,0:T(8,128)S(1)} %get-tuple-element.47), channel_id=1, source_target_pairs={{16,32},{32,16},{48,64},{64,48},{80,96},{96,80},{112,128},{128,112... | collective-permute-start | bytes 786440 | tf_op jit(solution)/shard_map/ppermute | solution.py:211
  6.6 15.4 %collective-permute-start.2 = (f32[8,32,128]{2,1,0:T(8,128)S(1)}, f32[8,32,128]{2,1,0:T(8,128)S(1)}, u32[]{:S(2)}, u32[]{:S(2)}) collective-permute-start(f32[8,32,128]{2,1,0:T(8,128)S(1)} %get-tuple-element.48), channel_id=1, source_target_pairs={{0,4},{4,0},{8,12},{12,8},{1,5},{5,1},{9,13},{13,9},{2,6},{6,2},{1... | collective-permute-start | bytes 393224 | tf_op jit(solution)/shard_map/ppermute | solution.py:211
  8.9 11.3 %collective-permute-start.4 = (f32[8,16,128]{2,1,0:T(8,128)S(1)}, f32[8,16,128]{2,1,0:T(8,128)S(1)}, u32[]{:S(2)}, u32[]{:S(2)}) collective-permute-start(f32[8,16,128]{2,1,0:T(8,128)S(1)} %get-tuple-element.50), channel_id=1, source_target_pairs={{0,2},{2,0},{1,3},{3,1},{4,6},{6,4},{5,7},{7,5},{8,10},{10,8},{9,1... | collective-permute-start | bytes 196616 | tf_op jit(solution)/shard_map/ppermute | solution.py:211
  14.4 13.9 %collective-permute-start.3 = (f32[8,32,128]{2,1,0:T(8,128)S(1)}, f32[8,32,128]{2,1,0:T(8,128)S(1)}, u32[]{:S(2)}, u32[]{:S(2)}) collective-permute-start(f32[8,32,128]{2,1,0:T(8,128)S(1)} %get-tuple-element.49), channel_id=1, source_target_pairs={{4,8},{8,4},{5,9},{9,5},{6,10},{10,6},{7,11},{11,7},{20,24},{24,20... | collective-permute-start | bytes 393224 | tf_op jit(solution)/shard_map/ppermute | solution.py:211
  20.2 24.0 %collective-permute-start.15 = (f32[16,32,128]{2,1,0:T(8,128)S(1)}, f32[16,32,128]{2,1,0:T(8,128)S(1)}, u32[]{:S(2)}, u32[]{:S(2)}) collective-permute-start(f32[16,32,128]{2,1,0:T(8,128)S(1)} %get-tuple-element.66), channel_id=1, source_target_pairs={{0,16},{16,0},{32,48},{48,32},{64,80},{80,64},{96,112},{112,96},{1... | collective-permute-start | bytes 786440 | tf_op jit(solution)/shard_map/ppermute | solution.py:211
  22.0 24.4 %collective-permute-start.16 = (f32[16,32,128]{2,1,0:T(8,128)S(1)}, f32[16,32,128]{2,1,0:T(8,128)S(1)}, u32[]{:S(2)}, u32[]{:S(2)}) collective-permute-start(f32[16,32,128]{2,1,0:T(8,128)S(1)} %get-tuple-element.67), channel_id=1, source_target_pairs={{16,32},{32,16},{48,64},{64,48},{80,96},{96,80},{112,128},{128,112... | collective-permute-start | bytes 786440 | tf_op jit(solution)/shard_map/ppermute | solution.py:211
  28.3 13.1 %collective-permute-start.17 = (f32[8,32,128]{2,1,0:T(8,128)S(1)}, f32[8,32,128]{2,1,0:T(8,128)S(1)}, u32[]{:S(2)}, u32[]{:S(2)}) collective-permute-start(f32[8,32,128]{2,1,0:T(8,128)S(1)} %get-tuple-element.68), channel_id=1, source_target_pairs={{0,4},{4,0},{8,12},{12,8},{1,5},{5,1},{9,13},{13,9},{2,6},{6,2},{1... | collective-permute-start | bytes 393224 | tf_op jit(solution)/shard_map/ppermute | solution.py:211
  28.3 15.9 %collective-permute-start.18 = (f32[8,32,128]{2,1,0:T(8,128)S(1)}, f32[8,32,128]{2,1,0:T(8,128)S(1)}, u32[]{:S(2)}, u32[]{:S(2)}) collective-permute-start(f32[8,32,128]{2,1,0:T(8,128)S(1)} %get-tuple-element.69), channel_id=1, source_target_pairs={{4,8},{8,4},{5,9},{9,5},{6,10},{10,6},{7,11},{11,7},{20,24},{24,20... | collective-permute-start | bytes 393224 | tf_op jit(solution)/shard_map/ppermute | solution.py:211
  30.9 9.1 %collective-permute-start.19 = (f32[8,16,128]{2,1,0:T(8,128)S(1)}, f32[8,16,128]{2,1,0:T(8,128)S(1)}, u32[]{:S(2)}, u32[]{:S(2)}) collective-permute-start(f32[8,16,128]{2,1,0:T(8,128)S(1)} %get-tuple-element.70), channel_id=1, source_target_pairs={{0,2},{2,0},{1,3},{3,1},{4,6},{6,4},{5,7},{7,5},{8,10},{10,8},{9,1... | collective-permute-start | bytes 196616 | tf_op jit(solution)/shard_map/ppermute | solution.py:211
  40.0 20.6 %collective-permute-start.5 = (f32[16,32,128]{2,1,0:T(8,128)S(1)}, f32[16,32,128]{2,1,0:T(8,128)S(1)}, u32[]{:S(2)}, u32[]{:S(2)}) collective-permute-start(f32[16,32,128]{2,1,0:T(8,128)S(1)} %get-tuple-element.52), channel_id=1, source_target_pairs={{0,16},{16,0},{32,48},{48,32},{64,80},{80,64},{96,112},{112,96},{1... | collective-permute-start | bytes 786440 | tf_op jit(solution)/shard_map/ppermute | solution.py:211
  41.4 21.3 %collective-permute-start.6 = (f32[16,32,128]{2,1,0:T(8,128)S(1)}, f32[16,32,128]{2,1,0:T(8,128)S(1)}, u32[]{:S(2)}, u32[]{:S(2)}) collective-permute-start(f32[16,32,128]{2,1,0:T(8,128)S(1)} %get-tuple-element.53), channel_id=1, source_target_pairs={{16,32},{32,16},{48,64},{64,48},{80,96},{96,80},{112,128},{128,112... | collective-permute-start | bytes 786440 | tf_op jit(solution)/shard_map/ppermute | solution.py:211
  44.2 11.8 %collective-permute-start.7 = (f32[8,32,128]{2,1,0:T(8,128)S(1)}, f32[8,32,128]{2,1,0:T(8,128)S(1)}, u32[]{:S(2)}, u32[]{:S(2)}) collective-permute-start(f32[8,32,128]{2,1,0:T(8,128)S(1)} %get-tuple-element.54), channel_id=1, source_target_pairs={{0,4},{4,0},{8,12},{12,8},{1,5},{5,1},{9,13},{13,9},{2,6},{6,2},{1... | collective-permute-start | bytes 393224 | tf_op jit(solution)/shard_map/ppermute | solution.py:211
  44.2 8.2 %collective-permute-start.9 = (f32[8,16,128]{2,1,0:T(8,128)S(1)}, f32[8,16,128]{2,1,0:T(8,128)S(1)}, u32[]{:S(2)}, u32[]{:S(2)}) collective-permute-start(f32[8,16,128]{2,1,0:T(8,128)S(1)} %get-tuple-element.56), channel_id=1, source_target_pairs={{0,2},{2,0},{1,3},{3,1},{4,6},{6,4},{5,7},{7,5},{8,10},{10,8},{9,1... | collective-permute-start | bytes 196616 | tf_op jit(solution)/shard_map/ppermute | solution.py:211
  46.5 14.1 %collective-permute-start.8 = (f32[8,32,128]{2,1,0:T(8,128)S(1)}, f32[8,32,128]{2,1,0:T(8,128)S(1)}, u32[]{:S(2)}, u32[]{:S(2)}) collective-permute-start(f32[8,32,128]{2,1,0:T(8,128)S(1)} %get-tuple-element.55), channel_id=1, source_target_pairs={{4,8},{8,4},{5,9},{9,5},{6,10},{10,6},{7,11},{11,7},{20,24},{24,20... | collective-permute-start | bytes 393224 | tf_op jit(solution)/shard_map/ppermute | solution.py:211
  52.4 25.0 %collective-permute-start.20 = (f32[16,32,128]{2,1,0:T(8,128)S(1)}, f32[16,32,128]{2,1,0:T(8,128)S(1)}, u32[]{:S(2)}, u32[]{:S(2)}) collective-permute-start(f32[16,32,128]{2,1,0:T(8,128)S(1)} %get-tuple-element.72), channel_id=1, source_target_pairs={{0,16},{16,0},{32,48},{48,32},{64,80},{80,64},{96,112},{112,96},{1... | collective-permute-start | bytes 786440 | tf_op jit(solution)/shard_map/ppermute | solution.py:211
  56.1 23.8 %collective-permute-start.21 = (f32[16,32,128]{2,1,0:T(8,128)S(1)}, f32[16,32,128]{2,1,0:T(8,128)S(1)}, u32[]{:S(2)}, u32[]{:S(2)}) collective-permute-start(f32[16,32,128]{2,1,0:T(8,128)S(1)} %get-tuple-element.73), channel_id=1, source_target_pairs={{16,32},{32,16},{48,64},{64,48},{80,96},{96,80},{112,128},{128,112... | collective-permute-start | bytes 786440 | tf_op jit(solution)/shard_map/ppermute | solution.py:211
  60.6 13.4 %collective-permute-start.22 = (f32[8,32,128]{2,1,0:T(8,128)S(1)}, f32[8,32,128]{2,1,0:T(8,128)S(1)}, u32[]{:S(2)}, u32[]{:S(2)}) collective-permute-start(f32[8,32,128]{2,1,0:T(8,128)S(1)} %get-tuple-element.74), channel_id=1, source_target_pairs={{0,4},{4,0},{8,12},{12,8},{1,5},{5,1},{9,13},{13,9},{2,6},{6,2},{1... | collective-permute-start | bytes 393224 | tf_op jit(solution)/shard_map/ppermute | solution.py:211
  60.6 16.2 %collective-permute-start.23 = (f32[8,32,128]{2,1,0:T(8,128)S(1)}, f32[8,32,128]{2,1,0:T(8,128)S(1)}, u32[]{:S(2)}, u32[]{:S(2)}) collective-permute-start(f32[8,32,128]{2,1,0:T(8,128)S(1)} %get-tuple-element.75), channel_id=1, source_target_pairs={{4,8},{8,4},{5,9},{9,5},{6,10},{10,6},{7,11},{11,7},{20,24},{24,20... | collective-permute-start | bytes 393224 | tf_op jit(solution)/shard_map/ppermute | solution.py:211
  62.7 9.7 %collective-permute-start.24 = (f32[8,16,128]{2,1,0:T(8,128)S(1)}, f32[8,16,128]{2,1,0:T(8,128)S(1)}, u32[]{:S(2)}, u32[]{:S(2)}) collective-permute-start(f32[8,16,128]{2,1,0:T(8,128)S(1)} %get-tuple-element.76), channel_id=1, source_target_pairs={{0,2},{2,0},{1,3},{3,1},{4,6},{6,4},{5,7},{7,5},{8,10},{10,8},{9,1... | collective-permute-start | bytes 196616 | tf_op jit(solution)/shard_map/ppermute | solution.py:211
  72.5 18.7 %collective-permute-start.10 = (f32[16,32,128]{2,1,0:T(8,128)S(1)}, f32[16,32,128]{2,1,0:T(8,128)S(1)}, u32[]{:S(2)}, u32[]{:S(2)}) collective-permute-start(f32[16,32,128]{2,1,0:T(8,128)S(1)} %get-tuple-element.58), channel_id=1, source_target_pairs={{0,16},{16,0},{32,48},{48,32},{64,80},{80,64},{96,112},{112,96},{1... | collective-permute-start | bytes 786440 | tf_op jit(solution)/shard_map/ppermute | solution.py:211
  73.9 15.9 %collective-permute-start.12 = (f32[8,32,128]{2,1,0:T(8,128)S(1)}, f32[8,32,128]{2,1,0:T(8,128)S(1)}, u32[]{:S(2)}, u32[]{:S(2)}) collective-permute-start(f32[8,32,128]{2,1,0:T(8,128)S(1)} %get-tuple-element.60), channel_id=1, source_target_pairs={{0,4},{4,0},{8,12},{12,8},{1,5},{5,1},{9,13},{13,9},{2,6},{6,2},{1... | collective-permute-start | bytes 393224 | tf_op jit(solution)/shard_map/ppermute | solution.py:211
  76.8 21.8 %collective-permute-start.11 = (f32[16,32,128]{2,1,0:T(8,128)S(1)}, f32[16,32,128]{2,1,0:T(8,128)S(1)}, u32[]{:S(2)}, u32[]{:S(2)}) collective-permute-start(f32[16,32,128]{2,1,0:T(8,128)S(1)} %get-tuple-element.59), channel_id=1, source_target_pairs={{16,32},{32,16},{48,64},{64,48},{80,96},{96,80},{112,128},{128,112... | collective-permute-start | bytes 786440 | tf_op jit(solution)/shard_map/ppermute | solution.py:211
  77.5 8.3 %collective-permute-start.14 = (f32[8,16,128]{2,1,0:T(8,128)S(1)}, f32[8,16,128]{2,1,0:T(8,128)S(1)}, u32[]{:S(2)}, u32[]{:S(2)}) collective-permute-start(f32[8,16,128]{2,1,0:T(8,128)S(1)} %get-tuple-element.62), channel_id=1, source_target_pairs={{0,2},{2,0},{1,3},{3,1},{4,6},{6,4},{5,7},{7,5},{8,10},{10,8},{9,1... | collective-permute-start | bytes 196616 | tf_op jit(solution)/shard_map/ppermute | solution.py:211
  79.9 11.3 %collective-permute-start.13 = (f32[8,32,128]{2,1,0:T(8,128)S(1)}, f32[8,32,128]{2,1,0:T(8,128)S(1)}, u32[]{:S(2)}, u32[]{:S(2)}) collective-permute-start(f32[8,32,128]{2,1,0:T(8,128)S(1)} %get-tuple-element.61), channel_id=1, source_target_pairs={{4,8},{8,4},{5,9},{9,5},{6,10},{10,6},{7,11},{11,7},{20,24},{24,20... | collective-permute-start | bytes 393224 | tf_op jit(solution)/shard_map/ppermute | solution.py:211
  85.7 21.7 %collective-permute-start.25 = (f32[16,32,128]{2,1,0:T(8,128)S(1)}, f32[16,32,128]{2,1,0:T(8,128)S(1)}, u32[]{:S(2)}, u32[]{:S(2)}) collective-permute-start(f32[16,32,128]{2,1,0:T(8,128)S(1)} %get-tuple-element.78), channel_id=1, source_target_pairs={{0,16},{16,0},{32,48},{48,32},{64,80},{80,64},{96,112},{112,96},{1... | collective-permute-start | bytes 786440 | tf_op jit(solution)/shard_map/ppermute | solution.py:211
  89.8 17.7 %collective-permute-start.26 = (f32[16,32,128]{2,1,0:T(8,128)S(1)}, f32[16,32,128]{2,1,0:T(8,128)S(1)}, u32[]{:S(2)}, u32[]{:S(2)}) collective-permute-start(f32[16,32,128]{2,1,0:T(8,128)S(1)} %get-tuple-element.79), channel_id=1, source_target_pairs={{16,32},{32,16},{48,64},{64,48},{80,96},{96,80},{112,128},{128,112... | collective-permute-start | bytes 786440 | tf_op jit(solution)/shard_map/ppermute | solution.py:211
  91.2 16.2 %collective-permute-start.27 = (f32[8,32,128]{2,1,0:T(8,128)S(1)}, f32[8,32,128]{2,1,0:T(8,128)S(1)}, u32[]{:S(2)}, u32[]{:S(2)}) collective-permute-start(f32[8,32,128]{2,1,0:T(8,128)S(1)} %get-tuple-element.80), channel_id=1, source_target_pairs={{0,4},{4,0},{8,12},{12,8},{1,5},{5,1},{9,13},{13,9},{2,6},{6,2},{1... | collective-permute-start | bytes 393224 | tf_op jit(solution)/shard_map/ppermute | solution.py:211
  91.2 16.2 %collective-permute-start.28 = (f32[8,32,128]{2,1,0:T(8,128)S(1)}, f32[8,32,128]{2,1,0:T(8,128)S(1)}, u32[]{:S(2)}, u32[]{:S(2)}) collective-permute-start(f32[8,32,128]{2,1,0:T(8,128)S(1)} %get-tuple-element.81), channel_id=1, source_target_pairs={{4,8},{8,4},{5,9},{9,5},{6,10},{10,6},{7,11},{11,7},{20,24},{24,20... | collective-permute-start | bytes 393224 | tf_op jit(solution)/shard_map/ppermute | solution.py:211
  98.5 8.9 %collective-permute-start.29 = (f32[8,16,128]{2,1,0:T(8,128)S(1)}, f32[8,16,128]{2,1,0:T(8,128)S(1)}, u32[]{:S(2)}, u32[]{:S(2)}) collective-permute-start(f32[8,16,128]{2,1,0:T(8,128)S(1)} %get-tuple-element.82), channel_id=1, source_target_pairs={{0,2},{2,0},{1,3},{3,1},{4,6},{6,4},{5,7},{7,5},{8,10},{10,8},{9,1... | collective-permute-start | bytes 196616 | tf_op jit(solution)/shard_map/ppermute | solution.py:211

commit v2 on v1

--- a/solution.py
+++ b/solution.py
@@ -167,23 +167,47 @@
             state = state + g[d]
 
 
-def finish_body(scale, fa, fb, base, potential, field):
-    nj, _, nk = fa.shape[:3]
+GROUP = 2
+
+
+def finish_body(scale, fa, fb, base, potential, field, pot, end, sems):
+    nj, ni, nk = fa.shape[:3]
     m = left()
-    for t in range(nk // TILE):
-        lo, hi = pl.ds(t * TILE, TILE), pl.ds(nk + t * TILE, TILE)
-
-        def both(a, b):
-            return jnp.where(m, a, swap(b)), jnp.where(m, swap(a), b)
-
-        acc0, acc1 = both(base[0, lo, :], base[0, hi, :])
-        for j in range(nj):
-            v0, v1 = both(fa[j, 0, lo, :], fb[j, 0, lo, :])
-            field[j, 0, lo, :] = v0
-            field[j, 0, hi, :] = v1
-            acc0, acc1 = acc0 + v0, acc1 + v1
-            potential[j, 0, lo, :] = acc0 * scale
-            potential[j, 0, hi, :] = acc1 * scale
+
+    def both(a, b):
+        return jnp.where(m, a, swap(b)), jnp.where(m, swap(a), b)
+
+    def copies(g):
+        part = pl.ds(g * GROUP, GROUP)
+        return (
+            pltpu.make_async_copy(pot.at[:, part], potential.at[:, part], sems.at[g, 0]),
+            pltpu.make_async_copy(end.at[:, part], field.at[:, part], sems.at[g, 1]),
+        )
+
+    def at(g, _):
+        for n in range(GROUP):
+            i = g * GROUP + n
+            for t in range(nk // TILE):
+                lo, hi = pl.ds(t * TILE, TILE), pl.ds(nk + t * TILE, TILE)
+                acc0, acc1 = both(base[i, lo, :], base[i, hi, :])
+                for j in range(nj):
+                    v0, v1 = both(fa[j, i, lo, :], fb[j, i, lo, :])
+                    end[j, i, lo, :] = v0
+                    end[j, i, hi, :] = v1
+                    acc0, acc1 = acc0 + v0, acc1 + v1
+                    pot[j, i, lo, :] = acc0 * scale
+                    pot[j, i, hi, :] = acc1 * scale
+        for copy in copies(g):
+            copy.start()
+        return 0
+
+    def finished(g, _):
+        for copy in copies(g):
+            copy.wait()
+        return 0
+
+    lax.fori_loop(0, ni // GROUP, at, 0)
+    lax.fori_loop(0, ni // GROUP, finished, 0)
 
 
 def pairs(size, start):
@@ -193,7 +217,7 @@
     return out
 
 
-KINDS = ("k", "c1", "c0", "r0", "r1")
+KINDS = ("r1", "c1", "k", "c0", "r0")
 
 
 def exchange(faces):
@@ -251,16 +275,15 @@
     gathered = lax.all_to_all(total.reshape(rows, ni * nk // rows, nl), "rows", 0, 0, tiled=True)
     before = call(prefix_body, [gathered.shape], (gathered,))[0]
     base = lax.all_to_all(before, "rows", 0, 0, tiled=True).reshape(ni, nk, nl)
-    full = pl.BlockSpec((nj, 1, nk, nl), lambda i: (0, i, 0, 0))
-    part = pl.BlockSpec((nj, 1, nk // 2, nl), lambda i: (0, i, 0, 0))
-    potential, field = call(
+    potential, field = pl.pallas_call(
         functools.partial(finish_body, 1.0 / (nj * rows)),
-        [field_values.shape] * 2,
-        (f[0], f[1], base),
-        grid=(ni,),
-        in_specs=[part, part, pl.BlockSpec((1, nk, nl), lambda i: (i, 0, 0))],
-        out_specs=[full, full],
-    )
+        out_shape=[jax.ShapeDtypeStruct(field_values.shape, jnp.float32)] * 2,
+        in_specs=[VMEM] * 3,
+        out_specs=[pl.BlockSpec(memory_space=pltpu.MemorySpace.HBM)] * 2,
+        scratch_shapes=[pltpu.VMEM(field_values.shape, jnp.float32)] * 2
+        + [pltpu.SemaphoreType.DMA((ni // GROUP, 2))],
+        compiler_params=pltpu.CompilerParams(vmem_limit_bytes=16 * 1024 * 1024),
+    )(f[0], f[1], base)
     return potential, field
 
 

time: 152 us -> 148 us (0.974)
  Pallas kernels: 23.7 us -> 19.5 us
    pallas_call x10 -> x9, Pallas kernels: 23.7 us -> 15.8 us  [call(): pl.pallas_call(body, out_shape=[jax.ShapeDtypeStruct(s, jnp.float32) for...]
    pallas_call x0 -> x1, Pallas kernels: none -> 3.65 us  [on_device(): pl.pallas_call(functools.partial(finish_body, 1.0 / (nj * rows)), out_sha...]
  transfers between devices with their start and end apart: 30 -> 30, of which waited for: 10 -> 10; matrix products, arithmetic and copies ran while one was open for 0% -> 0% of each run, Pallas kernels for 7% -> 8%
where the time goes in v2:
time: 148 us
  starting transfers between devices  59.8 us (40%)
  blocking collectives  34.6 us (23%)
  waiting for transfers between devices  30.5 us (21%)
  Pallas kernels  19.5 us (13%)
  local copies, waits for them, and re-layouts  2.19 us (1%)
    ppermute x30, starting transfers between devices, exchange(): got[kind] = lax.ppermute(*sends[kind])  59.8 us
    ppermute x30, waiting for transfers between devices, exchange(): got[kind] = lax.ppermute(*sends[kind])  30.5 us
    all_to_all x1, blocking collectives, on_device(): lax.all_to_all(total.reshape(rows, ni * nk // rows, nl), 'rows', 0, 0, ti...  21.2 us
    pallas_call x9, Pallas kernels, call(): pl.pallas_call(body, out_shape=[jax.ShapeDtypeStruct(s, jnp.float32) for...  15.8 us
    all_to_all x1, blocking collectives, on_device(): base = lax.all_to_all(before, 'rows', 0, 0, tiled=True).reshape(ni, nk, nl)  13.5 us
    pallas_call x1, Pallas kernels, on_device(): pl.pallas_call(functools.partial(finish_body, 1.0 / (nj * rows)), out_sha...  3.65 us
  transfers between devices with their start and end apart: 30, of which 10 were waited for; matrix products, arithmetic and copies ran while one was open for 0% of the time, Pallas kernels for 8%

profile of v2, /device:TPU:4, one launch (start us, length us, event | category | flops | bytes accessed | tf_op | source)
XLA Modules:
  0.0 147.6 jit_solution(4604208539846982298)
XLA Ops:
  0.6 0.1 pad_add_fusion.place
  0.7 2.2 %copy-done = f32[8,16,64,128]{3,2,1,0:T(8,128)S(1)} copy-done((f32[8,16,64,128]{3,2,1,0:T(8,128)S(1)}, f32[8,16,64,128]{3,2,1,0:T(8,128)}, u32[]{:S(2)}) %copy-start) | copy-done | bytes 4194328
  2.9 2.9 %shard_map.41 = (f32[8,16,32,128]{3,2,1,0:T(8,128)S(1)}, f32[8,16,32,128]{3,2,1,0:T(8,128)S(1)}, f32[16,32,128]{2,1,0:T(8,128)S(1)}, f32[16,32,128]{2,1,0:T(8,12...) custom-call(s32[3]{0:T(128)S(1)} %pad_add_fusion.place, ...), custom_call_target="tpu_custom_call" | custom-call | tf_op jit(solution)/shard_map/pallas_call | solution.py:19
  5.8 0.1 collective-permute-start
  5.9 0.7 collective-permute-start.1
  6.6 2.3 %collective-permute-start.2 = (f32[8,32,128]{2,1,0:T(8,128)S(1)}, f32[8,32,128]{2,1,0:T(8,128)S(1)}, u32[]{:S(2)}, u32[]{:S(2)}) collective-permute-start(f32[8,32,128]{2,1,0:T(8,128)S(1)} %get-tuple-element.48), channel_id=1, source_target_pairs={{0,4},{4,0},{8,12},{12,8},{1,5},{5,1},{9,13},{13,9},{2,6},{6,2},{1... | collective-permute-start | bytes 393224 | tf_op jit(solution)/shard_map/ppermute | solution.py:235
  8.9 5.5 %collective-permute-start.4 = (f32[8,16,128]{2,1,0:T(8,128)S(1)}, f32[8,16,128]{2,1,0:T(8,128)S(1)}, u32[]{:S(2)}, u32[]{:S(2)}) collective-permute-start(f32[8,16,128]{2,1,0:T(8,128)S(1)} %get-tuple-element.50), channel_id=1, source_target_pairs={{0,2},{2,0},{1,3},{3,1},{4,6},{6,4},{5,7},{7,5},{8,10},{10,8},{9,1... | collective-permute-start | bytes 196616 | tf_op jit(solution)/shard_map/ppermute | solution.py:235
  14.4 5.8 %collective-permute-start.3 = (f32[8,32,128]{2,1,0:T(8,128)S(1)}, f32[8,32,128]{2,1,0:T(8,128)S(1)}, u32[]{:S(2)}, u32[]{:S(2)}) collective-permute-start(f32[8,32,128]{2,1,0:T(8,128)S(1)} %get-tuple-element.49), channel_id=1, source_target_pairs={{4,8},{8,4},{5,9},{9,5},{6,10},{10,6},{7,11},{11,7},{20,24},{24,20... | collective-permute-start | bytes 393224 | tf_op jit(solution)/shard_map/ppermute | solution.py:235
  20.2 1.8 %collective-permute-start.15 = (f32[16,32,128]{2,1,0:T(8,128)S(1)}, f32[16,32,128]{2,1,0:T(8,128)S(1)}, u32[]{:S(2)}, u32[]{:S(2)}) collective-permute-start(f32[16,32,128]{2,1,0:T(8,128)S(1)} %get-tuple-element.66), channel_id=1, source_target_pairs={{0,16},{16,0},{32,48},{48,32},{64,80},{80,64},{96,112},{112,96},{1... | collective-permute-start | bytes 786440 | tf_op jit(solution)/shard_map/ppermute | solution.py:235
  22.0 0.7 collective-permute-start.16
  22.7 5.6 %collective-permute-done.3.c1 = f32[8,32,128]{2,1,0:T(8,128)S(1)} collective-permute-done((f32[8,32,128]{2,1,0:T(8,128)S(1)}, f32[8,32,128]{2,1,0:T(8,128)S(1)}, u32[]{:S(2)}, u32[]{:S(2)}) %collective-permute-start.3) | collective-permute-done | bytes 131104 | tf_op jit(solution)/shard_map/ppermute | solution.py:235
  28.3 0.0 collective-permute-done.r0
  28.3 2.6 %collective-permute-start.18 = (f32[8,32,128]{2,1,0:T(8,128)S(1)}, f32[8,32,128]{2,1,0:T(8,128)S(1)}, u32[]{:S(2)}, u32[]{:S(2)}) collective-permute-start(f32[8,32,128]{2,1,0:T(8,128)S(1)} %get-tuple-element.69), channel_id=1, source_target_pairs={{4,8},{8,4},{5,9},{9,5},{6,10},{10,6},{7,11},{11,7},{20,24},{24,20... | collective-permute-start | bytes 393224 | tf_op jit(solution)/shard_map/ppermute | solution.py:235
  30.9 0.0 collective-permute-done.1.r1
  30.9 1.8 %collective-permute-start.19 = (f32[8,16,128]{2,1,0:T(8,128)S(1)}, f32[8,16,128]{2,1,0:T(8,128)S(1)}, u32[]{:S(2)}, u32[]{:S(2)}) collective-permute-start(f32[8,16,128]{2,1,0:T(8,128)S(1)} %get-tuple-element.70), channel_id=1, source_target_pairs={{0,2},{2,0},{1,3},{3,1},{4,6},{6,4},{5,7},{7,5},{8,10},{10,8},{9,1... | collective-permute-start | bytes 196616 | tf_op jit(solution)/shard_map/ppermute | solution.py:235
  32.7 2.2 %shard_map.42 = (f32[8,16,32,128]{3,2,1,0:T(8,128)S(1)}, f32[8,16,32,128]{3,2,1,0:T(8,128)S(1)}) custom-call(f32[8,16,64,128]{3,2,1,0:T(8,128)S(1)} %copy-done.1), custom_call_target="tpu_custom_call" | custom-call | tf_op jit(solution)/shard_map/pallas_call | solution.py:19
  34.9 1.8 %shard_map.43 = (f32[8,16,32,128]{3,2,1,0:T(8,128)S(1)}, f32[16,32,128]{2,1,0:T(8,128)S(1)}, f32[16,32,128]{2,1,0:T(8,128)S(1)}, f32[8,32,128]{2,1,0:T(8,128)S(1...) custom-call(s32[3]{0:T(128)S(1)} %pad_add_fusion.place, f32[8,16,32,128]{3,2,1,0:T(8,128)S(1)} %get-tuple-element.44.f, ...), custom_call_target="tpu_custom_call" | custom-call | tf_op jit(solution)/shard_map/pallas_call | solution.py:19
  36.7 3.3 %collective-permute-done.19.ks = f32[8,16,128]{2,1,0:T(8,128)S(1)} collective-permute-done((f32[8,16,128]{2,1,0:T(8,128)S(1)}, f32[8,16,128]{2,1,0:T(8,128)S(1)}, u32[]{:S(2)}, u32[]{:S(2)}) %collective-permute-start.19) | collective-permute-done | bytes 65568 | tf_op jit(solution)/shard_map/ppermute | solution.py:235
  40.0 1.4 collective-permute-start.5
  41.4 0.7 collective-permute-start.6
  42.1 2.1 %collective-permute-done.18.c1 = f32[8,32,128]{2,1,0:T(8,128)S(1)} collective-permute-done((f32[8,32,128]{2,1,0:T(8,128)S(1)}, f32[8,32,128]{2,1,0:T(8,128)S(1)}, u32[]{:S(2)}, u32[]{:S(2)}) %collective-permute-start.18) | collective-permute-done | bytes 131104 | tf_op jit(solution)/shard_map/ppermute | solution.py:235
  44.2 0.0 collective-permute-start.7
  44.2 0.0 collective-permute-done.15.r0
  44.2 2.2 %collective-permute-start.9 = (f32[8,16,128]{2,1,0:T(8,128)S(1)}, f32[8,16,128]{2,1,0:T(8,128)S(1)}, u32[]{:S(2)}, u32[]{:S(2)}) collective-permute-start(f32[8,16,128]{2,1,0:T(8,128)S(1)} %get-tuple-element.56), channel_id=1, source_target_pairs={{0,2},{2,0},{1,3},{3,1},{4,6},{6,4},{5,7},{7,5},{8,10},{10,8},{9,1... | collective-permute-start | bytes 196616 | tf_op jit(solution)/shard_map/ppermute | solution.py:235
  46.5 2.9 %collective-permute-start.8 = (f32[8,32,128]{2,1,0:T(8,128)S(1)}, f32[8,32,128]{2,1,0:T(8,128)S(1)}, u32[]{:S(2)}, u32[]{:S(2)}) collective-permute-start(f32[8,32,128]{2,1,0:T(8,128)S(1)} %get-tuple-element.55), channel_id=1, source_target_pairs={{4,8},{8,4},{5,9},{9,5},{6,10},{10,6},{7,11},{11,7},{20,24},{24,20... | collective-permute-start | bytes 393224 | tf_op jit(solution)/shard_map/ppermute | solution.py:235
  49.4 1.8 %shard_map.46 = (f32[8,16,32,128]{3,2,1,0:T(8,128)S(1)}, f32[16,32,128]{2,1,0:T(8,128)S(1)}, f32[16,32,128]{2,1,0:T(8,128)S(1)}, f32[8,32,128]{2,1,0:T(8,128)S(1...) custom-call(s32[3]{0:T(128)S(1)} %pad_add_fusion.place, f32[8,16,32,128]{3,2,1,0:T(8,128)S(1)} %get-tuple-element.64.f, ...), custom_call_target="tpu_custom_call" | custom-call | tf_op jit(solution)/shard_map/pallas_call | solution.py:19
  51.2 1.2 collective-permute-done.9.ks
  52.4 3.7 %collective-permute-start.20 = (f32[16,32,128]{2,1,0:T(8,128)S(1)}, f32[16,32,128]{2,1,0:T(8,128)S(1)}, u32[]{:S(2)}, u32[]{:S(2)}) collective-permute-start(f32[16,32,128]{2,1,0:T(8,128)S(1)} %get-tuple-element.72), channel_id=1, source_target_pairs={{0,16},{16,0},{32,48},{48,32},{64,80},{80,64},{96,112},{112,96},{1... | collective-permute-start | bytes 786440 | tf_op jit(solution)/shard_map/ppermute | solution.py:235
  56.1 0.7 collective-permute-start.21
  56.8 3.8 %collective-permute-done.8.c1 = f32[8,32,128]{2,1,0:T(8,128)S(1)} collective-permute-done((f32[8,32,128]{2,1,0:T(8,128)S(1)}, f32[8,32,128]{2,1,0:T(8,128)S(1)}, u32[]{:S(2)}, u32[]{:S(2)}) %collective-permute-start.8) | collective-permute-done | bytes 131104 | tf_op jit(solution)/shard_map/ppermute | solution.py:235
  60.6 0.0 collective-permute-start.22
  60.6 0.0 collective-permute-done.5.r0
  60.6 2.1 %collective-permute-start.23 = (f32[8,32,128]{2,1,0:T(8,128)S(1)}, f32[8,32,128]{2,1,0:T(8,128)S(1)}, u32[]{:S(2)}, u32[]{:S(2)}) collective-permute-start(f32[8,32,128]{2,1,0:T(8,128)S(1)} %get-tuple-element.75), channel_id=1, source_target_pairs={{4,8},{8,4},{5,9},{9,5},{6,10},{10,6},{7,11},{11,7},{20,24},{24,20... | collective-permute-start | bytes 393224 | tf_op jit(solution)/shard_map/ppermute | solution.py:235
  62.7 0.0 collective-permute-done.6.r1
  62.7 3.8 %collective-permute-start.24 = (f32[8,16,128]{2,1,0:T(8,128)S(1)}, f32[8,16,128]{2,1,0:T(8,128)S(1)}, u32[]{:S(2)}, u32[]{:S(2)}) collective-permute-start(f32[8,16,128]{2,1,0:T(8,128)S(1)} %get-tuple-element.76), channel_id=1, source_target_pairs={{0,2},{2,0},{1,3},{3,1},{4,6},{6,4},{5,7},{7,5},{8,10},{10,8},{9,1... | collective-permute-start | bytes 196616 | tf_op jit(solution)/shard_map/ppermute | solution.py:235
  66.6 1.8 %shard_map.44 = (f32[8,16,32,128]{3,2,1,0:T(8,128)S(1)}, f32[16,32,128]{2,1,0:T(8,128)S(1)}, f32[16,32,128]{2,1,0:T(8,128)S(1)}, f32[8,32,128]{2,1,0:T(8,128)S(1...) custom-call(s32[3]{0:T(128)S(1)} %pad_add_fusion.place, f32[8,16,32,128]{3,2,1,0:T(8,128)S(1)} %get-tuple-element.51.f, ...), custom_call_target="tpu_custom_call" | custom-call | tf_op jit(solution)/shard_map/pallas_call | solution.py:19
  68.4 4.1 %collective-permute-done.24.ks = f32[8,16,128]{2,1,0:T(8,128)S(1)} collective-permute-done((f32[8,16,128]{2,1,0:T(8,128)S(1)}, f32[8,16,128]{2,1,0:T(8,128)S(1)}, u32[]{:S(2)}, u32[]{:S(2)}) %collective-permute-start.24) | collective-permute-done | bytes 65568 | tf_op jit(solution)/shard_map/ppermute | solution.py:235
  72.5 1.4 collective-permute-start.10
  73.9 0.0 collective-permute-done.22.c0
  73.9 0.0 collective-permute-start.12
  73.9 2.9 %collective-permute-done.23.c1 = f32[8,32,128]{2,1,0:T(8,128)S(1)} collective-permute-done((f32[8,32,128]{2,1,0:T(8,128)S(1)}, f32[8,32,128]{2,1,0:T(8,128)S(1)}, u32[]{:S(2)}, u32[]{:S(2)}) %collective-permute-start.23) | collective-permute-done | bytes 131104 | tf_op jit(solution)/shard_map/ppermute | solution.py:235
  76.8 0.7 collective-permute-start.11
  77.5 0.0 collective-permute-done.20.r0
  77.5 2.4 %collective-permute-start.14 = (f32[8,16,128]{2,1,0:T(8,128)S(1)}, f32[8,16,128]{2,1,0:T(8,128)S(1)}, u32[]{:S(2)}, u32[]{:S(2)}) collective-permute-start(f32[8,16,128]{2,1,0:T(8,128)S(1)} %get-tuple-element.62), channel_id=1, source_target_pairs={{0,2},{2,0},{1,3},{3,1},{4,6},{6,4},{5,7},{7,5},{8,10},{10,8},{9,1... | collective-permute-start | bytes 196616 | tf_op jit(solution)/shard_map/ppermute | solution.py:235
  79.9 0.0 collective-permute-done.21.r1
  79.9 3.0 %collective-permute-start.13 = (f32[8,32,128]{2,1,0:T(8,128)S(1)}, f32[8,32,128]{2,1,0:T(8,128)S(1)}, u32[]{:S(2)}, u32[]{:S(2)}) collective-permute-start(f32[8,32,128]{2,1,0:T(8,128)S(1)} %get-tuple-element.61), channel_id=1, source_target_pairs={{4,8},{8,4},{5,9},{9,5},{6,10},{10,6},{7,11},{11,7},{20,24},{24,20... | collective-permute-start | bytes 393224 | tf_op jit(solution)/shard_map/ppermute | solution.py:235
  83.0 1.8 %shard_map.47 = (f32[8,16,32,128]{3,2,1,0:T(8,128)S(1)}, f32[16,32,128]{2,1,0:T(8,128)S(1)}, f32[16,32,128]{2,1,0:T(8,128)S(1)}, f32[8,32,128]{2,1,0:T(8,128)S(1...) custom-call(s32[3]{0:T(128)S(1)} %pad_add_fusion.place, f32[8,16,32,128]{3,2,1,0:T(8,128)S(1)} %get-tuple-element.71.f, ...), custom_call_target="tpu_custom_call" | custom-call | tf_op jit(solution)/shard_map/pallas_call | solution.py:19
  84.8 1.0 collective-permute-done.14.ks
  85.7 4.1 %collective-permute-start.25 = (f32[16,32,128]{2,1,0:T(8,128)S(1)}, f32[16,32,128]{2,1,0:T(8,128)S(1)}, u32[]{:S(2)}, u32[]{:S(2)}) collective-permute-start(f32[16,32,128]{2,1,0:T(8,128)S(1)} %get-tuple-element.78), channel_id=1, source_target_pairs={{0,16},{16,0},{32,48},{48,32},{64,80},{80,64},{96,112},{112,96},{1... | collective-permute-start | bytes 786440 | tf_op jit(solution)/shard_map/ppermute | solution.py:235
  89.8 0.0 collective-permute-done.12.c0
  89.8 0.7 collective-permute-start.26
  90.5 0.7 collective-permute-done.13.c1
  91.2 0.0 collective-permute-start.27
  91.2 0.0 collective-permute-done.10.r0
  91.2 7.3 %collective-permute-start.28 = (f32[8,32,128]{2,1,0:T(8,128)S(1)}, f32[8,32,128]{2,1,0:T(8,128)S(1)}, u32[]{:S(2)}, u32[]{:S(2)}) collective-permute-start(f32[8,32,128]{2,1,0:T(8,128)S(1)} %get-tuple-element.81), channel_id=1, source_target_pairs={{4,8},{8,4},{5,9},{9,5},{6,10},{10,6},{7,11},{11,7},{20,24},{24,20... | collective-permute-start | bytes 393224 | tf_op jit(solution)/shard_map/ppermute | solution.py:235
  98.5 0.0 collective-permute-done.11.r1
  98.5 1.4 collective-permute-start.29
  100.0 1.8 %shard_map.45 = (f32[8,16,32,128]{3,2,1,0:T(8,128)S(1)}, f32[16,32,128]{2,1,0:T(8,128)S(1)}) custom-call(s32[3]{0:T(128)S(1)} %pad_add_fusion.place, f32[8,16,32,128]{3,2,1,0:T(8,128)S(1)} %get-tuple-element.57.f, f32[8,16,32,128]{3,2,1,0:T(8,128)S(1)} %get-tuple-element.45.c, f32[16,32,128]{2,1,0:T(8,128)S(1)} %collective-permute-done.10.r0, ...), custom_call_target="tpu_custom_call" | custom-call | tf_op jit(solution)/shard_map/pallas_call | solution.py:19
  101.8 5.7 %collective-permute-done.29.ks = f32[8,16,128]{2,1,0:T(8,128)S(1)} collective-permute-done((f32[8,16,128]{2,1,0:T(8,128)S(1)}, f32[8,16,128]{2,1,0:T(8,128)S(1)}, u32[]{:S(2)}, u32[]{:S(2)}) %collective-permute-start.29) | collective-permute-done | bytes 65568 | tf_op jit(solution)/shard_map/ppermute | solution.py:235
  107.4 0.0 collective-permute-done.27.c0
  107.5 1.8 %shard_map.48 = (f32[8,16,32,128]{3,2,1,0:T(8,128)S(1)}, f32[16,64,128]{2,1,0:T(8,128)S(1)}) custom-call(s32[3]{0:T(128)S(1)} %pad_add_fusion.place, f32[8,16,32,128]{3,2,1,0:T(8,128)S(1)} %get-tuple-element.77.f, f32[8,16,32,128]{3,2,1,0:T(8,128)S(1)} %get-tuple-element.65.c, f32[16,32,128]{2,1,0:T(8,128)S(1)} %collective-permute-done.25.r0, ...), custom_call_target="tpu_custom_call" | custom-call | tf_op jit(solution)/shard_map/pallas_call | solution.py:19
  109.2 21.2 %all_to_all.10.g = f32[16,64,128]{2,1,0:T(8,128)S(1)} all-to-all(f32[16,64,128]{2,1,0:T(8,128)S(1)} %get-tuple-element.85), channel_id=1, replica_groups=mesh['rows'=16,'cols'=4,'slabs'=2,'trial'=2] {'rows'}, dimensions={0} | all-to-all | bytes 1048576 | tf_op jit(solution)/shard_map/all_to_all | solution.py:275
  130.5 13.5 %all_to_all.11.base = f32[16,64,128]{2,1,0:T(8,128)S(1)} all-to-all(f32[16,64,128]{2,1,0:T(8,128)S(1)} %shard_map.49), channel_id=1, replica_groups=mesh['rows'=16,'cols'=4,'slabs'=2,'trial'=2] {'rows'}, dimensions={0} | all-to-all | bytes 1048576 | tf_op jit(solution)/shard_map/all_to_all | solution.py:277
  143.9 3.6 %shard_map.50 = (f32[8,16,64,128]{3,2,1,0:T(8,128)}, f32[8,16,64,128]{3,2,1,0:T(8,128)}) custom-call(f32[8,16,32,128]{3,2,1,0:T(8,128)S(1)} %get-tuple-element.63.fa, f32[8,16,32,128]{3,2,1,0:T(8,128)S(1)} %get-tuple-element.84.fb, f32[16,64,128]{2,1,0:T(8,128)S(1)} %all_to_all.11.base), custom_call_target="tpu_custom_call" | custom-call | tf_op jit(solution)/shard_map/pallas_call | solution.py:278
  (13 shorter events, 0.1 us)
Async XLA Ops:
  0.7 2.2 %copy-start = (f32[8,16,64,128]{3,2,1,0:T(8,128)S(1)}, f32[8,16,64,128]{3,2,1,0:T(8,128)}, u32[]{:S(2)}) copy-start(f32[8,16,64,128]{3,2,1,0:T(8,128)} %f.1) | copy-start | bytes 12582916
  2.9 29.8 %copy-start.1 = (f32[8,16,64,128]{3,2,1,0:T(8,128)S(1)}, f32[8,16,64,128]{3,2,1,0:T(8,128)}, u32[]{:S(2)}) copy-start(f32[8,16,64,128]{3,2,1,0:T(8,128)} %c.1) | copy-start | bytes 12582916
  5.8 22.5 %collective-permute-start = (f32[16,32,128]{2,1,0:T(8,128)S(1)}, f32[16,32,128]{2,1,0:T(8,128)S(1)}, u32[]{:S(2)}, u32[]{:S(2)}) collective-permute-start(f32[16,32,128]{2,1,0:T(8,128)S(1)} %get-tuple-element.46), channel_id=1, source_target_pairs={{0,16},{16,0},{32,48},{48,32},{64,80},{80,64},{96,112},{112,96},{1... | collective-permute-start | bytes 786440 | tf_op jit(solution)/shard_map/ppermute | solution.py:235
  5.9 25.0 %collective-permute-start.1 = (f32[16,32,128]{2,1,0:T(8,128)S(1)}, f32[16,32,128]{2,1,0:T(8,128)S(1)}, u32[]{:S(2)}, u32[]{:S(2)}) collective-permute-start(f32[16,32,128]{2,1,0:T(8,128)S(1)} %get-tuple-element.47), channel_id=1, source_target_pairs={{16,32},{32,16},{48,64},{64,48},{80,96},{96,80},{112,128},{128,112... | collective-permute-start | bytes 786440 | tf_op jit(solution)/shard_map/ppermute | solution.py:235
  6.6 15.4 %collective-permute-start.2 = (f32[8,32,128]{2,1,0:T(8,128)S(1)}, f32[8,32,128]{2,1,0:T(8,128)S(1)}, u32[]{:S(2)}, u32[]{:S(2)}) collective-permute-start(f32[8,32,128]{2,1,0:T(8,128)S(1)} %get-tuple-element.48), channel_id=1, source_target_pairs={{0,4},{4,0},{8,12},{12,8},{1,5},{5,1},{9,13},{13,9},{2,6},{6,2},{1... | collective-permute-start | bytes 393224 | tf_op jit(solution)/shard_map/ppermute | solution.py:235
  8.9 11.3 %collective-permute-start.4 = (f32[8,16,128]{2,1,0:T(8,128)S(1)}, f32[8,16,128]{2,1,0:T(8,128)S(1)}, u32[]{:S(2)}, u32[]{:S(2)}) collective-permute-start(f32[8,16,128]{2,1,0:T(8,128)S(1)} %get-tuple-element.50), channel_id=1, source_target_pairs={{0,2},{2,0},{1,3},{3,1},{4,6},{6,4},{5,7},{7,5},{8,10},{10,8},{9,1... | collective-permute-start | bytes 196616 | tf_op jit(solution)/shard_map/ppermute | solution.py:235
  14.4 13.9 %collective-permute-start.3 = (f32[8,32,128]{2,1,0:T(8,128)S(1)}, f32[8,32,128]{2,1,0:T(8,128)S(1)}, u32[]{:S(2)}, u32[]{:S(2)}) collective-permute-start(f32[8,32,128]{2,1,0:T(8,128)S(1)} %get-tuple-element.49), channel_id=1, source_target_pairs={{4,8},{8,4},{5,9},{9,5},{6,10},{10,6},{7,11},{11,7},{20,24},{24,20... | collective-permute-start | bytes 393224 | tf_op jit(solution)/shard_map/ppermute | solution.py:235
  20.2 24.0 %collective-permute-start.15 = (f32[16,32,128]{2,1,0:T(8,128)S(1)}, f32[16,32,128]{2,1,0:T(8,128)S(1)}, u32[]{:S(2)}, u32[]{:S(2)}) collective-permute-start(f32[16,32,128]{2,1,0:T(8,128)S(1)} %get-tuple-element.66), channel_id=1, source_target_pairs={{0,16},{16,0},{32,48},{48,32},{64,80},{80,64},{96,112},{112,96},{1... | collective-permute-start | bytes 786440 | tf_op jit(solution)/shard_map/ppermute | solution.py:235
  22.0 24.4 %collective-permute-start.16 = (f32[16,32,128]{2,1,0:T(8,128)S(1)}, f32[16,32,128]{2,1,0:T(8,128)S(1)}, u32[]{:S(2)}, u32[]{:S(2)}) collective-permute-start(f32[16,32,128]{2,1,0:T(8,128)S(1)} %get-tuple-element.67), channel_id=1, source_target_pairs={{16,32},{32,16},{48,64},{64,48},{80,96},{96,80},{112,128},{128,112... | collective-permute-start | bytes 786440 | tf_op jit(solution)/shard_map/ppermute | solution.py:235
  28.3 13.1 %collective-permute-start.17 = (f32[8,32,128]{2,1,0:T(8,128)S(1)}, f32[8,32,128]{2,1,0:T(8,128)S(1)}, u32[]{:S(2)}, u32[]{:S(2)}) collective-permute-start(f32[8,32,128]{2,1,0:T(8,128)S(1)} %get-tuple-element.68), channel_id=1, source_target_pairs={{0,4},{4,0},{8,12},{12,8},{1,5},{5,1},{9,13},{13,9},{2,6},{6,2},{1... | collective-permute-start | bytes 393224 | tf_op jit(solution)/shard_map/ppermute | solution.py:235
  28.3 15.9 %collective-permute-start.18 = (f32[8,32,128]{2,1,0:T(8,128)S(1)}, f32[8,32,128]{2,1,0:T(8,128)S(1)}, u32[]{:S(2)}, u32[]{:S(2)}) collective-permute-start(f32[8,32,128]{2,1,0:T(8,128)S(1)} %get-tuple-element.69), channel_id=1, source_target_pairs={{4,8},{8,4},{5,9},{9,5},{6,10},{10,6},{7,11},{11,7},{20,24},{24,20... | collective-permute-start | bytes 393224 | tf_op jit(solution)/shard_map/ppermute | solution.py:235
  30.9 9.1 %collective-permute-start.19 = (f32[8,16,128]{2,1,0:T(8,128)S(1)}, f32[8,16,128]{2,1,0:T(8,128)S(1)}, u32[]{:S(2)}, u32[]{:S(2)}) collective-permute-start(f32[8,16,128]{2,1,0:T(8,128)S(1)} %get-tuple-element.70), channel_id=1, source_target_pairs={{0,2},{2,0},{1,3},{3,1},{4,6},{6,4},{5,7},{7,5},{8,10},{10,8},{9,1... | collective-permute-start | bytes 196616 | tf_op jit(solution)/shard_map/ppermute | solution.py:235
  40.0 20.6 %collective-permute-start.5 = (f32[16,32,128]{2,1,0:T(8,128)S(1)}, f32[16,32,128]{2,1,0:T(8,128)S(1)}, u32[]{:S(2)}, u32[]{:S(2)}) collective-permute-start(f32[16,32,128]{2,1,0:T(8,128)S(1)} %get-tuple-element.52), channel_id=1, source_target_pairs={{0,16},{16,0},{32,48},{48,32},{64,80},{80,64},{96,112},{112,96},{1... | collective-permute-start | bytes 786440 | tf_op jit(solution)/shard_map/ppermute | solution.py:235
  41.4 21.3 %collective-permute-start.6 = (f32[16,32,128]{2,1,0:T(8,128)S(1)}, f32[16,32,128]{2,1,0:T(8,128)S(1)}, u32[]{:S(2)}, u32[]{:S(2)}) collective-permute-start(f32[16,32,128]{2,1,0:T(8,128)S(1)} %get-tuple-element.53), channel_id=1, source_target_pairs={{16,32},{32,16},{48,64},{64,48},{80,96},{96,80},{112,128},{128,112... | collective-permute-start | bytes 786440 | tf_op jit(solution)/shard_map/ppermute | solution.py:235
  44.2 11.8 %collective-permute-start.7 = (f32[8,32,128]{2,1,0:T(8,128)S(1)}, f32[8,32,128]{2,1,0:T(8,128)S(1)}, u32[]{:S(2)}, u32[]{:S(2)}) collective-permute-start(f32[8,32,128]{2,1,0:T(8,128)S(1)} %get-tuple-element.54), channel_id=1, source_target_pairs={{0,4},{4,0},{8,12},{12,8},{1,5},{5,1},{9,13},{13,9},{2,6},{6,2},{1... | collective-permute-start | bytes 393224 | tf_op jit(solution)/shard_map/ppermute | solution.py:235
  44.2 8.2 %collective-permute-start.9 = (f32[8,16,128]{2,1,0:T(8,128)S(1)}, f32[8,16,128]{2,1,0:T(8,128)S(1)}, u32[]{:S(2)}, u32[]{:S(2)}) collective-permute-start(f32[8,16,128]{2,1,0:T(8,128)S(1)} %get-tuple-element.56), channel_id=1, source_target_pairs={{0,2},{2,0},{1,3},{3,1},{4,6},{6,4},{5,7},{7,5},{8,10},{10,8},{9,1... | collective-permute-start | bytes 196616 | tf_op jit(solution)/shard_map/ppermute | solution.py:235
  46.5 14.1 %collective-permute-start.8 = (f32[8,32,128]{2,1,0:T(8,128)S(1)}, f32[8,32,128]{2,1,0:T(8,128)S(1)}, u32[]{:S(2)}, u32[]{:S(2)}) collective-permute-start(f32[8,32,128]{2,1,0:T(8,128)S(1)} %get-tuple-element.55), channel_id=1, source_target_pairs={{4,8},{8,4},{5,9},{9,5},{6,10},{10,6},{7,11},{11,7},{20,24},{24,20... | collective-permute-start | bytes 393224 | tf_op jit(solution)/shard_map/ppermute | solution.py:235
  52.4 25.0 %collective-permute-start.20 = (f32[16,32,128]{2,1,0:T(8,128)S(1)}, f32[16,32,128]{2,1,0:T(8,128)S(1)}, u32[]{:S(2)}, u32[]{:S(2)}) collective-permute-start(f32[16,32,128]{2,1,0:T(8,128)S(1)} %get-tuple-element.72), channel_id=1, source_target_pairs={{0,16},{16,0},{32,48},{48,32},{64,80},{80,64},{96,112},{112,96},{1... | collective-permute-start | bytes 786440 | tf_op jit(solution)/shard_map/ppermute | solution.py:235
  56.1 23.8 %collective-permute-start.21 = (f32[16,32,128]{2,1,0:T(8,128)S(1)}, f32[16,32,128]{2,1,0:T(8,128)S(1)}, u32[]{:S(2)}, u32[]{:S(2)}) collective-permute-start(f32[16,32,128]{2,1,0:T(8,128)S(1)} %get-tuple-element.73), channel_id=1, source_target_pairs={{16,32},{32,16},{48,64},{64,48},{80,96},{96,80},{112,128},{128,112... | collective-permute-start | bytes 786440 | tf_op jit(solution)/shard_map/ppermute | solution.py:235
  60.6 13.4 %collective-permute-start.22 = (f32[8,32,128]{2,1,0:T(8,128)S(1)}, f32[8,32,128]{2,1,0:T(8,128)S(1)}, u32[]{:S(2)}, u32[]{:S(2)}) collective-permute-start(f32[8,32,128]{2,1,0:T(8,128)S(1)} %get-tuple-element.74), channel_id=1, source_target_pairs={{0,4},{4,0},{8,12},{12,8},{1,5},{5,1},{9,13},{13,9},{2,6},{6,2},{1... | collective-permute-start | bytes 393224 | tf_op jit(solution)/shard_map/ppermute | solution.py:235
  60.6 16.2 %collective-permute-start.23 = (f32[8,32,128]{2,1,0:T(8,128)S(1)}, f32[8,32,128]{2,1,0:T(8,128)S(1)}, u32[]{:S(2)}, u32[]{:S(2)}) collective-permute-start(f32[8,32,128]{2,1,0:T(8,128)S(1)} %get-tuple-element.75), channel_id=1, source_target_pairs={{4,8},{8,4},{5,9},{9,5},{6,10},{10,6},{7,11},{11,7},{20,24},{24,20... | collective-permute-start | bytes 393224 | tf_op jit(solution)/shard_map/ppermute | solution.py:235
  62.7 9.7 %collective-permute-start.24 = (f32[8,16,128]{2,1,0:T(8,128)S(1)}, f32[8,16,128]{2,1,0:T(8,128)S(1)}, u32[]{:S(2)}, u32[]{:S(2)}) collective-permute-start(f32[8,16,128]{2,1,0:T(8,128)S(1)} %get-tuple-element.76), channel_id=1, source_target_pairs={{0,2},{2,0},{1,3},{3,1},{4,6},{6,4},{5,7},{7,5},{8,10},{10,8},{9,1... | collective-permute-start | bytes 196616 | tf_op jit(solution)/shard_map/ppermute | solution.py:235
  72.5 18.7 %collective-permute-start.10 = (f32[16,32,128]{2,1,0:T(8,128)S(1)}, f32[16,32,128]{2,1,0:T(8,128)S(1)}, u32[]{:S(2)}, u32[]{:S(2)}) collective-permute-start(f32[16,32,128]{2,1,0:T(8,128)S(1)} %get-tuple-element.58), channel_id=1, source_target_pairs={{0,16},{16,0},{32,48},{48,32},{64,80},{80,64},{96,112},{112,96},{1... | collective-permute-start | bytes 786440 | tf_op jit(solution)/shard_map/ppermute | solution.py:235
  73.9 15.9 %collective-permute-start.12 = (f32[8,32,128]{2,1,0:T(8,128)S(1)}, f32[8,32,128]{2,1,0:T(8,128)S(1)}, u32[]{:S(2)}, u32[]{:S(2)}) collective-permute-start(f32[8,32,128]{2,1,0:T(8,128)S(1)} %get-tuple-element.60), channel_id=1, source_target_pairs={{0,4},{4,0},{8,12},{12,8},{1,5},{5,1},{9,13},{13,9},{2,6},{6,2},{1... | collective-permute-start | bytes 393224 | tf_op jit(solution)/shard_map/ppermute | solution.py:235
  76.8 21.8 %collective-permute-start.11 = (f32[16,32,128]{2,1,0:T(8,128)S(1)}, f32[16,32,128]{2,1,0:T(8,128)S(1)}, u32[]{:S(2)}, u32[]{:S(2)}) collective-permute-start(f32[16,32,128]{2,1,0:T(8,128)S(1)} %get-tuple-element.59), channel_id=1, source_target_pairs={{16,32},{32,16},{48,64},{64,48},{80,96},{96,80},{112,128},{128,112... | collective-permute-start | bytes 786440 | tf_op jit(solution)/shard_map/ppermute | solution.py:235
  77.5 8.3 %collective-permute-start.14 = (f32[8,16,128]{2,1,0:T(8,128)S(1)}, f32[8,16,128]{2,1,0:T(8,128)S(1)}, u32[]{:S(2)}, u32[]{:S(2)}) collective-permute-start(f32[8,16,128]{2,1,0:T(8,128)S(1)} %get-tuple-element.62), channel_id=1, source_target_pairs={{0,2},{2,0},{1,3},{3,1},{4,6},{6,4},{5,7},{7,5},{8,10},{10,8},{9,1... | collective-permute-start | bytes 196616 | tf_op jit(solution)/shard_map/ppermute | solution.py:235
  79.9 11.3 %collective-permute-start.13 = (f32[8,32,128]{2,1,0:T(8,128)S(1)}, f32[8,32,128]{2,1,0:T(8,128)S(1)}, u32[]{:S(2)}, u32[]{:S(2)}) collective-permute-start(f32[8,32,128]{2,1,0:T(8,128)S(1)} %get-tuple-element.61), channel_id=1, source_target_pairs={{4,8},{8,4},{5,9},{9,5},{6,10},{10,6},{7,11},{11,7},{20,24},{24,20... | collective-permute-start | bytes 393224 | tf_op jit(solution)/shard_map/ppermute | solution.py:235
  85.7 21.7 %collective-permute-start.25 = (f32[16,32,128]{2,1,0:T(8,128)S(1)}, f32[16,32,128]{2,1,0:T(8,128)S(1)}, u32[]{:S(2)}, u32[]{:S(2)}) collective-permute-start(f32[16,32,128]{2,1,0:T(8,128)S(1)} %get-tuple-element.78), channel_id=1, source_target_pairs={{0,16},{16,0},{32,48},{48,32},{64,80},{80,64},{96,112},{112,96},{1... | collective-permute-start | bytes 786440 | tf_op jit(solution)/shard_map/ppermute | solution.py:235
  89.8 17.7 %collective-permute-start.26 = (f32[16,32,128]{2,1,0:T(8,128)S(1)}, f32[16,32,128]{2,1,0:T(8,128)S(1)}, u32[]{:S(2)}, u32[]{:S(2)}) collective-permute-start(f32[16,32,128]{2,1,0:T(8,128)S(1)} %get-tuple-element.79), channel_id=1, source_target_pairs={{16,32},{32,16},{48,64},{64,48},{80,96},{96,80},{112,128},{128,112... | collective-permute-start | bytes 786440 | tf_op jit(solution)/shard_map/ppermute | solution.py:235
  91.2 16.2 %collective-permute-start.27 = (f32[8,32,128]{2,1,0:T(8,128)S(1)}, f32[8,32,128]{2,1,0:T(8,128)S(1)}, u32[]{:S(2)}, u32[]{:S(2)}) collective-permute-start(f32[8,32,128]{2,1,0:T(8,128)S(1)} %get-tuple-element.80), channel_id=1, source_target_pairs={{0,4},{4,0},{8,12},{12,8},{1,5},{5,1},{9,13},{13,9},{2,6},{6,2},{1... | collective-permute-start | bytes 393224 | tf_op jit(solution)/shard_map/ppermute | solution.py:235
  91.2 16.2 %collective-permute-start.28 = (f32[8,32,128]{2,1,0:T(8,128)S(1)}, f32[8,32,128]{2,1,0:T(8,128)S(1)}, u32[]{:S(2)}, u32[]{:S(2)}) collective-permute-start(f32[8,32,128]{2,1,0:T(8,128)S(1)} %get-tuple-element.81), channel_id=1, source_target_pairs={{4,8},{8,4},{5,9},{9,5},{6,10},{10,6},{7,11},{11,7},{20,24},{24,20... | collective-permute-start | bytes 393224 | tf_op jit(solution)/shard_map/ppermute | solution.py:235
  98.5 8.9 %collective-permute-start.29 = (f32[8,16,128]{2,1,0:T(8,128)S(1)}, f32[8,16,128]{2,1,0:T(8,128)S(1)}, u32[]{:S(2)}, u32[]{:S(2)}) collective-permute-start(f32[8,16,128]{2,1,0:T(8,128)S(1)} %get-tuple-element.82), channel_id=1, source_target_pairs={{0,2},{2,0},{1,3},{3,1},{4,6},{6,4},{5,7},{7,5},{8,10},{10,8},{9,1... | collective-permute-start | bytes 196616 | tf_op jit(solution)/shard_map/ppermute | solution.py:235

commit v3 on v2

--- a/solution.py
+++ b/solution.py
@@ -40,13 +40,23 @@
     return jnp.where(m, a, swap(b)), jnp.where(m, swap(a), b)
 
 
-def write_faces(place, out, s_c0, s_c1, s_k):
-    nj, ni, nk = out.shape[:3]
+def edge_rows(place, block, j):
+    nk = block.shape[2]
+    return jnp.where(place[2] == 0, block[j, :, nk - 1, :], block[j, :, 0, :])
+
+
+def write_faces(place, out, s_c0, s_c1, s_k, other):
+    nj, ni = out.shape[:2]
+    wide = left((ni, 128))
     for j in range(nj):
         first, last = out[j, 0], out[j, ni - 1]
         s_c0[j] = jnp.where(place[1] == 0, last, first)
         s_c1[j] = jnp.where(place[1] == 0, first, last)
-        s_k[j] = jnp.where(place[2] == 0, out[j, :, nk - 1, :], out[j, :, 0, :])
+        rows = edge_rows(place, out, j)
+        if other is not None:
+            mine = swap(rows)
+            rows = jnp.where(place[2] == 0, jnp.where(wide, mine, other[j]), jnp.where(wide, other[j], mine))
+        s_k[j] = rows
 
 
 def pack_field(place, f, fa, fb, *faces):
@@ -69,8 +79,8 @@
         return 0
 
     lax.fori_loop(0, ni, at, 0)
-    write_faces(place, fa, *sa[2:])
-    write_faces(place, fb, *sb[2:])
+    write_faces(place, fa, *sa[2:], None)
+    write_faces(place, fb, *sb[2:], sa[4])
 
 
 def pack_crowding(c, ca, cb):
@@ -87,9 +97,10 @@
     lax.fori_loop(0, ni, at, 0)
 
 
-def step_body(last, with_total, place, f, c, r0, r1, c0, c1, ks, *rest):
+def step_body(last, h, place, f, c, r0, r1, c0, c1, ks, *rest):
     rest = list(rest)
-    earlier = rest.pop(0) if with_total else None
+    earlier = rest.pop(0) if h else None
+    with_total = last and h == 1
     out = rest.pop(0)
     if last:
         total = rest.pop(0)
@@ -101,7 +112,7 @@
     tiles = nk // TILE
     wide = left((ni, 128))
     for j in range(nj):
-        x = swap(ks[j])
+        x = ks[j] if h else swap(ks[j])
         low_side = jnp.where(place[2] == 1, x, 0.0)
         high_side = jnp.where(place[2] == 0, x, 0.0)
         kl[j] = jnp.where(wide, low_side, swap(f[j, :, nk - 1, :]))
@@ -155,7 +166,7 @@
     lax.fori_loop(1, ni - 1, inner, 0)
     at(ni - 1, lambda j, t: f[j, ni - 2, ds(t), :], lambda j, t: jnp.where(even_c, c0[j, ds(t), :], c1[j, ds(t), :]))
     if not last:
-        write_faces(place, out, s_c0, s_c1, s_k)
+        write_faces(place, out, s_c0, s_c1, s_k, earlier)
 
 
 def prefix_body(g, out):
@@ -217,10 +228,10 @@
     return out
 
 
-KINDS = ("r1", "c1", "k", "c0", "r0")
-
-
-def exchange(faces):
+KINDS = (("r1", "c1", "c0", "r0"), ("k", "r1", "c1", "c0", "r0"))
+
+
+def exchange(faces, h):
     r0, r1, c0, c1, k = faces
     rows, cols, slabs = lax.axis_size("rows"), lax.axis_size("cols"), lax.axis_size("slabs")
     sends = {
@@ -231,9 +242,9 @@
         "r1": (r1, "rows", pairs(rows, 1)),
     }
     got = {}
-    for kind in KINDS:
+    for kind in KINDS[h]:
         got[kind] = lax.ppermute(*sends[kind])
-    return [got[kind] for kind in ("r0", "r1", "c0", "c1", "k")]
+    return [got[kind] for kind in ("r0", "r1", "c0", "c1")], got.get("k")
 
 
 def on_device(field_values, crowding):
@@ -246,33 +257,35 @@
         pack_field, [half, half] + faces + faces, (place, field_values), in_specs=[SMEM, VMEM]
     )
     f, sent = [out[0], out[1]], [out[2:7], out[7:12]]
-    halos = [exchange(sent[0]), exchange(sent[1])]
+    halos = [None, None]
+    for h in range(2):
+        halos[h], across = exchange(sent[h], h)
     c = call(pack_crowding, [half, half], (crowding,))
     scratch = [(nj, ni, nl)] * 2
-    total = None
+    extra = None
     for step in range(STEPS):
         last = step == STEPS - 1
         for h in range(2):
-            with_total = last and h == 1
-            args = (place, f[h], c[h], *halos[h]) + ((total,) if with_total else ())
+            args = (place, f[h], c[h], *halos[h], across) + ((extra,) if h else ())
             if last:
-                outs = [half, (ni, nk if with_total else nk // 2, nl)]
+                outs = [half, (ni, nk if h else nk // 2, nl)]
             else:
                 outs = [half] + faces
             res = call(
-                functools.partial(step_body, last, with_total),
+                functools.partial(step_body, last, h),
                 outs,
                 args,
                 scratch,
                 in_specs=[SMEM] + [VMEM] * (len(args) - 1),
             )
             f[h] = res[0]
-            if last:
-                total = res[1]
-            else:
-                halos[h] = exchange(res[1:])
+            extra = res[-1]
+            if not last:
+                halos[h], got = exchange(res[1:], h)
+        if not last:
+            across = got
     rows = lax.axis_size("rows")
-    gathered = lax.all_to_all(total.reshape(rows, ni * nk // rows, nl), "rows", 0, 0, tiled=True)
+    gathered = lax.all_to_all(extra.reshape(rows, ni * nk // rows, nl), "rows", 0, 0, tiled=True)
     before = call(prefix_body, [gathered.shape], (gathered,))[0]
     base = lax.all_to_all(before, "rows", 0, 0, tiled=True).reshape(ni, nk, nl)
     potential, field = pl.pallas_call(
@@ -289,6 +302,4 @@
 
 def solution(mesh):
     spec = P(("trial", "rows"), "cols", "slabs", None)
-    return jax.shard_map(
-        on_device, mesh=mesh, in_specs=(spec, spec), out_specs=(spec, spec), check_vma=False
-    )
+    return jax.shard_map(on_device, mesh=mesh, in_specs=(spec, spec), out_specs=(spec, spec), check_vma=False)

time: 148 us -> 139 us (0.939)
  the two profiles are of different devices: /device:TPU:4 before, /device:TPU:36 now
where the time goes in v3:
time: 139 us
  starting transfers between devices  69.9 us (50%)
  blocking collectives  34.9 us (25%)
  Pallas kernels  20.3 us (15%)
  waiting for transfers between devices  10.3 us (7%)
  local copies, waits for them, and re-layouts  2.19 us (2%)
    ppermute x27, starting transfers between devices, exchange(): got[kind] = lax.ppermute(*sends[kind])  69.9 us
    all_to_all x1, blocking collectives, on_device(): lax.all_to_all(extra.reshape(rows, ni * nk // rows, nl), 'rows', 0, 0, ti...  21.4 us
    pallas_call x9, Pallas kernels, call(): pl.pallas_call(body, out_shape=[jax.ShapeDtypeStruct(s, jnp.float32) for...  16.6 us
    all_to_all x1, blocking collectives, on_device(): base = lax.all_to_all(before, 'rows', 0, 0, tiled=True).reshape(ni, nk, nl)  13.5 us
    ppermute x27, waiting for transfers between devices, exchange(): got[kind] = lax.ppermute(*sends[kind])  10.3 us
    pallas_call x1, Pallas kernels, on_device(): pl.pallas_call(functools.partial(finish_body, 1.0 / (nj * rows)), out_sha...  3.65 us
  transfers between devices with their start and end apart: 27, of which 4 were waited for; matrix products, arithmetic and copies ran while one was open for 0% of the time, Pallas kernels for 8%

profile of v3, /device:TPU:36, one launch (start us, length us, event | category | flops | bytes accessed | tf_op | source)
XLA Modules:
  0.0 138.5 jit_solution(14436119738328628879)
XLA Ops:
  0.6 0.1 pad_add_fusion.place
  0.7 2.2 %copy-done = f32[8,16,64,128]{3,2,1,0:T(8,128)S(1)} copy-done((f32[8,16,64,128]{3,2,1,0:T(8,128)S(1)}, f32[8,16,64,128]{3,2,1,0:T(8,128)}, u32[]{:S(2)}) %copy-start) | copy-done | bytes 4194328
  2.9 3.5 %shard_map.41 = (f32[8,16,32,128]{3,2,1,0:T(8,128)S(1)}, f32[8,16,32,128]{3,2,1,0:T(8,128)S(1)}, f32[16,32,128]{2,1,0:T(8,128)S(1)}, f32[16,32,128]{2,1,0:T(8,12...) custom-call(s32[3]{0:T(128)S(1)} %pad_add_fusion.place, ...), custom_call_target="tpu_custom_call" | custom-call | tf_op jit(solution)/shard_map/pallas_call | solution.py:19
  6.4 0.0 collective-permute-start
  6.4 0.5 collective-permute-start.2
  7.0 6.3 %collective-permute-start.4 = (f32[8,16,128]{2,1,0:T(8,128)S(1)}, f32[8,16,128]{2,1,0:T(8,128)S(1)}, u32[]{:S(2)}, u32[]{:S(2)}) collective-permute-start(f32[8,16,128]{2,1,0:T(8,128)S(1)} %get-tuple-element.49), channel_id=1, source_target_pairs={{0,2},{2,0},{1,3},{3,1},{4,6},{6,4},{5,7},{7,5},{8,10},{10,8},{9,1... | collective-permute-start | bytes 196616 | tf_op jit(solution)/shard_map/ppermute | solution.py:246
  13.2 0.7 collective-permute-start.1
  13.9 5.8 %collective-permute-start.3 = (f32[8,32,128]{2,1,0:T(8,128)S(1)}, f32[8,32,128]{2,1,0:T(8,128)S(1)}, u32[]{:S(2)}, u32[]{:S(2)}) collective-permute-start(f32[8,32,128]{2,1,0:T(8,128)S(1)} %get-tuple-element.48), channel_id=1, source_target_pairs={{4,8},{8,4},{5,9},{9,5},{6,10},{10,6},{7,11},{11,7},{20,24},{24,20... | collective-permute-start | bytes 393224 | tf_op jit(solution)/shard_map/ppermute | solution.py:246
  19.8 0.0 collective-permute-done.4.ks
  19.8 1.7 %collective-permute-start.9 = (f32[16,32,128]{2,1,0:T(8,128)S(1)}, f32[16,32,128]{2,1,0:T(8,128)S(1)}, u32[]{:S(2)}, u32[]{:S(2)}) collective-permute-start(f32[16,32,128]{2,1,0:T(8,128)S(1)} %get-tuple-element.57), channel_id=1, source_target_pairs={{0,16},{16,0},{32,48},{48,32},{64,80},{80,64},{96,112},{112,96},{1... | collective-permute-start | bytes 786440 | tf_op jit(solution)/shard_map/ppermute | solution.py:246
  21.5 0.0 collective-permute-done.2.c0
  21.5 0.7 collective-permute-start.10
  22.2 3.7 %collective-permute-done.3.c1 = f32[8,32,128]{2,1,0:T(8,128)S(1)} collective-permute-done((f32[8,32,128]{2,1,0:T(8,128)S(1)}, f32[8,32,128]{2,1,0:T(8,128)S(1)}, u32[]{:S(2)}, u32[]{:S(2)}) %collective-permute-start.3) | collective-permute-done | bytes 131104 | tf_op jit(solution)/shard_map/ppermute | solution.py:246
  25.9 0.0 collective-permute-start.11
  25.9 0.0 collective-permute-done.r0
  25.9 7.7 %collective-permute-start.12 = (f32[8,32,128]{2,1,0:T(8,128)S(1)}, f32[8,32,128]{2,1,0:T(8,128)S(1)}, u32[]{:S(2)}, u32[]{:S(2)}) collective-permute-start(f32[8,32,128]{2,1,0:T(8,128)S(1)} %get-tuple-element.60), channel_id=1, source_target_pairs={{4,8},{8,4},{5,9},{9,5},{6,10},{10,6},{7,11},{11,7},{20,24},{24,20... | collective-permute-start | bytes 393224 | tf_op jit(solution)/shard_map/ppermute | solution.py:246
  33.6 2.2 %shard_map.42 = (f32[8,16,32,128]{3,2,1,0:T(8,128)S(1)}, f32[8,16,32,128]{3,2,1,0:T(8,128)S(1)}) custom-call(f32[8,16,64,128]{3,2,1,0:T(8,128)S(1)} %copy-done.1), custom_call_target="tpu_custom_call" | custom-call | tf_op jit(solution)/shard_map/pallas_call | solution.py:19
  35.8 0.0 collective-permute-done.1.r1
  35.8 1.8 %shard_map.43 = (f32[8,16,32,128]{3,2,1,0:T(8,128)S(1)}, f32[16,32,128]{2,1,0:T(8,128)S(1)}, f32[16,32,128]{2,1,0:T(8,128)S(1)}, f32[8,32,128]{2,1,0:T(8,128)S(1...) custom-call(s32[3]{0:T(128)S(1)} %pad_add_fusion.place, f32[8,16,32,128]{3,2,1,0:T(8,128)S(1)} %get-tuple-element.43.f, ...), custom_call_target="tpu_custom_call" | custom-call | tf_op jit(solution)/shard_map/pallas_call | solution.py:19
  37.6 0.2 collective-permute-start.5
  37.8 0.0 collective-permute-done.11.c0
  37.8 0.0 collective-permute-start.7
  37.8 0.0 collective-permute-done.12.c1
  37.8 0.0 collective-permute-done.9.r0
  37.8 0.0 collective-permute-done.10.r1
  37.8 1.9 %shard_map.44 = (f32[8,16,32,128]{3,2,1,0:T(8,128)S(1)}, f32[16,32,128]{2,1,0:T(8,128)S(1)}, f32[16,32,128]{2,1,0:T(8,128)S(1)}, f32[8,32,128]{2,1,0:T(8,128)S(1...) custom-call(s32[3]{0:T(128)S(1)} %pad_add_fusion.place, f32[8,16,32,128]{3,2,1,0:T(8,128)S(1)} %get-tuple-element.55.f, ...), custom_call_target="tpu_custom_call" | custom-call | tf_op jit(solution)/shard_map/pallas_call | solution.py:19
  39.7 1.6 %collective-permute-start.13 = (f32[8,16,128]{2,1,0:T(8,128)S(1)}, f32[8,16,128]{2,1,0:T(8,128)S(1)}, u32[]{:S(2)}, u32[]{:S(2)}) collective-permute-start(f32[8,16,128]{2,1,0:T(8,128)S(1)} %get-tuple-element.62), channel_id=1, source_target_pairs={{0,2},{2,0},{1,3},{3,1},{4,6},{6,4},{5,7},{7,5},{8,10},{10,8},{9,1... | collective-permute-start | bytes 196616 | tf_op jit(solution)/shard_map/ppermute | solution.py:246
  41.3 0.7 collective-permute-start.6
  42.0 7.4 %collective-permute-start.8 = (f32[8,32,128]{2,1,0:T(8,128)S(1)}, f32[8,32,128]{2,1,0:T(8,128)S(1)}, u32[]{:S(2)}, u32[]{:S(2)}) collective-permute-start(f32[8,32,128]{2,1,0:T(8,128)S(1)} %get-tuple-element.54), channel_id=1, source_target_pairs={{4,8},{8,4},{5,9},{9,5},{6,10},{10,6},{7,11},{11,7},{20,24},{24,20... | collective-permute-start | bytes 393224 | tf_op jit(solution)/shard_map/ppermute | solution.py:246
  49.4 0.0 collective-permute-done.13.ks
  49.4 3.0 %collective-permute-start.18 = (f32[16,32,128]{2,1,0:T(8,128)S(1)}, f32[16,32,128]{2,1,0:T(8,128)S(1)}, u32[]{:S(2)}, u32[]{:S(2)}) collective-permute-start(f32[16,32,128]{2,1,0:T(8,128)S(1)} %get-tuple-element.69), channel_id=1, source_target_pairs={{0,16},{16,0},{32,48},{48,32},{64,80},{80,64},{96,112},{112,96},{1... | collective-permute-start | bytes 786440 | tf_op jit(solution)/shard_map/ppermute | solution.py:246
  52.4 0.0 collective-permute-done.7.c0
  52.4 0.7 collective-permute-start.19
  53.0 0.0 collective-permute-done.8.c1
  53.0 0.1 collective-permute-start.20
  53.1 0.0 collective-permute-done.5.r0
  53.2 6.3 %collective-permute-start.21 = (f32[8,32,128]{2,1,0:T(8,128)S(1)}, f32[8,32,128]{2,1,0:T(8,128)S(1)}, u32[]{:S(2)}, u32[]{:S(2)}) collective-permute-start(f32[8,32,128]{2,1,0:T(8,128)S(1)} %get-tuple-element.72), channel_id=1, source_target_pairs={{4,8},{8,4},{5,9},{9,5},{6,10},{10,6},{7,11},{11,7},{20,24},{24,20... | collective-permute-start | bytes 393224 | tf_op jit(solution)/shard_map/ppermute | solution.py:246
  59.5 0.0 collective-permute-done.6.r1
  59.5 1.8 %shard_map.45 = (f32[8,16,32,128]{3,2,1,0:T(8,128)S(1)}, f32[16,32,128]{2,1,0:T(8,128)S(1)}, f32[16,32,128]{2,1,0:T(8,128)S(1)}, f32[8,32,128]{2,1,0:T(8,128)S(1...) custom-call(s32[3]{0:T(128)S(1)} %pad_add_fusion.place, f32[8,16,32,128]{3,2,1,0:T(8,128)S(1)} %get-tuple-element.50.f, ...), custom_call_target="tpu_custom_call" | custom-call | tf_op jit(solution)/shard_map/pallas_call | solution.py:19
  61.3 2.7 %collective-permute-start.14 = (f32[16,32,128]{2,1,0:T(8,128)S(1)}, f32[16,32,128]{2,1,0:T(8,128)S(1)}, u32[]{:S(2)}, u32[]{:S(2)}) collective-permute-start(f32[16,32,128]{2,1,0:T(8,128)S(1)} %get-tuple-element.64), channel_id=1, source_target_pairs={{0,16},{16,0},{32,48},{48,32},{64,80},{80,64},{96,112},{112,96},{1... | collective-permute-start | bytes 786440 | tf_op jit(solution)/shard_map/ppermute | solution.py:246
  64.0 0.0 collective-permute-done.20.c0
  64.0 0.0 collective-permute-start.16
  64.0 2.0 %collective-permute-done.21.c1 = f32[8,32,128]{2,1,0:T(8,128)S(1)} collective-permute-done((f32[8,32,128]{2,1,0:T(8,128)S(1)}, f32[8,32,128]{2,1,0:T(8,128)S(1)}, u32[]{:S(2)}, u32[]{:S(2)}) %collective-permute-start.21) | collective-permute-done | bytes 131104 | tf_op jit(solution)/shard_map/ppermute | solution.py:246
  66.1 0.0 collective-permute-done.18.r0
  66.1 0.0 collective-permute-done.19.r1
  66.1 1.9 %shard_map.46 = (f32[8,16,32,128]{3,2,1,0:T(8,128)S(1)}, f32[16,32,128]{2,1,0:T(8,128)S(1)}, f32[16,32,128]{2,1,0:T(8,128)S(1)}, f32[8,32,128]{2,1,0:T(8,128)S(1...) custom-call(s32[3]{0:T(128)S(1)} %pad_add_fusion.place, f32[8,16,32,128]{3,2,1,0:T(8,128)S(1)} %get-tuple-element.68.f, ...), custom_call_target="tpu_custom_call" | custom-call | tf_op jit(solution)/shard_map/pallas_call | solution.py:19
  67.9 4.1 %collective-permute-start.22 = (f32[8,16,128]{2,1,0:T(8,128)S(1)}, f32[8,16,128]{2,1,0:T(8,128)S(1)}, u32[]{:S(2)}, u32[]{:S(2)}) collective-permute-start(f32[8,16,128]{2,1,0:T(8,128)S(1)} %get-tuple-element.74), channel_id=1, source_target_pairs={{0,2},{2,0},{1,3},{3,1},{4,6},{6,4},{5,7},{7,5},{8,10},{10,8},{9,1... | collective-permute-start | bytes 196616 | tf_op jit(solution)/shard_map/ppermute | solution.py:246
  72.1 7.7 %collective-permute-start.17 = (f32[8,32,128]{2,1,0:T(8,128)S(1)}, f32[8,32,128]{2,1,0:T(8,128)S(1)}, u32[]{:S(2)}, u32[]{:S(2)}) collective-permute-start(f32[8,32,128]{2,1,0:T(8,128)S(1)} %get-tuple-element.67), channel_id=1, source_target_pairs={{4,8},{8,4},{5,9},{9,5},{6,10},{10,6},{7,11},{11,7},{20,24},{24,20... | collective-permute-start | bytes 393224 | tf_op jit(solution)/shard_map/ppermute | solution.py:246
  79.8 0.7 collective-permute-start.15
  80.5 0.0 collective-permute-done.22.ks
  80.5 6.5 %collective-permute-start.23 = (f32[16,32,128]{2,1,0:T(8,128)S(1)}, f32[16,32,128]{2,1,0:T(8,128)S(1)}, u32[]{:S(2)}, u32[]{:S(2)}) collective-permute-start(f32[16,32,128]{2,1,0:T(8,128)S(1)} %get-tuple-element.77), channel_id=1, source_target_pairs={{0,16},{16,0},{32,48},{48,32},{64,80},{80,64},{96,112},{112,96},{1... | collective-permute-start | bytes 786440 | tf_op jit(solution)/shard_map/ppermute | solution.py:246
  87.0 0.7 collective-permute-start.24
  87.7 0.0 collective-permute-done.17.c1
  87.7 0.1 collective-permute-start.25
  87.8 4.0 %collective-permute-start.26 = (f32[8,32,128]{2,1,0:T(8,128)S(1)}, f32[8,32,128]{2,1,0:T(8,128)S(1)}, u32[]{:S(2)}, u32[]{:S(2)}) collective-permute-start(f32[8,32,128]{2,1,0:T(8,128)S(1)} %get-tuple-element.80), channel_id=1, source_target_pairs={{4,8},{8,4},{5,9},{9,5},{6,10},{10,6},{7,11},{11,7},{20,24},{24,20... | collective-permute-start | bytes 393224 | tf_op jit(solution)/shard_map/ppermute | solution.py:246
  91.9 1.8 %shard_map.47 = (f32[8,16,32,128]{3,2,1,0:T(8,128)S(1)}, f32[16,32,128]{2,1,0:T(8,128)S(1)}) custom-call(s32[3]{0:T(128)S(1)} %pad_add_fusion.place, f32[8,16,32,128]{3,2,1,0:T(8,128)S(1)} %get-tuple-element.63.f, f32[8,16,32,128]{3,2,1,0:T(8,128)S(1)} %get-tuple-element.44.c, f32[16,32,128]{2,1,0:T(8,128)S(1)} %collective-permute-done.14.r0, ...), custom_call_target="tpu_custom_call" | custom-call | tf_op jit(solution)/shard_map/pallas_call | solution.py:19
  93.7 0.6 collective-permute-done.25.c0
  94.3 3.9 %collective-permute-done.26.c1 = f32[8,32,128]{2,1,0:T(8,128)S(1)} collective-permute-done((f32[8,32,128]{2,1,0:T(8,128)S(1)}, f32[8,32,128]{2,1,0:T(8,128)S(1)}, u32[]{:S(2)}, u32[]{:S(2)}) %collective-permute-start.26) | collective-permute-done | bytes 131104 | tf_op jit(solution)/shard_map/ppermute | solution.py:246
  98.2 0.0 collective-permute-done.23.r0
  98.2 0.0 collective-permute-done.24.r1
  98.2 1.8 %shard_map.48 = (f32[8,16,32,128]{3,2,1,0:T(8,128)S(1)}, f32[16,64,128]{2,1,0:T(8,128)S(1)}) custom-call(s32[3]{0:T(128)S(1)} %pad_add_fusion.place, f32[8,16,32,128]{3,2,1,0:T(8,128)S(1)} %get-tuple-element.76.f, f32[8,16,32,128]{3,2,1,0:T(8,128)S(1)} %get-tuple-element.56.c, f32[16,32,128]{2,1,0:T(8,128)S(1)} %collective-permute-done.23.r0, ...), custom_call_target="tpu_custom_call" | custom-call | tf_op jit(solution)/shard_map/pallas_call | solution.py:19
  100.0 21.4 %all_to_all.10.g = f32[16,64,128]{2,1,0:T(8,128)S(1)} all-to-all(f32[16,64,128]{2,1,0:T(8,128)S(1)} %get-tuple-element.83), channel_id=1, replica_groups=mesh['rows'=16,'cols'=4,'slabs'=2,'trial'=2] {'rows'}, dimensions={0} | all-to-all | bytes 1048576 | tf_op jit(solution)/shard_map/all_to_all | solution.py:288
  121.4 13.5 %all_to_all.11.base = f32[16,64,128]{2,1,0:T(8,128)S(1)} all-to-all(f32[16,64,128]{2,1,0:T(8,128)S(1)} %shard_map.49), channel_id=1, replica_groups=mesh['rows'=16,'cols'=4,'slabs'=2,'trial'=2] {'rows'}, dimensions={0} | all-to-all | bytes 1048576 | tf_op jit(solution)/shard_map/all_to_all | solution.py:290
  134.9 3.6 %shard_map.50 = (f32[8,16,64,128]{3,2,1,0:T(8,128)}, f32[8,16,64,128]{3,2,1,0:T(8,128)}) custom-call(f32[8,16,32,128]{3,2,1,0:T(8,128)S(1)} %get-tuple-element.75.fa, f32[8,16,32,128]{3,2,1,0:T(8,128)S(1)} %get-tuple-element.82.fb, f32[16,64,128]{2,1,0:T(8,128)S(1)} %all_to_all.11.base), custom_call_target="tpu_custom_call" | custom-call | tf_op jit(solution)/shard_map/pallas_call | solution.py:291
  (7 shorter events, 0.0 us)
Async XLA Ops:
  0.7 2.2 %copy-start = (f32[8,16,64,128]{3,2,1,0:T(8,128)S(1)}, f32[8,16,64,128]{3,2,1,0:T(8,128)}, u32[]{:S(2)}) copy-start(f32[8,16,64,128]{3,2,1,0:T(8,128)} %f.1) | copy-start | bytes 12582916
  2.9 30.7 %copy-start.1 = (f32[8,16,64,128]{3,2,1,0:T(8,128)S(1)}, f32[8,16,64,128]{3,2,1,0:T(8,128)}, u32[]{:S(2)}) copy-start(f32[8,16,64,128]{3,2,1,0:T(8,128)} %c.1) | copy-start | bytes 12582916
  6.4 19.5 %collective-permute-start = (f32[16,32,128]{2,1,0:T(8,128)S(1)}, f32[16,32,128]{2,1,0:T(8,128)S(1)}, u32[]{:S(2)}, u32[]{:S(2)}) collective-permute-start(f32[16,32,128]{2,1,0:T(8,128)S(1)} %get-tuple-element.45), channel_id=1, source_target_pairs={{0,16},{16,0},{32,48},{48,32},{64,80},{80,64},{96,112},{112,96},{1... | collective-permute-start | bytes 786440 | tf_op jit(solution)/shard_map/ppermute | solution.py:246
  6.4 15.1 %collective-permute-start.2 = (f32[8,32,128]{2,1,0:T(8,128)S(1)}, f32[8,32,128]{2,1,0:T(8,128)S(1)}, u32[]{:S(2)}, u32[]{:S(2)}) collective-permute-start(f32[8,32,128]{2,1,0:T(8,128)S(1)} %get-tuple-element.47), channel_id=1, source_target_pairs={{0,4},{4,0},{8,12},{12,8},{1,5},{5,1},{9,13},{13,9},{2,6},{6,2},{1... | collective-permute-start | bytes 393224 | tf_op jit(solution)/shard_map/ppermute | solution.py:246
  7.0 12.8 %collective-permute-start.4 = (f32[8,16,128]{2,1,0:T(8,128)S(1)}, f32[8,16,128]{2,1,0:T(8,128)S(1)}, u32[]{:S(2)}, u32[]{:S(2)}) collective-permute-start(f32[8,16,128]{2,1,0:T(8,128)S(1)} %get-tuple-element.49), channel_id=1, source_target_pairs={{0,2},{2,0},{1,3},{3,1},{4,6},{6,4},{5,7},{7,5},{8,10},{10,8},{9,1... | collective-permute-start | bytes 196616 | tf_op jit(solution)/shard_map/ppermute | solution.py:246
  13.2 22.5 %collective-permute-start.1 = (f32[16,32,128]{2,1,0:T(8,128)S(1)}, f32[16,32,128]{2,1,0:T(8,128)S(1)}, u32[]{:S(2)}, u32[]{:S(2)}) collective-permute-start(f32[16,32,128]{2,1,0:T(8,128)S(1)} %get-tuple-element.46), channel_id=1, source_target_pairs={{16,32},{32,16},{48,64},{64,48},{80,96},{96,80},{112,128},{128,112... | collective-permute-start | bytes 786440 | tf_op jit(solution)/shard_map/ppermute | solution.py:246
  13.9 12.0 %collective-permute-start.3 = (f32[8,32,128]{2,1,0:T(8,128)S(1)}, f32[8,32,128]{2,1,0:T(8,128)S(1)}, u32[]{:S(2)}, u32[]{:S(2)}) collective-permute-start(f32[8,32,128]{2,1,0:T(8,128)S(1)} %get-tuple-element.48), channel_id=1, source_target_pairs={{4,8},{8,4},{5,9},{9,5},{6,10},{10,6},{7,11},{11,7},{20,24},{24,20... | collective-permute-start | bytes 393224 | tf_op jit(solution)/shard_map/ppermute | solution.py:246
  19.8 18.0 %collective-permute-start.9 = (f32[16,32,128]{2,1,0:T(8,128)S(1)}, f32[16,32,128]{2,1,0:T(8,128)S(1)}, u32[]{:S(2)}, u32[]{:S(2)}) collective-permute-start(f32[16,32,128]{2,1,0:T(8,128)S(1)} %get-tuple-element.57), channel_id=1, source_target_pairs={{0,16},{16,0},{32,48},{48,32},{64,80},{80,64},{96,112},{112,96},{1... | collective-permute-start | bytes 786440 | tf_op jit(solution)/shard_map/ppermute | solution.py:246
  21.5 16.3 %collective-permute-start.10 = (f32[16,32,128]{2,1,0:T(8,128)S(1)}, f32[16,32,128]{2,1,0:T(8,128)S(1)}, u32[]{:S(2)}, u32[]{:S(2)}) collective-permute-start(f32[16,32,128]{2,1,0:T(8,128)S(1)} %get-tuple-element.58), channel_id=1, source_target_pairs={{16,32},{32,16},{48,64},{64,48},{80,96},{96,80},{112,128},{128,112... | collective-permute-start | bytes 786440 | tf_op jit(solution)/shard_map/ppermute | solution.py:246
  25.9 11.9 %collective-permute-start.11 = (f32[8,32,128]{2,1,0:T(8,128)S(1)}, f32[8,32,128]{2,1,0:T(8,128)S(1)}, u32[]{:S(2)}, u32[]{:S(2)}) collective-permute-start(f32[8,32,128]{2,1,0:T(8,128)S(1)} %get-tuple-element.59), channel_id=1, source_target_pairs={{0,4},{4,0},{8,12},{12,8},{1,5},{5,1},{9,13},{13,9},{2,6},{6,2},{1... | collective-permute-start | bytes 393224 | tf_op jit(solution)/shard_map/ppermute | solution.py:246
  25.9 11.9 %collective-permute-start.12 = (f32[8,32,128]{2,1,0:T(8,128)S(1)}, f32[8,32,128]{2,1,0:T(8,128)S(1)}, u32[]{:S(2)}, u32[]{:S(2)}) collective-permute-start(f32[8,32,128]{2,1,0:T(8,128)S(1)} %get-tuple-element.60), channel_id=1, source_target_pairs={{4,8},{8,4},{5,9},{9,5},{6,10},{10,6},{7,11},{11,7},{20,24},{24,20... | collective-permute-start | bytes 393224 | tf_op jit(solution)/shard_map/ppermute | solution.py:246
  37.6 15.6 %collective-permute-start.5 = (f32[16,32,128]{2,1,0:T(8,128)S(1)}, f32[16,32,128]{2,1,0:T(8,128)S(1)}, u32[]{:S(2)}, u32[]{:S(2)}) collective-permute-start(f32[16,32,128]{2,1,0:T(8,128)S(1)} %get-tuple-element.51), channel_id=1, source_target_pairs={{0,16},{16,0},{32,48},{48,32},{64,80},{80,64},{96,112},{112,96},{1... | collective-permute-start | bytes 786440 | tf_op jit(solution)/shard_map/ppermute | solution.py:246
  37.8 14.6 %collective-permute-start.7 = (f32[8,32,128]{2,1,0:T(8,128)S(1)}, f32[8,32,128]{2,1,0:T(8,128)S(1)}, u32[]{:S(2)}, u32[]{:S(2)}) collective-permute-start(f32[8,32,128]{2,1,0:T(8,128)S(1)} %get-tuple-element.53), channel_id=1, source_target_pairs={{0,4},{4,0},{8,12},{12,8},{1,5},{5,1},{9,13},{13,9},{2,6},{6,2},{1... | collective-permute-start | bytes 393224 | tf_op jit(solution)/shard_map/ppermute | solution.py:246
  39.7 9.6 %collective-permute-start.13 = (f32[8,16,128]{2,1,0:T(8,128)S(1)}, f32[8,16,128]{2,1,0:T(8,128)S(1)}, u32[]{:S(2)}, u32[]{:S(2)}) collective-permute-start(f32[8,16,128]{2,1,0:T(8,128)S(1)} %get-tuple-element.62), channel_id=1, source_target_pairs={{0,2},{2,0},{1,3},{3,1},{4,6},{6,4},{5,7},{7,5},{8,10},{10,8},{9,1... | collective-permute-start | bytes 196616 | tf_op jit(solution)/shard_map/ppermute | solution.py:246
  41.3 18.2 %collective-permute-start.6 = (f32[16,32,128]{2,1,0:T(8,128)S(1)}, f32[16,32,128]{2,1,0:T(8,128)S(1)}, u32[]{:S(2)}, u32[]{:S(2)}) collective-permute-start(f32[16,32,128]{2,1,0:T(8,128)S(1)} %get-tuple-element.52), channel_id=1, source_target_pairs={{16,32},{32,16},{48,64},{64,48},{80,96},{96,80},{112,128},{128,112... | collective-permute-start | bytes 786440 | tf_op jit(solution)/shard_map/ppermute | solution.py:246
  42.0 11.1 %collective-permute-start.8 = (f32[8,32,128]{2,1,0:T(8,128)S(1)}, f32[8,32,128]{2,1,0:T(8,128)S(1)}, u32[]{:S(2)}, u32[]{:S(2)}) collective-permute-start(f32[8,32,128]{2,1,0:T(8,128)S(1)} %get-tuple-element.54), channel_id=1, source_target_pairs={{4,8},{8,4},{5,9},{9,5},{6,10},{10,6},{7,11},{11,7},{20,24},{24,20... | collective-permute-start | bytes 393224 | tf_op jit(solution)/shard_map/ppermute | solution.py:246
  49.4 16.7 %collective-permute-start.18 = (f32[16,32,128]{2,1,0:T(8,128)S(1)}, f32[16,32,128]{2,1,0:T(8,128)S(1)}, u32[]{:S(2)}, u32[]{:S(2)}) collective-permute-start(f32[16,32,128]{2,1,0:T(8,128)S(1)} %get-tuple-element.69), channel_id=1, source_target_pairs={{0,16},{16,0},{32,48},{48,32},{64,80},{80,64},{96,112},{112,96},{1... | collective-permute-start | bytes 786440 | tf_op jit(solution)/shard_map/ppermute | solution.py:246
  52.4 13.7 %collective-permute-start.19 = (f32[16,32,128]{2,1,0:T(8,128)S(1)}, f32[16,32,128]{2,1,0:T(8,128)S(1)}, u32[]{:S(2)}, u32[]{:S(2)}) collective-permute-start(f32[16,32,128]{2,1,0:T(8,128)S(1)} %get-tuple-element.70), channel_id=1, source_target_pairs={{16,32},{32,16},{48,64},{64,48},{80,96},{96,80},{112,128},{128,112... | collective-permute-start | bytes 786440 | tf_op jit(solution)/shard_map/ppermute | solution.py:246
  53.0 11.0 %collective-permute-start.20 = (f32[8,32,128]{2,1,0:T(8,128)S(1)}, f32[8,32,128]{2,1,0:T(8,128)S(1)}, u32[]{:S(2)}, u32[]{:S(2)}) collective-permute-start(f32[8,32,128]{2,1,0:T(8,128)S(1)} %get-tuple-element.71), channel_id=1, source_target_pairs={{0,4},{4,0},{8,12},{12,8},{1,5},{5,1},{9,13},{13,9},{2,6},{6,2},{1... | collective-permute-start | bytes 393224 | tf_op jit(solution)/shard_map/ppermute | solution.py:246
  53.2 12.9 %collective-permute-start.21 = (f32[8,32,128]{2,1,0:T(8,128)S(1)}, f32[8,32,128]{2,1,0:T(8,128)S(1)}, u32[]{:S(2)}, u32[]{:S(2)}) collective-permute-start(f32[8,32,128]{2,1,0:T(8,128)S(1)} %get-tuple-element.72), channel_id=1, source_target_pairs={{4,8},{8,4},{5,9},{9,5},{6,10},{10,6},{7,11},{11,7},{20,24},{24,20... | collective-permute-start | bytes 393224 | tf_op jit(solution)/shard_map/ppermute | solution.py:246
  61.3 26.5 %collective-permute-start.14 = (f32[16,32,128]{2,1,0:T(8,128)S(1)}, f32[16,32,128]{2,1,0:T(8,128)S(1)}, u32[]{:S(2)}, u32[]{:S(2)}) collective-permute-start(f32[16,32,128]{2,1,0:T(8,128)S(1)} %get-tuple-element.64), channel_id=1, source_target_pairs={{0,16},{16,0},{32,48},{48,32},{64,80},{80,64},{96,112},{112,96},{1... | collective-permute-start | bytes 786440 | tf_op jit(solution)/shard_map/ppermute | solution.py:246
  64.0 23.0 %collective-permute-start.16 = (f32[8,32,128]{2,1,0:T(8,128)S(1)}, f32[8,32,128]{2,1,0:T(8,128)S(1)}, u32[]{:S(2)}, u32[]{:S(2)}) collective-permute-start(f32[8,32,128]{2,1,0:T(8,128)S(1)} %get-tuple-element.66), channel_id=1, source_target_pairs={{0,4},{4,0},{8,12},{12,8},{1,5},{5,1},{9,13},{13,9},{2,6},{6,2},{1... | collective-permute-start | bytes 393224 | tf_op jit(solution)/shard_map/ppermute | solution.py:246
  67.9 12.5 %collective-permute-start.22 = (f32[8,16,128]{2,1,0:T(8,128)S(1)}, f32[8,16,128]{2,1,0:T(8,128)S(1)}, u32[]{:S(2)}, u32[]{:S(2)}) collective-permute-start(f32[8,16,128]{2,1,0:T(8,128)S(1)} %get-tuple-element.74), channel_id=1, source_target_pairs={{0,2},{2,0},{1,3},{3,1},{4,6},{6,4},{5,7},{7,5},{8,10},{10,8},{9,1... | collective-permute-start | bytes 196616 | tf_op jit(solution)/shard_map/ppermute | solution.py:246
  72.1 15.6 %collective-permute-start.17 = (f32[8,32,128]{2,1,0:T(8,128)S(1)}, f32[8,32,128]{2,1,0:T(8,128)S(1)}, u32[]{:S(2)}, u32[]{:S(2)}) collective-permute-start(f32[8,32,128]{2,1,0:T(8,128)S(1)} %get-tuple-element.67), channel_id=1, source_target_pairs={{4,8},{8,4},{5,9},{9,5},{6,10},{10,6},{7,11},{11,7},{20,24},{24,20... | collective-permute-start | bytes 393224 | tf_op jit(solution)/shard_map/ppermute | solution.py:246
  79.8 12.1 %collective-permute-start.15 = (f32[16,32,128]{2,1,0:T(8,128)S(1)}, f32[16,32,128]{2,1,0:T(8,128)S(1)}, u32[]{:S(2)}, u32[]{:S(2)}) collective-permute-start(f32[16,32,128]{2,1,0:T(8,128)S(1)} %get-tuple-element.65), channel_id=1, source_target_pairs={{16,32},{32,16},{48,64},{64,48},{80,96},{96,80},{112,128},{128,112... | collective-permute-start | bytes 786440 | tf_op jit(solution)/shard_map/ppermute | solution.py:246
  80.5 17.7 %collective-permute-start.23 = (f32[16,32,128]{2,1,0:T(8,128)S(1)}, f32[16,32,128]{2,1,0:T(8,128)S(1)}, u32[]{:S(2)}, u32[]{:S(2)}) collective-permute-start(f32[16,32,128]{2,1,0:T(8,128)S(1)} %get-tuple-element.77), channel_id=1, source_target_pairs={{0,16},{16,0},{32,48},{48,32},{64,80},{80,64},{96,112},{112,96},{1... | collective-permute-start | bytes 786440 | tf_op jit(solution)/shard_map/ppermute | solution.py:246
  87.0 11.2 %collective-permute-start.24 = (f32[16,32,128]{2,1,0:T(8,128)S(1)}, f32[16,32,128]{2,1,0:T(8,128)S(1)}, u32[]{:S(2)}, u32[]{:S(2)}) collective-permute-start(f32[16,32,128]{2,1,0:T(8,128)S(1)} %get-tuple-element.78), channel_id=1, source_target_pairs={{16,32},{32,16},{48,64},{64,48},{80,96},{96,80},{112,128},{128,112... | collective-permute-start | bytes 786440 | tf_op jit(solution)/shard_map/ppermute | solution.py:246
  87.7 6.6 %collective-permute-start.25 = (f32[8,32,128]{2,1,0:T(8,128)S(1)}, f32[8,32,128]{2,1,0:T(8,128)S(1)}, u32[]{:S(2)}, u32[]{:S(2)}) collective-permute-start(f32[8,32,128]{2,1,0:T(8,128)S(1)} %get-tuple-element.79), channel_id=1, source_target_pairs={{0,4},{4,0},{8,12},{12,8},{1,5},{5,1},{9,13},{13,9},{2,6},{6,2},{1... | collective-permute-start | bytes 393224 | tf_op jit(solution)/shard_map/ppermute | solution.py:246
  87.8 10.4 %collective-permute-start.26 = (f32[8,32,128]{2,1,0:T(8,128)S(1)}, f32[8,32,128]{2,1,0:T(8,128)S(1)}, u32[]{:S(2)}, u32[]{:S(2)}) collective-permute-start(f32[8,32,128]{2,1,0:T(8,128)S(1)} %get-tuple-element.80), channel_id=1, source_target_pairs={{4,8},{8,4},{5,9},{9,5},{6,10},{10,6},{7,11},{11,7},{20,24},{24,20... | collective-permute-start | bytes 393224 | tf_op jit(solution)/shard_map/ppermute | solution.py:246

commit v4 on v3

--- a/solution.py
+++ b/solution.py
@@ -15,7 +15,12 @@
 SMEM = pl.BlockSpec(memory_space=pltpu.MemorySpace.SMEM)
 
 
+def near(args):
+    return [pltpu.with_memory_space_constraint(a, pltpu.MemorySpace.VMEM) if a.size > 8 else a for a in args]
+
+
 def call(body, outs, args, scratch=(), limit=16, **more):
+    args = near(args)
     return pl.pallas_call(
         body,
         out_shape=[jax.ShapeDtypeStruct(s, jnp.float32) for s in outs],
@@ -33,11 +38,16 @@
     return pltpu.roll(v, HALF, v.ndim - 1)
 
 
+def exchange_halves(a, b):
+    m = left()
+    moved = swap(jnp.where(m, b, a))
+    return jnp.where(m, a, moved), jnp.where(m, moved, b)
+
+
 def pack_tiles(ref, j, i, t, nk):
     a = ref[j, i, pl.ds(t * TILE, TILE), :]
     b = ref[j, i, pl.ds(nk // 2 + t * TILE, TILE), :]
-    m = left()
-    return jnp.where(m, a, swap(b)), jnp.where(m, swap(a), b)
+    return exchange_halves(a, b)
 
 
 def edge_rows(place, block, j):
@@ -97,16 +107,19 @@
     lax.fori_loop(0, ni, at, 0)
 
 
-def step_body(last, h, place, f, c, r0, r1, c0, c1, ks, *rest):
+def step_body(kind, h, place, f, c, r0, r1, c0, c1, ks, *rest):
     rest = list(rest)
-    earlier = rest.pop(0) if h else None
-    with_total = last and h == 1
+    last, with_sums = kind == "last", kind == "sums"
+    earlier = rest.pop(0) if h and not last else None
     out = rest.pop(0)
     if last:
-        total = rest.pop(0)
+        fix = rest.pop(0)
     else:
         s_r0, s_r1, s_c0, s_c1, s_k = rest[:5]
         rest = rest[5:]
+        if with_sums:
+            g_sum, f_sum = rest[:2]
+            rest = rest[2:]
     kl, kh = rest
     nj, ni, nk = f.shape[:3]
     tiles = nk // TILE
@@ -127,36 +140,43 @@
     def at(i, below, above):
         down = [jnp.where(even_r, r1[i, ds(t), :], r0[i, ds(t), :]) for t in range(tiles)]
         mid = [f[0, i, ds(t), :] for t in range(tiles)]
-        sums, first = [None] * tiles, [None] * tiles
+        first, grown, total = [None] * tiles, [None] * tiles, [None] * tiles
+        if last:
+            for t in range(tiles):
+                fix[i, ds(t), :] = jnp.where(place[3] == 0, 0.1 * (mid[t] - down[t]), 0.0)
         for j in range(nj):
             if j + 1 < nj:
                 up = [f[j + 1, i, ds(t), :] for t in range(tiles)]
             else:
                 up = [jnp.where(even_r, r0[i, ds(t), :], r1[i, ds(t), :]) for t in range(tiles)]
-            fwd = [pltpu.roll(v, 1, 0) for v in mid]
-            bwd = [pltpu.roll(v, TILE - 1, 0) for v in mid]
             low = jnp.broadcast_to(kl[j, pl.ds(i, 1), :], (TILE, 128))
             high = jnp.broadcast_to(kh[j, pl.ds(i, 1), :], (TILE, 128))
             for t in range(tiles):
-                before = jnp.where(top, fwd[t - 1] if t else low, fwd[t])
-                after = jnp.where(bottom, bwd[t + 1] if t + 1 < tiles else high, bwd[t])
+                if t:
+                    before = f[j, i, pl.ds(t * TILE - 1, TILE), :]
+                else:
+                    before = jnp.where(top, low, pltpu.roll(mid[t], 1, 0))
+                if t + 1 < tiles:
+                    after = f[j, i, pl.ds(t * TILE + 1, TILE), :]
+                else:
+                    after = jnp.where(bottom, high, pltpu.roll(mid[t], TILE - 1, 0))
                 around = (down[t] + up[t]) + (below(j, t) + above(j, t)) + (before + after)
                 v = mid[t] * (0.6 - c[j, i, ds(t), :] * mid[t]) + 0.1 * around
                 out[j, i, ds(t), :] = v
-                if last:
-                    sums[t] = v if j == 0 else sums[t] + v
-                elif j == 0:
+                if j == 0:
                     first[t] = v
-                elif j == nj - 1:
+                elif j == nj - 1 and not last:
                     s_r0[i, ds(t), :] = jnp.where(even_r, v, first[t])
                     s_r1[i, ds(t), :] = jnp.where(even_r, first[t], v)
+                if with_sums:
+                    own = v * (0.6 - c[j, i, ds(t), :] * v)
+                    grown[t] = own if j == 0 else grown[t] + own
+                    total[t] = v if j == 0 else total[t] + v
             down, mid = mid, up
-        if last:
-            base = nk if with_total else 0
+        if with_sums:
             for t in range(tiles):
-                total[i, pl.ds(base + t * TILE, TILE), :] = sums[t]
-                if with_total:
-                    total[i, ds(t), :] = earlier[i, ds(t), :]
+                g_sum[i, ds(t), :] = grown[t] - jnp.where(place[3] == 1, 0.1 * first[t], 0.0)
+                f_sum[i, ds(t), :] = total[t]
 
     def inner(i, _):
         at(i, lambda j, t: f[j, i - 1, ds(t), :], lambda j, t: f[j, i + 1, ds(t), :])
@@ -167,6 +187,48 @@
     at(ni - 1, lambda j, t: f[j, ni - 2, ds(t), :], lambda j, t: jnp.where(even_c, c0[j, ds(t), :], c1[j, ds(t), :]))
     if not last:
         write_faces(place, out, s_c0, s_c1, s_k, earlier)
+
+
+def totals_body(place, g_a, s_a, g_b, s_b, c0_a, c1_a, c0_b, c1_b, ks, out, kl, kh):
+    ni, nk = g_a.shape[:2]
+    nj = ks.shape[0]
+    tiles = nk // TILE
+    wide = left((ni, 128))
+    row = lax.broadcasted_iota(jnp.int32, (TILE, 128), 0)
+    top, bottom = row == 0, row == TILE - 1
+    even_c = place[1] == 0
+    across = ks[0]
+    for j in range(1, nj):
+        across = across + ks[j]
+    for h, (g, s, c0, c1) in enumerate(((g_a, s_a, c0_a, c1_a), (g_b, s_b, c0_b, c1_b))):
+        x = across if h else swap(across)
+        kl[h] = jnp.where(wide, jnp.where(place[2] == 1, x, 0.0), swap(s[:, nk - 1, :]))
+        kh[h] = jnp.where(wide, swap(s[:, 0, :]), jnp.where(place[2] == 0, x, 0.0))
+        ends = []
+        for t in range(tiles):
+            part = pl.ds(t * TILE, TILE)
+            sum0, sum1 = c0[0, part, :], c1[0, part, :]
+            for j in range(1, nj):
+                sum0, sum1 = sum0 + c0[j, part, :], sum1 + c1[j, part, :]
+            ends.append((jnp.where(even_c, sum1, sum0), jnp.where(even_c, sum0, sum1)))
+        for i in range(ni):
+            low = jnp.broadcast_to(kl[h, pl.ds(i, 1), :], (TILE, 128))
+            high = jnp.broadcast_to(kh[h, pl.ds(i, 1), :], (TILE, 128))
+            for t in range(tiles):
+                part = pl.ds(t * TILE, TILE)
+                mid = s[i, part, :]
+                below = s[i - 1, part, :] if i else ends[t][0]
+                above = s[i + 1, part, :] if i + 1 < ni else ends[t][1]
+                if t:
+                    before = s[i, pl.ds(t * TILE - 1, TILE), :]
+                else:
+                    before = jnp.where(top, low, pltpu.roll(mid, 1, 0))
+                if t + 1 < tiles:
+                    after = s[i, pl.ds(t * TILE + 1, TILE), :]
+                else:
+                    after = jnp.where(bottom, high, pltpu.roll(mid, TILE - 1, 0))
+                around = (mid + mid) + (below + above) + (before + after)
+                out[i, pl.ds(h * nk + t * TILE, TILE), :] = g[i, part, :] + 0.1 * around
 
 
 def prefix_body(g, out):
@@ -181,12 +243,8 @@
 GROUP = 2
 
 
-def finish_body(scale, fa, fb, base, potential, field, pot, end, sems):
+def finish_body(scale, fa, fb, base, fix_a, fix_b, potential, field, pot, end, sems):
     nj, ni, nk = fa.shape[:3]
-    m = left()
-
-    def both(a, b):
-        return jnp.where(m, a, swap(b)), jnp.where(m, swap(a), b)
 
     def copies(g):
         part = pl.ds(g * GROUP, GROUP)
@@ -200,9 +258,9 @@
             i = g * GROUP + n
             for t in range(nk // TILE):
                 lo, hi = pl.ds(t * TILE, TILE), pl.ds(nk + t * TILE, TILE)
-                acc0, acc1 = both(base[i, lo, :], base[i, hi, :])
+                acc0, acc1 = exchange_halves(base[i, lo, :] + fix_a[i, lo, :], base[i, hi, :] + fix_b[i, lo, :])
                 for j in range(nj):
-                    v0, v1 = both(fa[j, i, lo, :], fb[j, i, lo, :])
+                    v0, v1 = exchange_halves(fa[j, i, lo, :], fb[j, i, lo, :])
                     end[j, i, lo, :] = v0
                     end[j, i, hi, :] = v1
                     acc0, acc1 = acc0 + v0, acc1 + v1
@@ -229,9 +287,14 @@
 
 
 KINDS = (("r1", "c1", "c0", "r0"), ("k", "r1", "c1", "c0", "r0"))
-
-
-def exchange(faces, h):
+LAST = (("r1", "c1", "c0", "r0"), ("c1", "c0", "k", "r1", "r0"))
+
+
+def kinds(step, h):
+    return (LAST if step == STEPS - 1 else KINDS)[h]
+
+
+def exchange(faces, step, h):
     r0, r1, c0, c1, k = faces
     rows, cols, slabs = lax.axis_size("rows"), lax.axis_size("cols"), lax.axis_size("slabs")
     sends = {
@@ -242,7 +305,7 @@
         "r1": (r1, "rows", pairs(rows, 1)),
     }
     got = {}
-    for kind in KINDS[h]:
+    for kind in kinds(step, h):
         got[kind] = lax.ppermute(*sends[kind])
     return [got[kind] for kind in ("r0", "r1", "c0", "c1")], got.get("k")
 
@@ -251,7 +314,8 @@
     nj, ni, nk, nl = field_values.shape
     half = (nj, ni, nk // 2, nl)
     faces = [(ni, nk // 2, nl)] * 2 + [(nj, nk // 2, nl)] * 2 + [(nj, ni, nl)]
-    place = jnp.stack([lax.axis_index("rows") % 2, lax.axis_index("cols") % 2, lax.axis_index("slabs")])
+    row = lax.axis_index("rows")
+    place = jnp.stack([row % 2, lax.axis_index("cols") % 2, lax.axis_index("slabs"), row == 0])
     place = place.astype(jnp.int32)
     out = call(
         pack_field, [half, half] + faces + faces, (place, field_values), in_specs=[SMEM, VMEM]
@@ -259,44 +323,57 @@
     f, sent = [out[0], out[1]], [out[2:7], out[7:12]]
     halos = [None, None]
     for h in range(2):
-        halos[h], across = exchange(sent[h], h)
+        halos[h], across = exchange(sent[h], 0, h)
     c = call(pack_crowding, [half, half], (crowding,))
     scratch = [(nj, ni, nl)] * 2
-    extra = None
+    sums, fix, other = [None, None], [None, None], None
+    rows = lax.axis_size("rows")
     for step in range(STEPS):
-        last = step == STEPS - 1
+        kind = {STEPS - 1: "last", STEPS - 2: "sums"}.get(step, "plain")
+        last = kind == "last"
+        if last:
+            total = call(
+                totals_body,
+                [(ni, nk, nl)],
+                (place, *sums[0], *sums[1], *halos[0][2:], *halos[1][2:], across),
+                [(2, ni, nl)] * 2,
+                in_specs=[SMEM] + [VMEM] * 9,
+            )[0]
+            total = total.reshape(rows, ni * nk // rows, nl)
+            gathered = lax.all_to_all(total, "rows", 0, 0, tiled=True)
+            gathered, place = lax.optimization_barrier((gathered, place))
+            before = call(prefix_body, [gathered.shape], (gathered,))[0]
         for h in range(2):
-            args = (place, f[h], c[h], *halos[h], across) + ((extra,) if h else ())
-            if last:
-                outs = [half, (ni, nk if h else nk // 2, nl)]
-            else:
-                outs = [half] + faces
+            args = (place, f[h], c[h], *halos[h], across) + ((other,) if h and not last else ())
+            plane = (ni, nk // 2, nl)
+            outs = [half] + {"last": [plane], "sums": faces + [plane] * 2, "plain": faces}[kind]
             res = call(
-                functools.partial(step_body, last, h),
+                functools.partial(step_body, kind, h),
                 outs,
                 args,
                 scratch,
                 in_specs=[SMEM] + [VMEM] * (len(args) - 1),
             )
             f[h] = res[0]
-            extra = res[-1]
-            if not last:
-                halos[h], got = exchange(res[1:], h)
+            if last:
+                fix[h] = res[1]
+            else:
+                sums[h] = res[6:]
+                other = res[5]
+                halos[h], got = exchange(res[1:6], step + 1, h)
         if not last:
             across = got
-    rows = lax.axis_size("rows")
-    gathered = lax.all_to_all(extra.reshape(rows, ni * nk // rows, nl), "rows", 0, 0, tiled=True)
-    before = call(prefix_body, [gathered.shape], (gathered,))[0]
+    before, *f = lax.optimization_barrier((before, *f))
     base = lax.all_to_all(before, "rows", 0, 0, tiled=True).reshape(ni, nk, nl)
     potential, field = pl.pallas_call(
         functools.partial(finish_body, 1.0 / (nj * rows)),
         out_shape=[jax.ShapeDtypeStruct(field_values.shape, jnp.float32)] * 2,
-        in_specs=[VMEM] * 3,
+        in_specs=[VMEM] * 5,
         out_specs=[pl.BlockSpec(memory_space=pltpu.MemorySpace.HBM)] * 2,
         scratch_shapes=[pltpu.VMEM(field_values.shape, jnp.float32)] * 2
         + [pltpu.SemaphoreType.DMA((ni // GROUP, 2))],
         compiler_params=pltpu.CompilerParams(vmem_limit_bytes=16 * 1024 * 1024),
-    )(f[0], f[1], base)
+    )(*near([f[0], f[1], base, *fix]))
     return potential, field
 
 

time: 139 us -> 143 us (1.029)
  the two profiles are of different devices: /device:TPU:36 before, /device:TPU:4 now
where the time goes in v4:
time: 143 us; the launch traced here: 142 us
  starting transfers between devices  60.6 us (42%)
  waiting for transfers between devices  31 us (22%)
  Pallas kernels  22.3 us (16%)
  blocking collectives  19.1 us (13%)
  local copies, waits for them, and re-layouts  8.12 us (6%)
    ppermute x27, starting transfers between devices, exchange(): got[kind] = lax.ppermute(*sends[kind])  50.6 us
    ppermute x27, waiting for transfers between devices, exchange(): got[kind] = lax.ppermute(*sends[kind])  25.7 us
    all_to_all x1, blocking collectives, on_device(): base = lax.all_to_all(before, 'rows', 0, 0, tiled=True).reshape(ni, nk, nl)  19.1 us
    pallas_call x10, Pallas kernels, call(): pl.pallas_call(body, out_shape=[jax.ShapeDtypeStruct(s, jnp.float32) for...  18.7 us
    all_to_all x1, starting transfers between devices, on_device(): gathered = lax.all_to_all(total, 'rows', 0, 0, tiled=True)  10 us
    unnamed x20, local copies, waits for them, and re-layouts  8.12 us
    all_to_all x1, waiting for transfers between devices, on_device(): gathered = lax.all_to_all(total, 'rows', 0, 0, tiled=True)  5.31 us
    pallas_call x1, Pallas kernels, on_device(): pl.pallas_call(functools.partial(finish_body, 1.0 / (nj * rows)), out_sha...  3.58 us
  transfers between devices with their start and end apart: 28, of which 9 were waited for; matrix products, arithmetic and copies ran while one was open for 0% of the time, Pallas kernels for 9%

profile of v4, /device:TPU:4, one launch (start us, length us, event | category | flops | bytes accessed | tf_op | source)
XLA Modules:
  0.0 142.2 jit_solution(11690955416894151722)
XLA Ops:
  0.6 0.1 pad_add_fusion.place
  0.7 2.2 %copy-done.2 = f32[8,16,64,128]{3,2,1,0:T(8,128)S(1)} copy-done((f32[8,16,64,128]{3,2,1,0:T(8,128)S(1)}, f32[8,16,64,128]{3,2,1,0:T(8,128)}, u32[]{:S(2)}) %copy-start.2) | copy-done | bytes 4194328
  2.9 3.0 %shard_map.41 = (f32[8,16,32,128]{3,2,1,0:T(8,128)S(1)}, f32[8,16,32,128]{3,2,1,0:T(8,128)S(1)}, f32[16,32,128]{2,1,0:T(8,128)S(1)}, f32[16,32,128]{2,1,0:T(8,12...) custom-call(s32[4]{0:T(128)S(1)} %pad_add_fusion.place, ...), custom_call_target="tpu_custom_call" | custom-call | tf_op jit(solution)/shard_map/pallas_call | solution.py:24
  5.9 2.2 %collective-permute-start.2 = (f32[8,32,128]{2,1,0:T(8,128)S(1)}, f32[8,32,128]{2,1,0:T(8,128)S(1)}, u32[]{:S(2)}, u32[]{:S(2)}) collective-permute-start(f32[8,32,128]{2,1,0:T(8,128)S(1)} %get-tuple-element.56), channel_id=1, source_target_pairs={{0,4},{4,0},{8,12},{12,8},{1,5},{5,1},{9,13},{13,9},{2,6},{6,2},{1... | collective-permute-start | bytes 393224 | tf_op jit(solution)/shard_map/ppermute | solution.py:309
  8.2 5.5 %collective-permute-start.4 = (f32[8,16,128]{2,1,0:T(8,128)S(1)}, f32[8,16,128]{2,1,0:T(8,128)S(1)}, u32[]{:S(2)}, u32[]{:S(2)}) collective-permute-start(f32[8,16,128]{2,1,0:T(8,128)S(1)} %get-tuple-element.58), channel_id=1, source_target_pairs={{0,2},{2,0},{1,3},{3,1},{4,6},{6,4},{5,7},{7,5},{8,10},{10,8},{9,1... | collective-permute-start | bytes 196616 | tf_op jit(solution)/shard_map/ppermute | solution.py:309
  13.6 0.7 collective-permute-start.1
  14.3 5.8 %collective-permute-start.3 = (f32[8,32,128]{2,1,0:T(8,128)S(1)}, f32[8,32,128]{2,1,0:T(8,128)S(1)}, u32[]{:S(2)}, u32[]{:S(2)}) collective-permute-start(f32[8,32,128]{2,1,0:T(8,128)S(1)} %get-tuple-element.57), channel_id=1, source_target_pairs={{4,8},{8,4},{5,9},{9,5},{6,10},{10,6},{7,11},{11,7},{20,24},{24,20... | collective-permute-start | bytes 393224 | tf_op jit(solution)/shard_map/ppermute | solution.py:309
  20.2 0.0 collective-permute-done.4.ks
  20.2 1.7 %collective-permute-start.9 = (f32[16,32,128]{2,1,0:T(8,128)S(1)}, f32[16,32,128]{2,1,0:T(8,128)S(1)}, u32[]{:S(2)}, u32[]{:S(2)}) collective-permute-start(f32[16,32,128]{2,1,0:T(8,128)S(1)} %get-tuple-element.66), channel_id=1, source_target_pairs={{0,16},{16,0},{32,48},{48,32},{64,80},{80,64},{96,112},{112,96},{1... | collective-permute-start | bytes 786440 | tf_op jit(solution)/shard_map/ppermute | solution.py:309
  21.9 0.0 collective-permute-done.2.c0
  21.9 0.7 collective-permute-start.10
  22.6 5.1 %collective-permute-done.3.c1 = f32[8,32,128]{2,1,0:T(8,128)S(1)} collective-permute-done((f32[8,32,128]{2,1,0:T(8,128)S(1)}, f32[8,32,128]{2,1,0:T(8,128)S(1)}, u32[]{:S(2)}, u32[]{:S(2)}) %collective-permute-start.3) | collective-permute-done | bytes 131104 | tf_op jit(solution)/shard_map/ppermute | solution.py:309
  27.7 0.0 collective-permute-start.11
  27.7 3.2 %collective-permute-start.12 = (f32[8,32,128]{2,1,0:T(8,128)S(1)}, f32[8,32,128]{2,1,0:T(8,128)S(1)}, u32[]{:S(2)}, u32[]{:S(2)}) collective-permute-start(f32[8,32,128]{2,1,0:T(8,128)S(1)} %get-tuple-element.69), channel_id=1, source_target_pairs={{4,8},{8,4},{5,9},{9,5},{6,10},{10,6},{7,11},{11,7},{20,24},{24,20... | collective-permute-start | bytes 393224 | tf_op jit(solution)/shard_map/ppermute | solution.py:309
  31.0 1.7 %shard_map.42 = (f32[8,16,32,128]{3,2,1,0:T(8,128)S(1)}, f32[8,16,32,128]{3,2,1,0:T(8,128)S(1)}) custom-call(f32[8,16,64,128]{3,2,1,0:T(8,128)S(1)} %copy-done.3), custom_call_target="tpu_custom_call" | custom-call | tf_op jit(solution)/shard_map/pallas_call | solution.py:24
  32.7 0.0 copy-start
  32.7 1.6 %shard_map.43 = (f32[8,16,32,128]{3,2,1,0:T(8,128)S(1)}, f32[16,32,128]{2,1,0:T(8,128)S(1)}, f32[16,32,128]{2,1,0:T(8,128)S(1)}, f32[8,32,128]{2,1,0:T(8,128)S(1...) custom-call(s32[4]{0:T(128)S(1)} %pad_add_fusion.place, f32[8,16,32,128]{3,2,1,0:T(8,128)S(1)} %get-tuple-element.52.f, ...), custom_call_target="tpu_custom_call" | custom-call | tf_op jit(solution)/shard_map/pallas_call | solution.py:24
  34.3 0.6 collective-permute-start.5
  34.9 0.6 collective-permute-done.11.c0
  35.5 0.5 collective-permute-start.7
  36.0 5.4 %collective-permute-done.12.c1 = f32[8,32,128]{2,1,0:T(8,128)S(1)} collective-permute-done((f32[8,32,128]{2,1,0:T(8,128)S(1)}, f32[8,32,128]{2,1,0:T(8,128)S(1)}, u32[]{:S(2)}, u32[]{:S(2)}) %collective-permute-start.12) | collective-permute-done | bytes 131104 | tf_op jit(solution)/shard_map/ppermute | solution.py:309
  41.4 0.0 collective-permute-done.9.r0
  41.4 0.0 collective-permute-done.10.r1
  41.4 1.7 %shard_map.44 = (f32[8,16,32,128]{3,2,1,0:T(8,128)S(1)}, f32[16,32,128]{2,1,0:T(8,128)S(1)}, f32[16,32,128]{2,1,0:T(8,128)S(1)}, f32[8,32,128]{2,1,0:T(8,128)S(1...) custom-call(s32[4]{0:T(128)S(1)} %pad_add_fusion.place, f32[8,16,32,128]{3,2,1,0:T(8,128)S(1)} %get-tuple-element.64.f, ...), custom_call_target="tpu_custom_call" | custom-call | tf_op jit(solution)/shard_map/pallas_call | solution.py:24
  43.1 1.5 %collective-permute-start.13 = (f32[8,16,128]{2,1,0:T(8,128)S(1)}, f32[8,16,128]{2,1,0:T(8,128)S(1)}, u32[]{:S(2)}, u32[]{:S(2)}) collective-permute-start(f32[8,16,128]{2,1,0:T(8,128)S(1)} %get-tuple-element.71), channel_id=1, source_target_pairs={{0,2},{2,0},{1,3},{3,1},{4,6},{6,4},{5,7},{7,5},{8,10},{10,8},{9,1... | collective-permute-start | bytes 196616 | tf_op jit(solution)/shard_map/ppermute | solution.py:309
  44.6 0.7 collective-permute-start.6
  45.3 1.9 %collective-permute-start.8 = (f32[8,32,128]{2,1,0:T(8,128)S(1)}, f32[8,32,128]{2,1,0:T(8,128)S(1)}, u32[]{:S(2)}, u32[]{:S(2)}) collective-permute-start(f32[8,32,128]{2,1,0:T(8,128)S(1)} %get-tuple-element.63), channel_id=1, source_target_pairs={{4,8},{8,4},{5,9},{9,5},{6,10},{10,6},{7,11},{11,7},{20,24},{24,20... | collective-permute-start | bytes 393224 | tf_op jit(solution)/shard_map/ppermute | solution.py:309
  47.2 4.1 %collective-permute-done.13.ks = f32[8,16,128]{2,1,0:T(8,128)S(1)} collective-permute-done((f32[8,16,128]{2,1,0:T(8,128)S(1)}, f32[8,16,128]{2,1,0:T(8,128)S(1)}, u32[]{:S(2)}, u32[]{:S(2)}) %collective-permute-start.13) | collective-permute-done | bytes 65568 | tf_op jit(solution)/shard_map/ppermute | solution.py:309
  51.3 0.2 collective-permute-start.14
  51.5 0.0 collective-permute-done.7.c0
  51.5 0.7 collective-permute-start.15
  52.2 3.3 %collective-permute-done.8.c1 = f32[8,32,128]{2,1,0:T(8,128)S(1)} collective-permute-done((f32[8,32,128]{2,1,0:T(8,128)S(1)}, f32[8,32,128]{2,1,0:T(8,128)S(1)}, u32[]{:S(2)}, u32[]{:S(2)}) %collective-permute-start.8) | collective-permute-done | bytes 131104 | tf_op jit(solution)/shard_map/ppermute | solution.py:309
  55.5 0.0 collective-permute-start.16
  55.5 0.0 collective-permute-done.5.r0
  55.5 3.8 %collective-permute-start.17 = (f32[8,32,128]{2,1,0:T(8,128)S(1)}, f32[8,32,128]{2,1,0:T(8,128)S(1)}, u32[]{:S(2)}, u32[]{:S(2)}) collective-permute-start(f32[8,32,128]{2,1,0:T(8,128)S(1)} %get-tuple-element.78), channel_id=1, source_target_pairs={{4,8},{8,4},{5,9},{9,5},{6,10},{10,6},{7,11},{11,7},{20,24},{24,20... | collective-permute-start | bytes 393224 | tf_op jit(solution)/shard_map/ppermute | solution.py:309
  59.3 2.8 %shard_map.45 = (f32[8,16,32,128]{3,2,1,0:T(8,128)S(1)}, f32[16,32,128]{2,1,0:T(8,128)}, f32[16,32,128]{2,1,0:T(8,128)}, f32[8,32,128]{2,1,0:T(8,128)S(1)}, f32[...) custom-call(s32[4]{0:T(128)S(1)} %pad_add_fusion.place, ...), custom_call_target="tpu_custom_call" | custom-call | tf_op jit(solution)/shard_map/pallas_call | solution.py:24
  62.1 0.4 collective-permute-start.18
  62.5 5.0 %collective-permute-start.19 = (f32[8,32,128]{2,1,0:T(8,128)S(1)}, f32[8,32,128]{2,1,0:T(8,128)S(1)}, u32[]{:S(2)}, u32[]{:S(2)}) collective-permute-start(f32[8,32,128]{2,1,0:T(8,128)S(1)} %get-tuple-element.83), channel_id=1, source_target_pairs={{4,8},{8,4},{5,9},{9,5},{6,10},{10,6},{7,11},{11,7},{20,24},{24,20... | collective-permute-start | bytes 393224 | tf_op jit(solution)/shard_map/ppermute | solution.py:309
  67.5 0.2 collective-permute-done.17.c1
  67.7 0.0 collective-permute-done.14.r0
  67.7 0.0 collective-permute-done.15.r1
  67.7 2.1 %shard_map.46 = (f32[8,16,32,128]{3,2,1,0:T(8,128)S(1)}, f32[16,32,128]{2,1,0:T(8,128)S(1)}, f32[16,32,128]{2,1,0:T(8,128)S(1)}, f32[8,32,128]{2,1,0:T(8,128)S(1...) custom-call(s32[4]{0:T(128)S(1)} %pad_add_fusion.place, ...), custom_call_target="tpu_custom_call" | custom-call | tf_op jit(solution)/shard_map/pallas_call | solution.py:24
  69.8 1.3 copy-done.6
  71.1 0.7 copy-done.8
  71.8 0.7 copy-done.9
  72.5 4.0 %collective-permute-start.21 = (f32[8,32,128]{2,1,0:T(8,128)S(1)}, f32[8,32,128]{2,1,0:T(8,128)S(1)}, u32[]{:S(2)}, u32[]{:S(2)}) collective-permute-start(f32[8,32,128]{2,1,0:T(8,128)S(1)} %get-tuple-element.85), channel_id=1, source_target_pairs={{4,8},{8,4},{5,9},{9,5},{6,10},{10,6},{7,11},{11,7},{20,24},{24,20... | collective-permute-start | bytes 393224 | tf_op jit(solution)/shard_map/ppermute | solution.py:309
  76.5 6.0 %collective-permute-start.22 = (f32[8,16,128]{2,1,0:T(8,128)S(1)}, f32[8,16,128]{2,1,0:T(8,128)S(1)}, u32[]{:S(2)}, u32[]{:S(2)}) collective-permute-start(f32[8,16,128]{2,1,0:T(8,128)S(1)} %get-tuple-element.86), channel_id=1, source_target_pairs={{0,2},{2,0},{1,3},{3,1},{4,6},{6,4},{5,7},{7,5},{8,10},{10,8},{9,1... | collective-permute-start | bytes 196616 | tf_op jit(solution)/shard_map/ppermute | solution.py:309
  82.5 6.7 %collective-permute-done.22.ks = f32[8,16,128]{2,1,0:T(8,128)S(1)} collective-permute-done((f32[8,16,128]{2,1,0:T(8,128)S(1)}, f32[8,16,128]{2,1,0:T(8,128)S(1)}, u32[]{:S(2)}, u32[]{:S(2)}) %collective-permute-start.22) | collective-permute-done | bytes 65568 | tf_op jit(solution)/shard_map/ppermute | solution.py:309
  89.3 0.0 collective-permute-done.18.c0_a.c0
  89.3 0.2 collective-permute-done.21.c1_b.c1
  89.5 1.6 %shard_map.47 = f32[16,64,128]{2,1,0:T(8,128)} custom-call(s32[4]{0:T(128)S(1)} %pad_add_fusion.place, f32[16,32,128]{2,1,0:T(8,128)S(1)} %get-tuple-element.72.g_a, f32[16,32,128]{2,1,0:T(8,128)S(1)} %get-tuple-element.73.s_a, f32[16,32,128]{2,1,0:T(8,128)S(1)} %get-tuple-element.80.g_b, f32[16,32,128]{2,1,0:T(8,128)S(1)} %get-tuple-element.81.s_b, ...), custom_call_target="tpu_custom_call" | custom-call | tf_op jit(solution)/shard_map/pallas_call | solution.py:24
  91.1 10.0 %all-to-all-start = ((f32[16,64,128]{2,1,0:T(8,128)}), f32[16,64,128]{2,1,0:T(8,128)S(1)}, u32[]{:S(2)}, u32[]{:S(2)}) async-start(f32[16,64,128]{2,1,0:T(8,128)} %shard_map.47), calls=%async_computation | async-start | bytes 1048576 | tf_op jit(solution)/shard_map/all_to_all | solution.py:343
  101.1 0.4 collective-permute-start.23
  101.5 1.4 collective-permute-start.24
  102.9 2.4 %collective-permute-start.25 = (f32[16,32,128]{2,1,0:T(8,128)}, f32[16,32,128]{2,1,0:T(8,128)S(1)}, u32[]{:S(2)}, u32[]{:S(2)}) collective-permute-start(f32[16,32,128]{2,1,0:T(8,128)} %copy-done.9), channel_id=1, source_target_pairs={{0,16},{16,0},{32,48},{48,32},{64,80},{80,64},{96,112},{112,96},{1... | collective-permute-start | bytes 786440 | tf_op jit(solution)/shard_map/ppermute | solution.py:309
  105.3 1.4 collective-permute-start.26
  106.6 5.3 %all-to-all-done.g = f32[16,64,128]{2,1,0:T(8,128)S(1)} async-done(((f32[16,64,128]{2,1,0:T(8,128)}), f32[16,64,128]{2,1,0:T(8,128)S(1)}, u32[]{:S(2)}, u32[]{:S(2)}) %all-to-all-start) | async-done | bytes 524320 | tf_op jit(solution)/shard_map/all_to_all | solution.py:343
  112.0 0.0 copy-start.1
  112.0 1.6 %copy-done.1 = f32[8,16,32,128]{3,2,1,0:T(8,128)S(1)} copy-done((f32[8,16,32,128]{3,2,1,0:T(8,128)S(1)}, f32[8,16,32,128]{3,2,1,0:T(8,128)}, u32[]{:S(2)}) %copy-start.1) | copy-done | bytes 2097176
  113.6 1.6 %copy-done.5 = f32[8,16,32,128]{3,2,1,0:T(8,128)S(1)} copy-done((f32[8,16,32,128]{3,2,1,0:T(8,128)S(1)}, f32[8,16,32,128]{3,2,1,0:T(8,128)}, u32[]{:S(2)}) %copy-start.5) | copy-done | bytes 2097176
  115.2 2.2 %shard_map.49 = (f32[8,16,32,128]{3,2,1,0:T(8,128)S(1)}, f32[16,32,128]{2,1,0:T(8,128)S(1)}) custom-call(s32[4]{0:T(128)S(1)} %pad_add_fusion.place, f32[8,16,32,128]{3,2,1,0:T(8,128)S(1)} %copy-done.5, f32[8,16,32,128]{3,2,1,0:T(8,128)S(1)} %copy-done.1, f32[16,32,128]{2,1,0:T(8,128)} %collective-permute-done.23.r0, ...), custom_call_target="tpu_custom_call" | custom-call | tf_op jit(solution)/shard_map/pallas_call | solution.py:24
  117.5 2.0 %shard_map.50 = (f32[8,16,32,128]{3,2,1,0:T(8,128)S(1)}, f32[16,32,128]{2,1,0:T(8,128)S(1)}) custom-call(s32[4]{0:T(128)S(1)} %pad_add_fusion.place, f32[8,16,32,128]{3,2,1,0:T(8,128)S(1)} %copy-done.7, f32[8,16,32,128]{3,2,1,0:T(8,128)S(1)} %get-tuple-element.65.c, f32[16,32,128]{2,1,0:T(8,128)S(1)} %collective-permute-done.25.r0, ...), custom_call_target="tpu_custom_call" | custom-call | tf_op jit(solution)/shard_map/pallas_call | solution.py:24
  119.5 19.1 %all_to_all.10.base = f32[16,64,128]{2,1,0:T(8,128)S(1)} all-to-all(f32[16,64,128]{2,1,0:T(8,128)S(1)} %shard_map.48), channel_id=1, replica_groups=mesh['rows'=16,'cols'=4,'slabs'=2,'trial'=2] {'rows'}, dimensions={0} | all-to-all | bytes 1048576 | tf_op jit(solution)/shard_map/all_to_all | solution.py:367
  138.6 3.6 %shard_map.51 = (f32[8,16,64,128]{3,2,1,0:T(8,128)}, f32[8,16,64,128]{3,2,1,0:T(8,128)}) custom-call(f32[8,16,32,128]{3,2,1,0:T(8,128)S(1)} %get-tuple-element.97.fa, f32[8,16,32,128]{3,2,1,0:T(8,128)S(1)} %get-tuple-element.98.fb, f32[16,64,128]{2,1,0:T(8,128)S(1)} %all_to_all.10.base, f32[16,32,128]{2,1,0:T(8,128)S(1)} %get-tuple-element.100.fix_a, ...), custom_call_target="tpu_custom_call" | custom-call | tf_op jit(solution)/shard_map/pallas_call | solution.py:368
  (25 shorter events, 0.1 us)
Async XLA Ops:
  0.7 2.2 %copy-start.2 = (f32[8,16,64,128]{3,2,1,0:T(8,128)S(1)}, f32[8,16,64,128]{3,2,1,0:T(8,128)}, u32[]{:S(2)}) copy-start(f32[8,16,64,128]{3,2,1,0:T(8,128)} %f.1) | copy-start | bytes 12582916
  2.9 28.0 %copy-start.3 = (f32[8,16,64,128]{3,2,1,0:T(8,128)S(1)}, f32[8,16,64,128]{3,2,1,0:T(8,128)}, u32[]{:S(2)}) copy-start(f32[8,16,64,128]{3,2,1,0:T(8,128)} %c.1) | copy-start | bytes 12582916
  5.9 21.8 %collective-permute-start = (f32[16,32,128]{2,1,0:T(8,128)S(1)}, f32[16,32,128]{2,1,0:T(8,128)S(1)}, u32[]{:S(2)}, u32[]{:S(2)}) collective-permute-start(f32[16,32,128]{2,1,0:T(8,128)S(1)} %get-tuple-element.54), channel_id=1, source_target_pairs={{0,16},{16,0},{32,48},{48,32},{64,80},{80,64},{96,112},{112,96},{1... | collective-permute-start | bytes 786440 | tf_op jit(solution)/shard_map/ppermute | solution.py:309
  5.9 16.0 %collective-permute-start.2 = (f32[8,32,128]{2,1,0:T(8,128)S(1)}, f32[8,32,128]{2,1,0:T(8,128)S(1)}, u32[]{:S(2)}, u32[]{:S(2)}) collective-permute-start(f32[8,32,128]{2,1,0:T(8,128)S(1)} %get-tuple-element.56), channel_id=1, source_target_pairs={{0,4},{4,0},{8,12},{12,8},{1,5},{5,1},{9,13},{13,9},{2,6},{6,2},{1... | collective-permute-start | bytes 393224 | tf_op jit(solution)/shard_map/ppermute | solution.py:309
  8.2 12.0 %collective-permute-start.4 = (f32[8,16,128]{2,1,0:T(8,128)S(1)}, f32[8,16,128]{2,1,0:T(8,128)S(1)}, u32[]{:S(2)}, u32[]{:S(2)}) collective-permute-start(f32[8,16,128]{2,1,0:T(8,128)S(1)} %get-tuple-element.58), channel_id=1, source_target_pairs={{0,2},{2,0},{1,3},{3,1},{4,6},{6,4},{5,7},{7,5},{8,10},{10,8},{9,1... | collective-permute-start | bytes 196616 | tf_op jit(solution)/shard_map/ppermute | solution.py:309
  13.6 19.0 %collective-permute-start.1 = (f32[16,32,128]{2,1,0:T(8,128)S(1)}, f32[16,32,128]{2,1,0:T(8,128)S(1)}, u32[]{:S(2)}, u32[]{:S(2)}) collective-permute-start(f32[16,32,128]{2,1,0:T(8,128)S(1)} %get-tuple-element.55), channel_id=1, source_target_pairs={{16,32},{32,16},{48,64},{64,48},{80,96},{96,80},{112,128},{128,112... | collective-permute-start | bytes 786440 | tf_op jit(solution)/shard_map/ppermute | solution.py:309
  14.3 13.4 %collective-permute-start.3 = (f32[8,32,128]{2,1,0:T(8,128)S(1)}, f32[8,32,128]{2,1,0:T(8,128)S(1)}, u32[]{:S(2)}, u32[]{:S(2)}) collective-permute-start(f32[8,32,128]{2,1,0:T(8,128)S(1)} %get-tuple-element.57), channel_id=1, source_target_pairs={{4,8},{8,4},{5,9},{9,5},{6,10},{10,6},{7,11},{11,7},{20,24},{24,20... | collective-permute-start | bytes 393224 | tf_op jit(solution)/shard_map/ppermute | solution.py:309
  20.2 21.2 %collective-permute-start.9 = (f32[16,32,128]{2,1,0:T(8,128)S(1)}, f32[16,32,128]{2,1,0:T(8,128)S(1)}, u32[]{:S(2)}, u32[]{:S(2)}) collective-permute-start(f32[16,32,128]{2,1,0:T(8,128)S(1)} %get-tuple-element.66), channel_id=1, source_target_pairs={{0,16},{16,0},{32,48},{48,32},{64,80},{80,64},{96,112},{112,96},{1... | collective-permute-start | bytes 786440 | tf_op jit(solution)/shard_map/ppermute | solution.py:309
  21.9 19.4 %collective-permute-start.10 = (f32[16,32,128]{2,1,0:T(8,128)S(1)}, f32[16,32,128]{2,1,0:T(8,128)S(1)}, u32[]{:S(2)}, u32[]{:S(2)}) collective-permute-start(f32[16,32,128]{2,1,0:T(8,128)S(1)} %get-tuple-element.67), channel_id=1, source_target_pairs={{16,32},{32,16},{48,64},{64,48},{80,96},{96,80},{112,128},{128,112... | collective-permute-start | bytes 786440 | tf_op jit(solution)/shard_map/ppermute | solution.py:309
  27.7 7.8 %collective-permute-start.11 = (f32[8,32,128]{2,1,0:T(8,128)S(1)}, f32[8,32,128]{2,1,0:T(8,128)S(1)}, u32[]{:S(2)}, u32[]{:S(2)}) collective-permute-start(f32[8,32,128]{2,1,0:T(8,128)S(1)} %get-tuple-element.68), channel_id=1, source_target_pairs={{0,4},{4,0},{8,12},{12,8},{1,5},{5,1},{9,13},{13,9},{2,6},{6,2},{1... | collective-permute-start | bytes 393224 | tf_op jit(solution)/shard_map/ppermute | solution.py:309
  27.7 13.6 %collective-permute-start.12 = (f32[8,32,128]{2,1,0:T(8,128)S(1)}, f32[8,32,128]{2,1,0:T(8,128)S(1)}, u32[]{:S(2)}, u32[]{:S(2)}) collective-permute-start(f32[8,32,128]{2,1,0:T(8,128)S(1)} %get-tuple-element.69), channel_id=1, source_target_pairs={{4,8},{8,4},{5,9},{9,5},{6,10},{10,6},{7,11},{11,7},{20,24},{24,20... | collective-permute-start | bytes 393224 | tf_op jit(solution)/shard_map/ppermute | solution.py:309
  32.7 26.6 %copy-start = (f32[8,16,32,128]{3,2,1,0:T(8,128)}, f32[8,16,32,128]{3,2,1,0:T(8,128)S(1)}, u32[]{:S(2)}) copy-start(f32[8,16,32,128]{3,2,1,0:T(8,128)S(1)} %get-tuple-element.53.c) | copy-start | bytes 6291460
  34.3 21.2 %collective-permute-start.5 = (f32[16,32,128]{2,1,0:T(8,128)S(1)}, f32[16,32,128]{2,1,0:T(8,128)S(1)}, u32[]{:S(2)}, u32[]{:S(2)}) collective-permute-start(f32[16,32,128]{2,1,0:T(8,128)S(1)} %get-tuple-element.60), channel_id=1, source_target_pairs={{0,16},{16,0},{32,48},{48,32},{64,80},{80,64},{96,112},{112,96},{1... | collective-permute-start | bytes 786440 | tf_op jit(solution)/shard_map/ppermute | solution.py:309
  35.5 16.0 %collective-permute-start.7 = (f32[8,32,128]{2,1,0:T(8,128)S(1)}, f32[8,32,128]{2,1,0:T(8,128)S(1)}, u32[]{:S(2)}, u32[]{:S(2)}) collective-permute-start(f32[8,32,128]{2,1,0:T(8,128)S(1)} %get-tuple-element.62), channel_id=1, source_target_pairs={{0,4},{4,0},{8,12},{12,8},{1,5},{5,1},{9,13},{13,9},{2,6},{6,2},{1... | collective-permute-start | bytes 393224 | tf_op jit(solution)/shard_map/ppermute | solution.py:309
  43.1 8.2 %collective-permute-start.13 = (f32[8,16,128]{2,1,0:T(8,128)S(1)}, f32[8,16,128]{2,1,0:T(8,128)S(1)}, u32[]{:S(2)}, u32[]{:S(2)}) collective-permute-start(f32[8,16,128]{2,1,0:T(8,128)S(1)} %get-tuple-element.71), channel_id=1, source_target_pairs={{0,2},{2,0},{1,3},{3,1},{4,6},{6,4},{5,7},{7,5},{8,10},{10,8},{9,1... | collective-permute-start | bytes 196616 | tf_op jit(solution)/shard_map/ppermute | solution.py:309
  44.6 14.7 %collective-permute-start.6 = (f32[16,32,128]{2,1,0:T(8,128)S(1)}, f32[16,32,128]{2,1,0:T(8,128)S(1)}, u32[]{:S(2)}, u32[]{:S(2)}) collective-permute-start(f32[16,32,128]{2,1,0:T(8,128)S(1)} %get-tuple-element.61), channel_id=1, source_target_pairs={{16,32},{32,16},{48,64},{64,48},{80,96},{96,80},{112,128},{128,112... | collective-permute-start | bytes 786440 | tf_op jit(solution)/shard_map/ppermute | solution.py:309
  45.3 10.2 %collective-permute-start.8 = (f32[8,32,128]{2,1,0:T(8,128)S(1)}, f32[8,32,128]{2,1,0:T(8,128)S(1)}, u32[]{:S(2)}, u32[]{:S(2)}) collective-permute-start(f32[8,32,128]{2,1,0:T(8,128)S(1)} %get-tuple-element.63), channel_id=1, source_target_pairs={{4,8},{8,4},{5,9},{9,5},{6,10},{10,6},{7,11},{11,7},{20,24},{24,20... | collective-permute-start | bytes 393224 | tf_op jit(solution)/shard_map/ppermute | solution.py:309
  51.3 16.4 %collective-permute-start.14 = (f32[16,32,128]{2,1,0:T(8,128)S(1)}, f32[16,32,128]{2,1,0:T(8,128)S(1)}, u32[]{:S(2)}, u32[]{:S(2)}) collective-permute-start(f32[16,32,128]{2,1,0:T(8,128)S(1)} %get-tuple-element.75), channel_id=1, source_target_pairs={{0,16},{16,0},{32,48},{48,32},{64,80},{80,64},{96,112},{112,96},{1... | collective-permute-start | bytes 786440 | tf_op jit(solution)/shard_map/ppermute | solution.py:309
  51.5 16.2 %collective-permute-start.15 = (f32[16,32,128]{2,1,0:T(8,128)S(1)}, f32[16,32,128]{2,1,0:T(8,128)S(1)}, u32[]{:S(2)}, u32[]{:S(2)}) collective-permute-start(f32[16,32,128]{2,1,0:T(8,128)S(1)} %get-tuple-element.76), channel_id=1, source_target_pairs={{16,32},{32,16},{48,64},{64,48},{80,96},{96,80},{112,128},{128,112... | collective-permute-start | bytes 786440 | tf_op jit(solution)/shard_map/ppermute | solution.py:309
  55.5 7.0 %collective-permute-start.16 = (f32[8,32,128]{2,1,0:T(8,128)S(1)}, f32[8,32,128]{2,1,0:T(8,128)S(1)}, u32[]{:S(2)}, u32[]{:S(2)}) collective-permute-start(f32[8,32,128]{2,1,0:T(8,128)S(1)} %get-tuple-element.77), channel_id=1, source_target_pairs={{0,4},{4,0},{8,12},{12,8},{1,5},{5,1},{9,13},{13,9},{2,6},{6,2},{1... | collective-permute-start | bytes 393224 | tf_op jit(solution)/shard_map/ppermute | solution.py:309
  55.5 12.2 %collective-permute-start.17 = (f32[8,32,128]{2,1,0:T(8,128)S(1)}, f32[8,32,128]{2,1,0:T(8,128)S(1)}, u32[]{:S(2)}, u32[]{:S(2)}) collective-permute-start(f32[8,32,128]{2,1,0:T(8,128)S(1)} %get-tuple-element.78), channel_id=1, source_target_pairs={{4,8},{8,4},{5,9},{9,5},{6,10},{10,6},{7,11},{11,7},{20,24},{24,20... | collective-permute-start | bytes 393224 | tf_op jit(solution)/shard_map/ppermute | solution.py:309
  62.1 7.7 %copy-start.4 = (f32[8,16,32,128]{3,2,1,0:T(8,128)}, f32[8,16,32,128]{3,2,1,0:T(8,128)S(1)}, u32[]{:S(2)}) copy-start(f32[8,16,32,128]{3,2,1,0:T(8,128)S(1)} %get-tuple-element.89.f) | copy-start | bytes 6291460
  62.1 27.2 %collective-permute-start.18 = (f32[8,32,128]{2,1,0:T(8,128)S(1)}, f32[8,32,128]{2,1,0:T(8,128)S(1)}, u32[]{:S(2)}, u32[]{:S(2)}) collective-permute-start(f32[8,32,128]{2,1,0:T(8,128)S(1)} %get-tuple-element.82), channel_id=1, source_target_pairs={{0,4},{4,0},{8,12},{12,8},{1,5},{5,1},{9,13},{13,9},{2,6},{6,2},{1... | collective-permute-start | bytes 393224 | tf_op jit(solution)/shard_map/ppermute | solution.py:309
  62.5 26.8 %collective-permute-start.19 = (f32[8,32,128]{2,1,0:T(8,128)S(1)}, f32[8,32,128]{2,1,0:T(8,128)S(1)}, u32[]{:S(2)}, u32[]{:S(2)}) collective-permute-start(f32[8,32,128]{2,1,0:T(8,128)S(1)} %get-tuple-element.83), channel_id=1, source_target_pairs={{4,8},{8,4},{5,9},{9,5},{6,10},{10,6},{7,11},{11,7},{20,24},{24,20... | collective-permute-start | bytes 393224 | tf_op jit(solution)/shard_map/ppermute | solution.py:309
  69.8 1.3 copy-start.6
  71.1 0.7 copy-start.8
  71.8 0.7 copy-start.9
  72.5 16.8 %collective-permute-start.20 = (f32[8,32,128]{2,1,0:T(8,128)S(1)}, f32[8,32,128]{2,1,0:T(8,128)S(1)}, u32[]{:S(2)}, u32[]{:S(2)}) collective-permute-start(f32[8,32,128]{2,1,0:T(8,128)S(1)} %get-tuple-element.84), channel_id=1, source_target_pairs={{0,4},{4,0},{8,12},{12,8},{1,5},{5,1},{9,13},{13,9},{2,6},{6,2},{1... | collective-permute-start | bytes 393224 | tf_op jit(solution)/shard_map/ppermute | solution.py:309
  72.5 17.0 %collective-permute-start.21 = (f32[8,32,128]{2,1,0:T(8,128)S(1)}, f32[8,32,128]{2,1,0:T(8,128)S(1)}, u32[]{:S(2)}, u32[]{:S(2)}) collective-permute-start(f32[8,32,128]{2,1,0:T(8,128)S(1)} %get-tuple-element.85), channel_id=1, source_target_pairs={{4,8},{8,4},{5,9},{9,5},{6,10},{10,6},{7,11},{11,7},{20,24},{24,20... | collective-permute-start | bytes 393224 | tf_op jit(solution)/shard_map/ppermute | solution.py:309
  76.5 12.8 %collective-permute-start.22 = (f32[8,16,128]{2,1,0:T(8,128)S(1)}, f32[8,16,128]{2,1,0:T(8,128)S(1)}, u32[]{:S(2)}, u32[]{:S(2)}) collective-permute-start(f32[8,16,128]{2,1,0:T(8,128)S(1)} %get-tuple-element.86), channel_id=1, source_target_pairs={{0,2},{2,0},{1,3},{3,1},{4,6},{6,4},{5,7},{7,5},{8,10},{10,8},{9,1... | collective-permute-start | bytes 196616 | tf_op jit(solution)/shard_map/ppermute | solution.py:309
  91.1 20.9 %all-to-all-start = ((f32[16,64,128]{2,1,0:T(8,128)}), f32[16,64,128]{2,1,0:T(8,128)S(1)}, u32[]{:S(2)}, u32[]{:S(2)}) async-start(f32[16,64,128]{2,1,0:T(8,128)} %shard_map.47), calls=%async_computation | async-start | bytes 1048576 | tf_op jit(solution)/shard_map/all_to_all | solution.py:343
  101.1 10.9 %collective-permute-start.23 = (f32[16,32,128]{2,1,0:T(8,128)}, f32[16,32,128]{2,1,0:T(8,128)}, u32[]{:S(2)}, u32[]{:S(2)}) collective-permute-start(f32[16,32,128]{2,1,0:T(8,128)} %get-tuple-element.90), channel_id=1, source_target_pairs={{0,16},{16,0},{32,48},{48,32},{64,80},{80,64},{96,112},{112,96},{1... | collective-permute-start | bytes 786440 | tf_op jit(solution)/shard_map/ppermute | solution.py:309
  101.5 10.5 %collective-permute-start.24 = (f32[16,32,128]{2,1,0:T(8,128)}, f32[16,32,128]{2,1,0:T(8,128)}, u32[]{:S(2)}, u32[]{:S(2)}) collective-permute-start(f32[16,32,128]{2,1,0:T(8,128)} %get-tuple-element.91), channel_id=1, source_target_pairs={{16,32},{32,16},{48,64},{64,48},{80,96},{96,80},{112,128},{128,112... | collective-permute-start | bytes 786440 | tf_op jit(solution)/shard_map/ppermute | solution.py:309
  102.9 14.5 %collective-permute-start.25 = (f32[16,32,128]{2,1,0:T(8,128)}, f32[16,32,128]{2,1,0:T(8,128)S(1)}, u32[]{:S(2)}, u32[]{:S(2)}) collective-permute-start(f32[16,32,128]{2,1,0:T(8,128)} %copy-done.9), channel_id=1, source_target_pairs={{0,16},{16,0},{32,48},{48,32},{64,80},{80,64},{96,112},{112,96},{1... | collective-permute-start | bytes 786440 | tf_op jit(solution)/shard_map/ppermute | solution.py:309
  105.3 12.2 %collective-permute-start.26 = (f32[16,32,128]{2,1,0:T(8,128)}, f32[16,32,128]{2,1,0:T(8,128)}, u32[]{:S(2)}, u32[]{:S(2)}) collective-permute-start(f32[16,32,128]{2,1,0:T(8,128)} %copy-done.8), channel_id=1, source_target_pairs={{16,32},{32,16},{48,64},{64,48},{80,96},{96,80},{112,128},{128,112... | collective-permute-start | bytes 786440 | tf_op jit(solution)/shard_map/ppermute | solution.py:309
  112.0 1.6 %copy-start.1 = (f32[8,16,32,128]{3,2,1,0:T(8,128)S(1)}, f32[8,16,32,128]{3,2,1,0:T(8,128)}, u32[]{:S(2)}) copy-start(f32[8,16,32,128]{3,2,1,0:T(8,128)} %copy-done) | copy-start | bytes 6291460
  113.6 1.6 %copy-start.5 = (f32[8,16,32,128]{3,2,1,0:T(8,128)S(1)}, f32[8,16,32,128]{3,2,1,0:T(8,128)}, u32[]{:S(2)}) copy-start(f32[8,16,32,128]{3,2,1,0:T(8,128)} %copy-done.4) | copy-start | bytes 6291460
  115.2 2.3 %copy-start.7 = (f32[8,16,32,128]{3,2,1,0:T(8,128)S(1)}, f32[8,16,32,128]{3,2,1,0:T(8,128)}, u32[]{:S(2)}) copy-start(f32[8,16,32,128]{3,2,1,0:T(8,128)} %copy-done.6) | copy-start | bytes 6291460

commit v5 on v4

--- a/solution.py
+++ b/solution.py
@@ -69,28 +69,62 @@
         s_k[j] = rows
 
 
-def pack_field(place, f, fa, fb, *faces):
+def pack_faces(place, f, *rest):
+    sa, sb, s_k = rest[:4], rest[4:8], rest[8]
+    rlo, rhi, clo, chi, klo, khi, sems = rest[9:]
     nj, ni, nk = f.shape[:3]
-    sa, sb = faces[:5], faces[5:]
+    copies = [
+        pltpu.make_async_copy(part, into, sems.at[n])
+        for n, (part, into) in enumerate(
+            (
+                (f.at[0], rlo),
+                (f.at[nj - 1], rhi),
+                (f.at[:, 0], clo),
+                (f.at[:, ni - 1], chi),
+                (f.at[:, :, pl.ds(0, TILE)], klo),
+                (f.at[:, :, pl.ds(nk - TILE, TILE)], khi),
+            )
+        )
+    ]
+    for copy in copies:
+        copy.start()
+
+    def face(n, low, high, even, slot):
+        for t in range(nk // 2 // TILE):
+            lo, hi = pl.ds(t * TILE, TILE), pl.ds(nk // 2 + t * TILE, TILE)
+            first = exchange_halves(low[n, lo, :], low[n, hi, :])
+            last = exchange_halves(high[n, lo, :], high[n, hi, :])
+            for s, v, w in zip((sa, sb), first, last):
+                s[slot][n, lo, :] = jnp.where(even, w, v)
+                s[slot + 1][n, lo, :] = jnp.where(even, v, w)
+
+    def along(pair, _):
+        for n in range(2):
+            face(2 * pair + n, rlo, rhi, place[0] == 0, 0)
+        return 0
+
+    copies[0].wait()
+    copies[1].wait()
+    lax.fori_loop(0, ni // 2, along, 0)
+    for copy in copies[2:]:
+        copy.wait()
+    for j in range(nj):
+        face(j, clo, chi, place[1] == 0, 2)
+        s_k[j] = jnp.where(place[2] == 0, swap(khi[j, :, TILE - 1, :]), klo[j, :, 0, :])
+
+
+def pack_field(f, fa, fb):
+    nj, ni, nk = f.shape[:3]
 
     def at(i, _):
-        for t in range(nk // 2 // TILE):
-            ends = {}
-            for j in range(nj):
+        for j in range(nj):
+            for t in range(nk // 2 // TILE):
                 a, b = pack_tiles(f, j, i, t, nk)
                 fa[j, i, pl.ds(t * TILE, TILE), :] = a
                 fb[j, i, pl.ds(t * TILE, TILE), :] = b
-                if j in (0, nj - 1):
-                    ends[j] = (a, b)
-            for n, s in ((0, sa), (1, sb)):
-                first, last = ends[0][n], ends[nj - 1][n]
-                s[0][i, pl.ds(t * TILE, TILE), :] = jnp.where(place[0] == 0, last, first)
-                s[1][i, pl.ds(t * TILE, TILE), :] = jnp.where(place[0] == 0, first, last)
         return 0
 
     lax.fori_loop(0, ni, at, 0)
-    write_faces(place, fa, *sa[2:], None)
-    write_faces(place, fb, *sb[2:], sa[4])
 
 
 def pack_crowding(c, ca, cb):
@@ -317,13 +351,21 @@
     row = lax.axis_index("rows")
     place = jnp.stack([row % 2, lax.axis_index("cols") % 2, lax.axis_index("slabs"), row == 0])
     place = place.astype(jnp.int32)
-    out = call(
-        pack_field, [half, half] + faces + faces, (place, field_values), in_specs=[SMEM, VMEM]
-    )
-    f, sent = [out[0], out[1]], [out[2:7], out[7:12]]
+    sent = pl.pallas_call(
+        pack_faces,
+        out_shape=[jax.ShapeDtypeStruct(shape, jnp.float32) for shape in faces[:4] * 2 + faces[4:]],
+        in_specs=[SMEM, pl.BlockSpec(memory_space=pltpu.MemorySpace.HBM)],
+        scratch_shapes=[pltpu.VMEM((ni, nk, nl), jnp.float32)] * 2
+        + [pltpu.VMEM((nj, nk, nl), jnp.float32)] * 2
+        + [pltpu.VMEM((nj, ni, TILE, nl), jnp.float32)] * 2
+        + [pltpu.SemaphoreType.DMA((6,))],
+        compiler_params=pltpu.CompilerParams(vmem_limit_bytes=16 * 1024 * 1024),
+    )(place, pltpu.with_memory_space_constraint(field_values, pltpu.MemorySpace.HBM))
+    sent = [[*sent[:4], None], sent[4:]]
     halos = [None, None]
     for h in range(2):
         halos[h], across = exchange(sent[h], 0, h)
+    f = list(call(pack_field, [half, half], (field_values,)))
     c = call(pack_crowding, [half, half], (crowding,))
     scratch = [(nj, ni, nl)] * 2
     sums, fix, other = [None, None], [None, None], None

time: 143 us -> 142 us (level)
  local copies, waits for them, and re-layouts: 8.12 us -> 5.93 us
  Pallas kernels: 22.3 us -> 23.9 us
  waiting for transfers between devices: 31 us -> 29.5 us
    pallas_call x0 -> x1, Pallas kernels: none -> 2.91 us  [on_device(): pl.pallas_call(pack_faces, out_shape=[jax.ShapeDtypeStruct(shape, jnp.flo...]
    unnamed x20, local copies, waits for them, and re-layouts: 8.12 us -> 5.93 us
    ppermute x27, waiting for transfers between devices: 25.7 us -> 24.2 us  [exchange(): got[kind] = lax.ppermute(*sends[kind])]
    all_to_all x1, starting transfers between devices: 10 us -> 11.5 us  [on_device(): gathered = lax.all_to_all(total, 'rows', 0, 0, tiled=True)]
  transfers between devices with their start and end apart: 28 -> 28, of which waited for: 9 -> 7; matrix products, arithmetic and copies ran while one was open for 0% -> 0% of each run, Pallas kernels for 9% -> 10%
where the time goes in v5:
time: 142 us; the launch traced here: 141 us
  starting transfers between devices  61.4 us (43%)
  waiting for transfers between devices  29.5 us (21%)
  Pallas kernels  23.9 us (17%)
  blocking collectives  19.1 us (13%)
  local copies, waits for them, and re-layouts  5.93 us (4%)
    ppermute x27, starting transfers between devices, exchange(): got[kind] = lax.ppermute(*sends[kind])  49.9 us
    ppermute x27, waiting for transfers between devices, exchange(): got[kind] = lax.ppermute(*sends[kind])  24.2 us
    all_to_all x1, blocking collectives, on_device(): base = lax.all_to_all(before, 'rows', 0, 0, tiled=True).reshape(ni, nk, nl)  19.1 us
    pallas_call x10, Pallas kernels, call(): pl.pallas_call(body, out_shape=[jax.ShapeDtypeStruct(s, jnp.float32) for...  17.4 us
    all_to_all x1, starting transfers between devices, on_device(): gathered = lax.all_to_all(total, 'rows', 0, 0, tiled=True)  11.5 us
    unnamed x20, local copies, waits for them, and re-layouts  5.93 us
    all_to_all x1, waiting for transfers between devices, on_device(): gathered = lax.all_to_all(total, 'rows', 0, 0, tiled=True)  5.32 us
    pallas_call x1, Pallas kernels, on_device(): pl.pallas_call(functools.partial(finish_body, 1.0 / (nj * rows)), out_sha...  3.58 us
  transfers between devices with their start and end apart: 28, of which 7 were waited for; matrix products, arithmetic and copies ran while one was open for 0% of the time, Pallas kernels for 10%

profile of v5, /device:TPU:4, one launch (start us, length us, event | category | flops | bytes accessed | tf_op | source)
XLA Modules:
  0.0 140.9 jit_solution(16380747150855810207)
XLA Ops:
  0.6 0.1 pad_add_fusion.place
  0.7 2.9 %shard_map.43 = (f32[16,32,128]{2,1,0:T(8,128)S(1)}, f32[16,32,128]{2,1,0:T(8,128)S(1)}, f32[8,32,128]{2,1,0:T(8,128)S(1)}, f32[8,32,128]{2,1,0:T(8,128)S(1)}, f...) custom-call(s32[4]{0:T(128)S(1)} %pad_add_fusion.place, ...), custom_call_target="tpu_custom_call" | custom-call | tf_op jit(solution)/shard_map/pallas_call | solution.py:354
  3.7 0.1 collective-permute-start
  3.8 2.3 %collective-permute-start.2 = (f32[8,32,128]{2,1,0:T(8,128)S(1)}, f32[8,32,128]{2,1,0:T(8,128)S(1)}, u32[]{:S(2)}, u32[]{:S(2)}) collective-permute-start(f32[8,32,128]{2,1,0:T(8,128)S(1)} %get-tuple-element.56), channel_id=1, source_target_pairs={{0,4},{4,0},{8,12},{12,8},{1,5},{5,1},{9,13},{13,9},{2,6},{6,2},{1... | collective-permute-start | bytes 393224 | tf_op jit(solution)/shard_map/ppermute | solution.py:343
  6.1 5.5 %collective-permute-start.4 = (f32[8,16,128]{2,1,0:T(8,128)S(1)}, f32[8,16,128]{2,1,0:T(8,128)S(1)}, u32[]{:S(2)}, u32[]{:S(2)}) collective-permute-start(f32[8,16,128]{2,1,0:T(8,128)S(1)} %get-tuple-element.58), channel_id=1, source_target_pairs={{0,2},{2,0},{1,3},{3,1},{4,6},{6,4},{5,7},{7,5},{8,10},{10,8},{9,1... | collective-permute-start | bytes 196616 | tf_op jit(solution)/shard_map/ppermute | solution.py:343
  11.5 0.7 collective-permute-start.1
  12.2 5.8 %collective-permute-start.3 = (f32[8,32,128]{2,1,0:T(8,128)S(1)}, f32[8,32,128]{2,1,0:T(8,128)S(1)}, u32[]{:S(2)}, u32[]{:S(2)}) collective-permute-start(f32[8,32,128]{2,1,0:T(8,128)S(1)} %get-tuple-element.57), channel_id=1, source_target_pairs={{4,8},{8,4},{5,9},{9,5},{6,10},{10,6},{7,11},{11,7},{20,24},{24,20... | collective-permute-start | bytes 393224 | tf_op jit(solution)/shard_map/ppermute | solution.py:343
  18.1 0.0 collective-permute-done.4.ks
  18.1 1.7 %collective-permute-start.9 = (f32[16,32,128]{2,1,0:T(8,128)S(1)}, f32[16,32,128]{2,1,0:T(8,128)S(1)}, u32[]{:S(2)}, u32[]{:S(2)}) collective-permute-start(f32[16,32,128]{2,1,0:T(8,128)S(1)} %get-tuple-element.66), channel_id=1, source_target_pairs={{0,16},{16,0},{32,48},{48,32},{64,80},{80,64},{96,112},{112,96},{1... | collective-permute-start | bytes 786440 | tf_op jit(solution)/shard_map/ppermute | solution.py:343
  19.8 0.0 collective-permute-done.2.c0
  19.8 0.7 collective-permute-start.10
  20.5 5.1 %collective-permute-done.3.c1 = f32[8,32,128]{2,1,0:T(8,128)S(1)} collective-permute-done((f32[8,32,128]{2,1,0:T(8,128)S(1)}, f32[8,32,128]{2,1,0:T(8,128)S(1)}, u32[]{:S(2)}, u32[]{:S(2)}) %collective-permute-start.3) | collective-permute-done | bytes 131104 | tf_op jit(solution)/shard_map/ppermute | solution.py:343
  25.6 0.0 collective-permute-start.11
  25.6 0.0 collective-permute-done.r0
  25.6 3.5 %collective-permute-start.12 = (f32[8,32,128]{2,1,0:T(8,128)S(1)}, f32[8,32,128]{2,1,0:T(8,128)S(1)}, u32[]{:S(2)}, u32[]{:S(2)}) collective-permute-start(f32[8,32,128]{2,1,0:T(8,128)S(1)} %get-tuple-element.69), channel_id=1, source_target_pairs={{4,8},{8,4},{5,9},{9,5},{6,10},{10,6},{7,11},{11,7},{20,24},{24,20... | collective-permute-start | bytes 393224 | tf_op jit(solution)/shard_map/ppermute | solution.py:343
  29.1 1.7 %shard_map.41 = (f32[8,16,32,128]{3,2,1,0:T(8,128)S(1)}, f32[8,16,32,128]{3,2,1,0:T(8,128)S(1)}) custom-call(f32[8,16,64,128]{3,2,1,0:T(8,128)S(1)} %copy-done.2), custom_call_target="tpu_custom_call" | custom-call | tf_op jit(solution)/shard_map/pallas_call | solution.py:24
  30.8 1.7 %shard_map.42 = (f32[8,16,32,128]{3,2,1,0:T(8,128)S(1)}, f32[8,16,32,128]{3,2,1,0:T(8,128)S(1)}) custom-call(f32[8,16,64,128]{3,2,1,0:T(8,128)S(1)} %copy-done.3), custom_call_target="tpu_custom_call" | custom-call | tf_op jit(solution)/shard_map/pallas_call | solution.py:24
  32.5 0.0 copy-start
  32.5 0.0 collective-permute-done.1.r1
  32.5 1.6 %shard_map.44 = (f32[8,16,32,128]{3,2,1,0:T(8,128)S(1)}, f32[16,32,128]{2,1,0:T(8,128)S(1)}, f32[16,32,128]{2,1,0:T(8,128)S(1)}, f32[8,32,128]{2,1,0:T(8,128)S(1...) custom-call(s32[4]{0:T(128)S(1)} %pad_add_fusion.place, f32[8,16,32,128]{3,2,1,0:T(8,128)S(1)} %get-tuple-element.52.f, ...), custom_call_target="tpu_custom_call" | custom-call | tf_op jit(solution)/shard_map/pallas_call | solution.py:24
  34.2 0.6 collective-permute-start.5
  34.8 0.0 collective-permute-done.11.c0
  34.8 0.9 collective-permute-start.7
  35.7 3.8 %collective-permute-done.12.c1 = f32[8,32,128]{2,1,0:T(8,128)S(1)} collective-permute-done((f32[8,32,128]{2,1,0:T(8,128)S(1)}, f32[8,32,128]{2,1,0:T(8,128)S(1)}, u32[]{:S(2)}, u32[]{:S(2)}) %collective-permute-start.12) | collective-permute-done | bytes 131104 | tf_op jit(solution)/shard_map/ppermute | solution.py:343
  39.5 1.7 %shard_map.45 = (f32[8,16,32,128]{3,2,1,0:T(8,128)S(1)}, f32[16,32,128]{2,1,0:T(8,128)S(1)}, f32[16,32,128]{2,1,0:T(8,128)S(1)}, f32[8,32,128]{2,1,0:T(8,128)S(1...) custom-call(s32[4]{0:T(128)S(1)} %pad_add_fusion.place, f32[8,16,32,128]{3,2,1,0:T(8,128)S(1)} %get-tuple-element.64.f, ...), custom_call_target="tpu_custom_call" | custom-call | tf_op jit(solution)/shard_map/pallas_call | solution.py:24
  41.2 1.5 %collective-permute-start.13 = (f32[8,16,128]{2,1,0:T(8,128)S(1)}, f32[8,16,128]{2,1,0:T(8,128)S(1)}, u32[]{:S(2)}, u32[]{:S(2)}) collective-permute-start(f32[8,16,128]{2,1,0:T(8,128)S(1)} %get-tuple-element.71), channel_id=1, source_target_pairs={{0,2},{2,0},{1,3},{3,1},{4,6},{6,4},{5,7},{7,5},{8,10},{10,8},{9,1... | collective-permute-start | bytes 196616 | tf_op jit(solution)/shard_map/ppermute | solution.py:343
  42.7 0.7 collective-permute-start.6
  43.4 1.9 %collective-permute-start.8 = (f32[8,32,128]{2,1,0:T(8,128)S(1)}, f32[8,32,128]{2,1,0:T(8,128)S(1)}, u32[]{:S(2)}, u32[]{:S(2)}) collective-permute-start(f32[8,32,128]{2,1,0:T(8,128)S(1)} %get-tuple-element.63), channel_id=1, source_target_pairs={{4,8},{8,4},{5,9},{9,5},{6,10},{10,6},{7,11},{11,7},{20,24},{24,20... | collective-permute-start | bytes 393224 | tf_op jit(solution)/shard_map/ppermute | solution.py:343
  45.3 4.5 %collective-permute-done.13.ks = f32[8,16,128]{2,1,0:T(8,128)S(1)} collective-permute-done((f32[8,16,128]{2,1,0:T(8,128)S(1)}, f32[8,16,128]{2,1,0:T(8,128)S(1)}, u32[]{:S(2)}, u32[]{:S(2)}) %collective-permute-start.13) | collective-permute-done | bytes 65568 | tf_op jit(solution)/shard_map/ppermute | solution.py:343
  49.8 0.7 collective-permute-start.15
  50.5 3.3 %collective-permute-done.8.c1 = f32[8,32,128]{2,1,0:T(8,128)S(1)} collective-permute-done((f32[8,32,128]{2,1,0:T(8,128)S(1)}, f32[8,32,128]{2,1,0:T(8,128)S(1)}, u32[]{:S(2)}, u32[]{:S(2)}) %collective-permute-start.8) | collective-permute-done | bytes 131104 | tf_op jit(solution)/shard_map/ppermute | solution.py:343
  53.8 0.0 collective-permute-done.5.r0
  53.8 3.8 %collective-permute-start.17 = (f32[8,32,128]{2,1,0:T(8,128)S(1)}, f32[8,32,128]{2,1,0:T(8,128)S(1)}, u32[]{:S(2)}, u32[]{:S(2)}) collective-permute-start(f32[8,32,128]{2,1,0:T(8,128)S(1)} %get-tuple-element.78), channel_id=1, source_target_pairs={{4,8},{8,4},{5,9},{9,5},{6,10},{10,6},{7,11},{11,7},{20,24},{24,20... | collective-permute-start | bytes 393224 | tf_op jit(solution)/shard_map/ppermute | solution.py:343
  57.6 0.0 collective-permute-done.6.r1
  57.6 2.8 %shard_map.46 = (f32[8,16,32,128]{3,2,1,0:T(8,128)S(1)}, f32[16,32,128]{2,1,0:T(8,128)}, f32[16,32,128]{2,1,0:T(8,128)}, f32[8,32,128]{2,1,0:T(8,128)S(1)}, f32[...) custom-call(s32[4]{0:T(128)S(1)} %pad_add_fusion.place, ...), custom_call_target="tpu_custom_call" | custom-call | tf_op jit(solution)/shard_map/pallas_call | solution.py:24
  60.4 0.4 collective-permute-start.18
  60.8 0.0 collective-permute-done.16.c0
  60.9 5.0 %collective-permute-start.19 = (f32[8,32,128]{2,1,0:T(8,128)S(1)}, f32[8,32,128]{2,1,0:T(8,128)S(1)}, u32[]{:S(2)}, u32[]{:S(2)}) collective-permute-start(f32[8,32,128]{2,1,0:T(8,128)S(1)} %get-tuple-element.83), channel_id=1, source_target_pairs={{4,8},{8,4},{5,9},{9,5},{6,10},{10,6},{7,11},{11,7},{20,24},{24,20... | collective-permute-start | bytes 393224 | tf_op jit(solution)/shard_map/ppermute | solution.py:343
  65.8 0.0 collective-permute-done.14.r0
  65.8 0.0 collective-permute-done.15.r1
  65.8 2.1 %shard_map.47 = (f32[8,16,32,128]{3,2,1,0:T(8,128)S(1)}, f32[16,32,128]{2,1,0:T(8,128)S(1)}, f32[16,32,128]{2,1,0:T(8,128)S(1)}, f32[8,32,128]{2,1,0:T(8,128)S(1...) custom-call(s32[4]{0:T(128)S(1)} %pad_add_fusion.place, ...), custom_call_target="tpu_custom_call" | custom-call | tf_op jit(solution)/shard_map/pallas_call | solution.py:24
  67.9 1.3 copy-done.6
  69.3 0.7 copy-done.8
  70.0 0.7 copy-done.9
  70.7 4.2 %collective-permute-start.21 = (f32[8,32,128]{2,1,0:T(8,128)S(1)}, f32[8,32,128]{2,1,0:T(8,128)S(1)}, u32[]{:S(2)}, u32[]{:S(2)}) collective-permute-start(f32[8,32,128]{2,1,0:T(8,128)S(1)} %get-tuple-element.85), channel_id=1, source_target_pairs={{4,8},{8,4},{5,9},{9,5},{6,10},{10,6},{7,11},{11,7},{20,24},{24,20... | collective-permute-start | bytes 393224 | tf_op jit(solution)/shard_map/ppermute | solution.py:343
  74.9 4.5 %collective-permute-start.22 = (f32[8,16,128]{2,1,0:T(8,128)S(1)}, f32[8,16,128]{2,1,0:T(8,128)S(1)}, u32[]{:S(2)}, u32[]{:S(2)}) collective-permute-start(f32[8,16,128]{2,1,0:T(8,128)S(1)} %get-tuple-element.86), channel_id=1, source_target_pairs={{0,2},{2,0},{1,3},{3,1},{4,6},{6,4},{5,7},{7,5},{8,10},{10,8},{9,1... | collective-permute-start | bytes 196616 | tf_op jit(solution)/shard_map/ppermute | solution.py:343
  79.4 5.1 %collective-permute-done.22.ks = f32[8,16,128]{2,1,0:T(8,128)S(1)} collective-permute-done((f32[8,16,128]{2,1,0:T(8,128)S(1)}, f32[8,16,128]{2,1,0:T(8,128)S(1)}, u32[]{:S(2)}, u32[]{:S(2)}) %collective-permute-start.22) | collective-permute-done | bytes 65568 | tf_op jit(solution)/shard_map/ppermute | solution.py:343
  84.4 2.3 %collective-permute-done.21.c1_b.c1 = f32[8,32,128]{2,1,0:T(8,128)S(1)} collective-permute-done((f32[8,32,128]{2,1,0:T(8,128)S(1)}, f32[8,32,128]{2,1,0:T(8,128)S(1)}, u32[]{:S(2)}, u32[]{:S(2)}) %collective-permute-start.21) | collective-permute-done | bytes 131104 | tf_op jit(solution)/shard_map/ppermute | solution.py:343
  86.7 1.6 %shard_map.48 = f32[16,64,128]{2,1,0:T(8,128)} custom-call(s32[4]{0:T(128)S(1)} %pad_add_fusion.place, f32[16,32,128]{2,1,0:T(8,128)S(1)} %get-tuple-element.72.g_a, f32[16,32,128]{2,1,0:T(8,128)S(1)} %get-tuple-element.73.s_a, f32[16,32,128]{2,1,0:T(8,128)S(1)} %get-tuple-element.80.g_b, f32[16,32,128]{2,1,0:T(8,128)S(1)} %get-tuple-element.81.s_b, ...), custom_call_target="tpu_custom_call" | custom-call | tf_op jit(solution)/shard_map/pallas_call | solution.py:24
  88.3 11.5 %all-to-all-start = ((f32[16,64,128]{2,1,0:T(8,128)}), f32[16,64,128]{2,1,0:T(8,128)S(1)}, u32[]{:S(2)}, u32[]{:S(2)}) async-start(f32[16,64,128]{2,1,0:T(8,128)} %shard_map.48), calls=%async_computation | async-start | bytes 1048576 | tf_op jit(solution)/shard_map/all_to_all | solution.py:385
  99.8 0.4 collective-permute-start.23
  100.2 1.4 collective-permute-start.24
  101.6 2.4 %collective-permute-start.25 = (f32[16,32,128]{2,1,0:T(8,128)}, f32[16,32,128]{2,1,0:T(8,128)S(1)}, u32[]{:S(2)}, u32[]{:S(2)}) collective-permute-start(f32[16,32,128]{2,1,0:T(8,128)} %copy-done.9), channel_id=1, source_target_pairs={{0,16},{16,0},{32,48},{48,32},{64,80},{80,64},{96,112},{112,96},{1... | collective-permute-start | bytes 786440 | tf_op jit(solution)/shard_map/ppermute | solution.py:343
  104.0 1.4 collective-permute-start.26
  105.3 5.3 %all-to-all-done.g = f32[16,64,128]{2,1,0:T(8,128)S(1)} async-done(((f32[16,64,128]{2,1,0:T(8,128)}), f32[16,64,128]{2,1,0:T(8,128)S(1)}, u32[]{:S(2)}, u32[]{:S(2)}) %all-to-all-start) | async-done | bytes 524320 | tf_op jit(solution)/shard_map/all_to_all | solution.py:385
  110.7 0.0 collective-permute-done.24.r1
  110.7 0.0 copy-start.1
  110.7 1.6 %copy-done.1 = f32[8,16,32,128]{3,2,1,0:T(8,128)S(1)} copy-done((f32[8,16,32,128]{3,2,1,0:T(8,128)S(1)}, f32[8,16,32,128]{3,2,1,0:T(8,128)}, u32[]{:S(2)}) %copy-start.1) | copy-done | bytes 2097176
  112.3 1.6 %copy-done.5 = f32[8,16,32,128]{3,2,1,0:T(8,128)S(1)} copy-done((f32[8,16,32,128]{3,2,1,0:T(8,128)S(1)}, f32[8,16,32,128]{3,2,1,0:T(8,128)}, u32[]{:S(2)}) %copy-start.5) | copy-done | bytes 2097176
  113.9 2.2 %shard_map.50 = (f32[8,16,32,128]{3,2,1,0:T(8,128)S(1)}, f32[16,32,128]{2,1,0:T(8,128)S(1)}) custom-call(s32[4]{0:T(128)S(1)} %pad_add_fusion.place, f32[8,16,32,128]{3,2,1,0:T(8,128)S(1)} %copy-done.5, f32[8,16,32,128]{3,2,1,0:T(8,128)S(1)} %copy-done.1, f32[16,32,128]{2,1,0:T(8,128)} %collective-permute-done.23.r0, ...), custom_call_target="tpu_custom_call" | custom-call | tf_op jit(solution)/shard_map/pallas_call | solution.py:24
  116.2 0.0 collective-permute-done.26.r1
  116.2 2.0 %shard_map.51 = (f32[8,16,32,128]{3,2,1,0:T(8,128)S(1)}, f32[16,32,128]{2,1,0:T(8,128)S(1)}) custom-call(s32[4]{0:T(128)S(1)} %pad_add_fusion.place, f32[8,16,32,128]{3,2,1,0:T(8,128)S(1)} %copy-done.7, f32[8,16,32,128]{3,2,1,0:T(8,128)S(1)} %get-tuple-element.65.c, f32[16,32,128]{2,1,0:T(8,128)S(1)} %collective-permute-done.25.r0, ...), custom_call_target="tpu_custom_call" | custom-call | tf_op jit(solution)/shard_map/pallas_call | solution.py:24
  118.2 19.1 %all_to_all.10.base = f32[16,64,128]{2,1,0:T(8,128)S(1)} all-to-all(f32[16,64,128]{2,1,0:T(8,128)S(1)} %shard_map.49), channel_id=1, replica_groups=mesh['rows'=16,'cols'=4,'slabs'=2,'trial'=2] {'rows'}, dimensions={0} | all-to-all | bytes 1048576 | tf_op jit(solution)/shard_map/all_to_all | solution.py:409
  137.3 3.6 %shard_map.52 = (f32[8,16,64,128]{3,2,1,0:T(8,128)}, f32[8,16,64,128]{3,2,1,0:T(8,128)}) custom-call(f32[8,16,32,128]{3,2,1,0:T(8,128)S(1)} %get-tuple-element.97.fa, f32[8,16,32,128]{3,2,1,0:T(8,128)S(1)} %get-tuple-element.98.fb, f32[16,64,128]{2,1,0:T(8,128)S(1)} %all_to_all.10.base, f32[16,32,128]{2,1,0:T(8,128)S(1)} %get-tuple-element.100.fix_a, ...), custom_call_target="tpu_custom_call" | custom-call | tf_op jit(solution)/shard_map/pallas_call | solution.py:410
  (26 shorter events, 0.1 us)
Async XLA Ops:
  0.7 28.4 %copy-start.2 = (f32[8,16,64,128]{3,2,1,0:T(8,128)S(1)}, f32[8,16,64,128]{3,2,1,0:T(8,128)}, u32[]{:S(2)}) copy-start(f32[8,16,64,128]{3,2,1,0:T(8,128)} %f.3) | copy-start | bytes 12582916
  3.7 22.0 %collective-permute-start = (f32[16,32,128]{2,1,0:T(8,128)S(1)}, f32[16,32,128]{2,1,0:T(8,128)S(1)}, u32[]{:S(2)}, u32[]{:S(2)}) collective-permute-start(f32[16,32,128]{2,1,0:T(8,128)S(1)} %get-tuple-element.54), channel_id=1, source_target_pairs={{0,16},{16,0},{32,48},{48,32},{64,80},{80,64},{96,112},{112,96},{1... | collective-permute-start | bytes 786440 | tf_op jit(solution)/shard_map/ppermute | solution.py:343
  3.8 16.1 %collective-permute-start.2 = (f32[8,32,128]{2,1,0:T(8,128)S(1)}, f32[8,32,128]{2,1,0:T(8,128)S(1)}, u32[]{:S(2)}, u32[]{:S(2)}) collective-permute-start(f32[8,32,128]{2,1,0:T(8,128)S(1)} %get-tuple-element.56), channel_id=1, source_target_pairs={{0,4},{4,0},{8,12},{12,8},{1,5},{5,1},{9,13},{13,9},{2,6},{6,2},{1... | collective-permute-start | bytes 393224 | tf_op jit(solution)/shard_map/ppermute | solution.py:343
  6.1 12.0 %collective-permute-start.4 = (f32[8,16,128]{2,1,0:T(8,128)S(1)}, f32[8,16,128]{2,1,0:T(8,128)S(1)}, u32[]{:S(2)}, u32[]{:S(2)}) collective-permute-start(f32[8,16,128]{2,1,0:T(8,128)S(1)} %get-tuple-element.58), channel_id=1, source_target_pairs={{0,2},{2,0},{1,3},{3,1},{4,6},{6,4},{5,7},{7,5},{8,10},{10,8},{9,1... | collective-permute-start | bytes 196616 | tf_op jit(solution)/shard_map/ppermute | solution.py:343
  11.5 21.0 %collective-permute-start.1 = (f32[16,32,128]{2,1,0:T(8,128)S(1)}, f32[16,32,128]{2,1,0:T(8,128)S(1)}, u32[]{:S(2)}, u32[]{:S(2)}) collective-permute-start(f32[16,32,128]{2,1,0:T(8,128)S(1)} %get-tuple-element.55), channel_id=1, source_target_pairs={{16,32},{32,16},{48,64},{64,48},{80,96},{96,80},{112,128},{128,112... | collective-permute-start | bytes 786440 | tf_op jit(solution)/shard_map/ppermute | solution.py:343
  12.2 13.4 %collective-permute-start.3 = (f32[8,32,128]{2,1,0:T(8,128)S(1)}, f32[8,32,128]{2,1,0:T(8,128)S(1)}, u32[]{:S(2)}, u32[]{:S(2)}) collective-permute-start(f32[8,32,128]{2,1,0:T(8,128)S(1)} %get-tuple-element.57), channel_id=1, source_target_pairs={{4,8},{8,4},{5,9},{9,5},{6,10},{10,6},{7,11},{11,7},{20,24},{24,20... | collective-permute-start | bytes 393224 | tf_op jit(solution)/shard_map/ppermute | solution.py:343
  18.1 21.4 %collective-permute-start.9 = (f32[16,32,128]{2,1,0:T(8,128)S(1)}, f32[16,32,128]{2,1,0:T(8,128)S(1)}, u32[]{:S(2)}, u32[]{:S(2)}) collective-permute-start(f32[16,32,128]{2,1,0:T(8,128)S(1)} %get-tuple-element.66), channel_id=1, source_target_pairs={{0,16},{16,0},{32,48},{48,32},{64,80},{80,64},{96,112},{112,96},{1... | collective-permute-start | bytes 786440 | tf_op jit(solution)/shard_map/ppermute | solution.py:343
  19.8 19.7 %collective-permute-start.10 = (f32[16,32,128]{2,1,0:T(8,128)S(1)}, f32[16,32,128]{2,1,0:T(8,128)S(1)}, u32[]{:S(2)}, u32[]{:S(2)}) collective-permute-start(f32[16,32,128]{2,1,0:T(8,128)S(1)} %get-tuple-element.67), channel_id=1, source_target_pairs={{16,32},{32,16},{48,64},{64,48},{80,96},{96,80},{112,128},{128,112... | collective-permute-start | bytes 786440 | tf_op jit(solution)/shard_map/ppermute | solution.py:343
  25.6 9.1 %collective-permute-start.11 = (f32[8,32,128]{2,1,0:T(8,128)S(1)}, f32[8,32,128]{2,1,0:T(8,128)S(1)}, u32[]{:S(2)}, u32[]{:S(2)}) collective-permute-start(f32[8,32,128]{2,1,0:T(8,128)S(1)} %get-tuple-element.68), channel_id=1, source_target_pairs={{0,4},{4,0},{8,12},{12,8},{1,5},{5,1},{9,13},{13,9},{2,6},{6,2},{1... | collective-permute-start | bytes 393224 | tf_op jit(solution)/shard_map/ppermute | solution.py:343
  25.6 5.2 %copy-start.3 = (f32[8,16,64,128]{3,2,1,0:T(8,128)S(1)}, f32[8,16,64,128]{3,2,1,0:T(8,128)}, u32[]{:S(2)}) copy-start(f32[8,16,64,128]{3,2,1,0:T(8,128)} %c.1) | copy-start | bytes 12582916
  25.6 13.9 %collective-permute-start.12 = (f32[8,32,128]{2,1,0:T(8,128)S(1)}, f32[8,32,128]{2,1,0:T(8,128)S(1)}, u32[]{:S(2)}, u32[]{:S(2)}) collective-permute-start(f32[8,32,128]{2,1,0:T(8,128)S(1)} %get-tuple-element.69), channel_id=1, source_target_pairs={{4,8},{8,4},{5,9},{9,5},{6,10},{10,6},{7,11},{11,7},{20,24},{24,20... | collective-permute-start | bytes 393224 | tf_op jit(solution)/shard_map/ppermute | solution.py:343
  32.5 25.1 %copy-start = (f32[8,16,32,128]{3,2,1,0:T(8,128)}, f32[8,16,32,128]{3,2,1,0:T(8,128)S(1)}, u32[]{:S(2)}) copy-start(f32[8,16,32,128]{3,2,1,0:T(8,128)S(1)} %get-tuple-element.53.c) | copy-start | bytes 6291460
  34.2 19.7 %collective-permute-start.5 = (f32[16,32,128]{2,1,0:T(8,128)S(1)}, f32[16,32,128]{2,1,0:T(8,128)S(1)}, u32[]{:S(2)}, u32[]{:S(2)}) collective-permute-start(f32[16,32,128]{2,1,0:T(8,128)S(1)} %get-tuple-element.60), channel_id=1, source_target_pairs={{0,16},{16,0},{32,48},{48,32},{64,80},{80,64},{96,112},{112,96},{1... | collective-permute-start | bytes 786440 | tf_op jit(solution)/shard_map/ppermute | solution.py:343
  34.8 15.1 %collective-permute-start.7 = (f32[8,32,128]{2,1,0:T(8,128)S(1)}, f32[8,32,128]{2,1,0:T(8,128)S(1)}, u32[]{:S(2)}, u32[]{:S(2)}) collective-permute-start(f32[8,32,128]{2,1,0:T(8,128)S(1)} %get-tuple-element.62), channel_id=1, source_target_pairs={{0,4},{4,0},{8,12},{12,8},{1,5},{5,1},{9,13},{13,9},{2,6},{6,2},{1... | collective-permute-start | bytes 393224 | tf_op jit(solution)/shard_map/ppermute | solution.py:343
  41.2 8.6 %collective-permute-start.13 = (f32[8,16,128]{2,1,0:T(8,128)S(1)}, f32[8,16,128]{2,1,0:T(8,128)S(1)}, u32[]{:S(2)}, u32[]{:S(2)}) collective-permute-start(f32[8,16,128]{2,1,0:T(8,128)S(1)} %get-tuple-element.71), channel_id=1, source_target_pairs={{0,2},{2,0},{1,3},{3,1},{4,6},{6,4},{5,7},{7,5},{8,10},{10,8},{9,1... | collective-permute-start | bytes 196616 | tf_op jit(solution)/shard_map/ppermute | solution.py:343
  42.7 14.9 %collective-permute-start.6 = (f32[16,32,128]{2,1,0:T(8,128)S(1)}, f32[16,32,128]{2,1,0:T(8,128)S(1)}, u32[]{:S(2)}, u32[]{:S(2)}) collective-permute-start(f32[16,32,128]{2,1,0:T(8,128)S(1)} %get-tuple-element.61), channel_id=1, source_target_pairs={{16,32},{32,16},{48,64},{64,48},{80,96},{96,80},{112,128},{128,112... | collective-permute-start | bytes 786440 | tf_op jit(solution)/shard_map/ppermute | solution.py:343
  43.4 10.4 %collective-permute-start.8 = (f32[8,32,128]{2,1,0:T(8,128)S(1)}, f32[8,32,128]{2,1,0:T(8,128)S(1)}, u32[]{:S(2)}, u32[]{:S(2)}) collective-permute-start(f32[8,32,128]{2,1,0:T(8,128)S(1)} %get-tuple-element.63), channel_id=1, source_target_pairs={{4,8},{8,4},{5,9},{9,5},{6,10},{10,6},{7,11},{11,7},{20,24},{24,20... | collective-permute-start | bytes 393224 | tf_op jit(solution)/shard_map/ppermute | solution.py:343
  49.8 16.0 %collective-permute-start.14 = (f32[16,32,128]{2,1,0:T(8,128)S(1)}, f32[16,32,128]{2,1,0:T(8,128)S(1)}, u32[]{:S(2)}, u32[]{:S(2)}) collective-permute-start(f32[16,32,128]{2,1,0:T(8,128)S(1)} %get-tuple-element.75), channel_id=1, source_target_pairs={{0,16},{16,0},{32,48},{48,32},{64,80},{80,64},{96,112},{112,96},{1... | collective-permute-start | bytes 786440 | tf_op jit(solution)/shard_map/ppermute | solution.py:343
  49.8 16.0 %collective-permute-start.15 = (f32[16,32,128]{2,1,0:T(8,128)S(1)}, f32[16,32,128]{2,1,0:T(8,128)S(1)}, u32[]{:S(2)}, u32[]{:S(2)}) collective-permute-start(f32[16,32,128]{2,1,0:T(8,128)S(1)} %get-tuple-element.76), channel_id=1, source_target_pairs={{16,32},{32,16},{48,64},{64,48},{80,96},{96,80},{112,128},{128,112... | collective-permute-start | bytes 786440 | tf_op jit(solution)/shard_map/ppermute | solution.py:343
  53.8 7.0 %collective-permute-start.16 = (f32[8,32,128]{2,1,0:T(8,128)S(1)}, f32[8,32,128]{2,1,0:T(8,128)S(1)}, u32[]{:S(2)}, u32[]{:S(2)}) collective-permute-start(f32[8,32,128]{2,1,0:T(8,128)S(1)} %get-tuple-element.77), channel_id=1, source_target_pairs={{0,4},{4,0},{8,12},{12,8},{1,5},{5,1},{9,13},{13,9},{2,6},{6,2},{1... | collective-permute-start | bytes 393224 | tf_op jit(solution)/shard_map/ppermute | solution.py:343
  53.8 12.0 %collective-permute-start.17 = (f32[8,32,128]{2,1,0:T(8,128)S(1)}, f32[8,32,128]{2,1,0:T(8,128)S(1)}, u32[]{:S(2)}, u32[]{:S(2)}) collective-permute-start(f32[8,32,128]{2,1,0:T(8,128)S(1)} %get-tuple-element.78), channel_id=1, source_target_pairs={{4,8},{8,4},{5,9},{9,5},{6,10},{10,6},{7,11},{11,7},{20,24},{24,20... | collective-permute-start | bytes 393224 | tf_op jit(solution)/shard_map/ppermute | solution.py:343
  60.4 7.5 %copy-start.4 = (f32[8,16,32,128]{3,2,1,0:T(8,128)}, f32[8,16,32,128]{3,2,1,0:T(8,128)S(1)}, u32[]{:S(2)}) copy-start(f32[8,16,32,128]{3,2,1,0:T(8,128)S(1)} %get-tuple-element.89.f) | copy-start | bytes 6291460
  60.4 24.0 %collective-permute-start.18 = (f32[8,32,128]{2,1,0:T(8,128)S(1)}, f32[8,32,128]{2,1,0:T(8,128)S(1)}, u32[]{:S(2)}, u32[]{:S(2)}) collective-permute-start(f32[8,32,128]{2,1,0:T(8,128)S(1)} %get-tuple-element.82), channel_id=1, source_target_pairs={{0,4},{4,0},{8,12},{12,8},{1,5},{5,1},{9,13},{13,9},{2,6},{6,2},{1... | collective-permute-start | bytes 393224 | tf_op jit(solution)/shard_map/ppermute | solution.py:343
  60.9 23.6 %collective-permute-start.19 = (f32[8,32,128]{2,1,0:T(8,128)S(1)}, f32[8,32,128]{2,1,0:T(8,128)S(1)}, u32[]{:S(2)}, u32[]{:S(2)}) collective-permute-start(f32[8,32,128]{2,1,0:T(8,128)S(1)} %get-tuple-element.83), channel_id=1, source_target_pairs={{4,8},{8,4},{5,9},{9,5},{6,10},{10,6},{7,11},{11,7},{20,24},{24,20... | collective-permute-start | bytes 393224 | tf_op jit(solution)/shard_map/ppermute | solution.py:343
  67.9 1.3 copy-start.6
  69.3 0.7 copy-start.8
  70.0 0.7 copy-start.9
  70.7 13.8 %collective-permute-start.20 = (f32[8,32,128]{2,1,0:T(8,128)S(1)}, f32[8,32,128]{2,1,0:T(8,128)S(1)}, u32[]{:S(2)}, u32[]{:S(2)}) collective-permute-start(f32[8,32,128]{2,1,0:T(8,128)S(1)} %get-tuple-element.84), channel_id=1, source_target_pairs={{0,4},{4,0},{8,12},{12,8},{1,5},{5,1},{9,13},{13,9},{2,6},{6,2},{1... | collective-permute-start | bytes 393224 | tf_op jit(solution)/shard_map/ppermute | solution.py:343
  70.7 16.1 %collective-permute-start.21 = (f32[8,32,128]{2,1,0:T(8,128)S(1)}, f32[8,32,128]{2,1,0:T(8,128)S(1)}, u32[]{:S(2)}, u32[]{:S(2)}) collective-permute-start(f32[8,32,128]{2,1,0:T(8,128)S(1)} %get-tuple-element.85), channel_id=1, source_target_pairs={{4,8},{8,4},{5,9},{9,5},{6,10},{10,6},{7,11},{11,7},{20,24},{24,20... | collective-permute-start | bytes 393224 | tf_op jit(solution)/shard_map/ppermute | solution.py:343
  74.9 9.6 %collective-permute-start.22 = (f32[8,16,128]{2,1,0:T(8,128)S(1)}, f32[8,16,128]{2,1,0:T(8,128)S(1)}, u32[]{:S(2)}, u32[]{:S(2)}) collective-permute-start(f32[8,16,128]{2,1,0:T(8,128)S(1)} %get-tuple-element.86), channel_id=1, source_target_pairs={{0,2},{2,0},{1,3},{3,1},{4,6},{6,4},{5,7},{7,5},{8,10},{10,8},{9,1... | collective-permute-start | bytes 196616 | tf_op jit(solution)/shard_map/ppermute | solution.py:343
  88.3 22.4 %all-to-all-start = ((f32[16,64,128]{2,1,0:T(8,128)}), f32[16,64,128]{2,1,0:T(8,128)S(1)}, u32[]{:S(2)}, u32[]{:S(2)}) async-start(f32[16,64,128]{2,1,0:T(8,128)} %shard_map.48), calls=%async_computation | async-start | bytes 1048576 | tf_op jit(solution)/shard_map/all_to_all | solution.py:385
  99.8 10.9 %collective-permute-start.23 = (f32[16,32,128]{2,1,0:T(8,128)}, f32[16,32,128]{2,1,0:T(8,128)}, u32[]{:S(2)}, u32[]{:S(2)}) collective-permute-start(f32[16,32,128]{2,1,0:T(8,128)} %get-tuple-element.90), channel_id=1, source_target_pairs={{0,16},{16,0},{32,48},{48,32},{64,80},{80,64},{96,112},{112,96},{1... | collective-permute-start | bytes 786440 | tf_op jit(solution)/shard_map/ppermute | solution.py:343
  100.2 10.5 %collective-permute-start.24 = (f32[16,32,128]{2,1,0:T(8,128)}, f32[16,32,128]{2,1,0:T(8,128)}, u32[]{:S(2)}, u32[]{:S(2)}) collective-permute-start(f32[16,32,128]{2,1,0:T(8,128)} %get-tuple-element.91), channel_id=1, source_target_pairs={{16,32},{32,16},{48,64},{64,48},{80,96},{96,80},{112,128},{128,112... | collective-permute-start | bytes 786440 | tf_op jit(solution)/shard_map/ppermute | solution.py:343
  101.6 14.5 %collective-permute-start.25 = (f32[16,32,128]{2,1,0:T(8,128)}, f32[16,32,128]{2,1,0:T(8,128)S(1)}, u32[]{:S(2)}, u32[]{:S(2)}) collective-permute-start(f32[16,32,128]{2,1,0:T(8,128)} %copy-done.9), channel_id=1, source_target_pairs={{0,16},{16,0},{32,48},{48,32},{64,80},{80,64},{96,112},{112,96},{1... | collective-permute-start | bytes 786440 | tf_op jit(solution)/shard_map/ppermute | solution.py:343
  104.0 12.2 %collective-permute-start.26 = (f32[16,32,128]{2,1,0:T(8,128)}, f32[16,32,128]{2,1,0:T(8,128)}, u32[]{:S(2)}, u32[]{:S(2)}) collective-permute-start(f32[16,32,128]{2,1,0:T(8,128)} %copy-done.8), channel_id=1, source_target_pairs={{16,32},{32,16},{48,64},{64,48},{80,96},{96,80},{112,128},{128,112... | collective-permute-start | bytes 786440 | tf_op jit(solution)/shard_map/ppermute | solution.py:343
  110.7 1.6 %copy-start.1 = (f32[8,16,32,128]{3,2,1,0:T(8,128)S(1)}, f32[8,16,32,128]{3,2,1,0:T(8,128)}, u32[]{:S(2)}) copy-start(f32[8,16,32,128]{3,2,1,0:T(8,128)} %copy-done) | copy-start | bytes 6291460
  112.3 1.6 %copy-start.5 = (f32[8,16,32,128]{3,2,1,0:T(8,128)S(1)}, f32[8,16,32,128]{3,2,1,0:T(8,128)}, u32[]{:S(2)}) copy-start(f32[8,16,32,128]{3,2,1,0:T(8,128)} %copy-done.4) | copy-start | bytes 6291460
  113.9 2.3 %copy-start.7 = (f32[8,16,32,128]{3,2,1,0:T(8,128)S(1)}, f32[8,16,32,128]{3,2,1,0:T(8,128)}, u32[]{:S(2)}) copy-start(f32[8,16,32,128]{3,2,1,0:T(8,128)} %copy-done.6) | copy-start | bytes 6291460

commit v6 on v5

--- a/solution.py
+++ b/solution.py
@@ -223,6 +223,11 @@
         write_faces(place, out, s_c0, s_c1, s_k, earlier)
 
 
+def pack_both(f, c, fa, fb, ca, cb):
+    pack_field(f, fa, fb)
+    pack_crowding(c, ca, cb)
+
+
 def totals_body(place, g_a, s_a, g_b, s_b, c0_a, c1_a, c0_b, c1_b, ks, out, kl, kh):
     ni, nk = g_a.shape[:2]
     nj = ks.shape[0]
@@ -365,8 +370,8 @@
     halos = [None, None]
     for h in range(2):
         halos[h], across = exchange(sent[h], 0, h)
-    f = list(call(pack_field, [half, half], (field_values,)))
-    c = call(pack_crowding, [half, half], (crowding,))
+    packed = call(pack_both, [half] * 4, (field_values, crowding))
+    f, c = list(packed[:2]), packed[2:]
     scratch = [(nj, ni, nl)] * 2
     sums, fix, other = [None, None], [None, None], None
     rows = lax.axis_size("rows")

time: 142 us -> 143 us (level)
  starting transfers between devices: 61.4 us -> 58.6 us
  waiting for transfers between devices: 29.5 us -> 31.8 us
  local copies, waits for them, and re-layouts: 5.93 us -> 8.11 us
    ppermute x27, waiting for transfers between devices: 24.2 us -> 26.5 us  [exchange(): got[kind] = lax.ppermute(*sends[kind])]
    all_to_all x1, starting transfers between devices: 11.5 us -> 9.32 us  [on_device(): gathered = lax.all_to_all(total, 'rows', 0, 0, tiled=True)]
    unnamed x20, local copies, waits for them, and re-layouts: 5.93 us -> 8.11 us
    pallas_call x10 -> x9, Pallas kernels: 17.4 us -> 17.3 us  [call(): pl.pallas_call(body, out_shape=[jax.ShapeDtypeStruct(s, jnp.float32) for...]
  transfers between devices with their start and end apart: 28 -> 28, of which waited for: 7 -> 8; matrix products, arithmetic and copies ran while one was open for 0% -> 0% of each run, Pallas kernels for 10% -> 10%
where the time goes in v6:
time: 143 us; the launch traced here: 142 us
  starting transfers between devices  58.6 us (41%)
  waiting for transfers between devices  31.8 us (22%)
  Pallas kernels  23.8 us (17%)
  blocking collectives  19.1 us (13%)
  local copies, waits for them, and re-layouts  8.11 us (6%)
    ppermute x27, starting transfers between devices, exchange(): got[kind] = lax.ppermute(*sends[kind])  49.3 us
    ppermute x27, waiting for transfers between devices, exchange(): got[kind] = lax.ppermute(*sends[kind])  26.5 us
    all_to_all x1, blocking collectives, on_device(): base = lax.all_to_all(before, 'rows', 0, 0, tiled=True).reshape(ni, nk, nl)  19.1 us
    pallas_call x9, Pallas kernels, call(): pl.pallas_call(body, out_shape=[jax.ShapeDtypeStruct(s, jnp.float32) for...  17.3 us
    all_to_all x1, starting transfers between devices, on_device(): gathered = lax.all_to_all(total, 'rows', 0, 0, tiled=True)  9.32 us
    unnamed x20, local copies, waits for them, and re-layouts  8.11 us
    all_to_all x1, waiting for transfers between devices, on_device(): gathered = lax.all_to_all(total, 'rows', 0, 0, tiled=True)  5.31 us
    pallas_call x1, Pallas kernels, on_device(): pl.pallas_call(functools.partial(finish_body, 1.0 / (nj * rows)), out_sha...  3.58 us
  transfers between devices with their start and end apart: 28, of which 8 were waited for; matrix products, arithmetic and copies ran while one was open for 0% of the time, Pallas kernels for 10%

profile of v6, /device:TPU:4, one launch (start us, length us, event | category | flops | bytes accessed | tf_op | source)
XLA Modules:
  0.0 142.5 jit_solution(18182457854569204693)
XLA Ops:
  0.6 0.1 pad_add_fusion.place
  0.7 2.9 %shard_map.42 = (f32[16,32,128]{2,1,0:T(8,128)S(1)}, f32[16,32,128]{2,1,0:T(8,128)S(1)}, f32[8,32,128]{2,1,0:T(8,128)S(1)}, f32[8,32,128]{2,1,0:T(8,128)S(1)}, f...) custom-call(s32[4]{0:T(128)S(1)} %pad_add_fusion.place, ...), custom_call_target="tpu_custom_call" | custom-call | tf_op jit(solution)/shard_map/pallas_call | solution.py:359
  3.7 0.1 collective-permute-start
  3.8 2.3 %collective-permute-start.2 = (f32[8,32,128]{2,1,0:T(8,128)S(1)}, f32[8,32,128]{2,1,0:T(8,128)S(1)}, u32[]{:S(2)}, u32[]{:S(2)}) collective-permute-start(f32[8,32,128]{2,1,0:T(8,128)S(1)} %get-tuple-element.56), channel_id=1, source_target_pairs={{0,4},{4,0},{8,12},{12,8},{1,5},{5,1},{9,13},{13,9},{2,6},{6,2},{1... | collective-permute-start | bytes 393224 | tf_op jit(solution)/shard_map/ppermute | solution.py:348
  6.1 5.5 %collective-permute-start.4 = (f32[8,16,128]{2,1,0:T(8,128)S(1)}, f32[8,16,128]{2,1,0:T(8,128)S(1)}, u32[]{:S(2)}, u32[]{:S(2)}) collective-permute-start(f32[8,16,128]{2,1,0:T(8,128)S(1)} %get-tuple-element.58), channel_id=1, source_target_pairs={{0,2},{2,0},{1,3},{3,1},{4,6},{6,4},{5,7},{7,5},{8,10},{10,8},{9,1... | collective-permute-start | bytes 196616 | tf_op jit(solution)/shard_map/ppermute | solution.py:348
  11.5 0.7 collective-permute-start.1
  12.2 5.8 %collective-permute-start.3 = (f32[8,32,128]{2,1,0:T(8,128)S(1)}, f32[8,32,128]{2,1,0:T(8,128)S(1)}, u32[]{:S(2)}, u32[]{:S(2)}) collective-permute-start(f32[8,32,128]{2,1,0:T(8,128)S(1)} %get-tuple-element.57), channel_id=1, source_target_pairs={{4,8},{8,4},{5,9},{9,5},{6,10},{10,6},{7,11},{11,7},{20,24},{24,20... | collective-permute-start | bytes 393224 | tf_op jit(solution)/shard_map/ppermute | solution.py:348
  18.1 0.0 collective-permute-done.4.ks
  18.1 1.7 %collective-permute-start.9 = (f32[16,32,128]{2,1,0:T(8,128)S(1)}, f32[16,32,128]{2,1,0:T(8,128)S(1)}, u32[]{:S(2)}, u32[]{:S(2)}) collective-permute-start(f32[16,32,128]{2,1,0:T(8,128)S(1)} %get-tuple-element.66), channel_id=1, source_target_pairs={{0,16},{16,0},{32,48},{48,32},{64,80},{80,64},{96,112},{112,96},{1... | collective-permute-start | bytes 786440 | tf_op jit(solution)/shard_map/ppermute | solution.py:348
  19.8 0.0 collective-permute-done.2.c0
  19.8 0.7 collective-permute-start.10
  20.5 5.1 %collective-permute-done.3.c1 = f32[8,32,128]{2,1,0:T(8,128)S(1)} collective-permute-done((f32[8,32,128]{2,1,0:T(8,128)S(1)}, f32[8,32,128]{2,1,0:T(8,128)S(1)}, u32[]{:S(2)}, u32[]{:S(2)}) %collective-permute-start.3) | collective-permute-done | bytes 131104 | tf_op jit(solution)/shard_map/ppermute | solution.py:348
  25.6 3.2 %collective-permute-start.12 = (f32[8,32,128]{2,1,0:T(8,128)S(1)}, f32[8,32,128]{2,1,0:T(8,128)S(1)}, u32[]{:S(2)}, u32[]{:S(2)}) collective-permute-start(f32[8,32,128]{2,1,0:T(8,128)S(1)} %get-tuple-element.69), channel_id=1, source_target_pairs={{4,8},{8,4},{5,9},{9,5},{6,10},{10,6},{7,11},{11,7},{20,24},{24,20... | collective-permute-start | bytes 393224 | tf_op jit(solution)/shard_map/ppermute | solution.py:348
  28.9 0.0 copy-start.3
  28.9 2.2 %copy-done.3 = f32[8,16,64,128]{3,2,1,0:T(8,128)S(1)} copy-done((f32[8,16,64,128]{3,2,1,0:T(8,128)S(1)}, f32[8,16,64,128]{3,2,1,0:T(8,128)}, u32[]{:S(2)}) %copy-start.3) | copy-done | bytes 4194328
  31.1 3.3 %shard_map.41 = (f32[8,16,32,128]{3,2,1,0:T(8,128)S(1)}, f32[8,16,32,128]{3,2,1,0:T(8,128)S(1)}, f32[8,16,32,128]{3,2,1,0:T(8,128)S(1)}, f32[8,16,32,128]{3,2,1,0:T(8,128)S(1)}) custom-call(f32[8,16,64,128]{3,2,1,0:T(8,128)S(1)} %copy-done.2, f32[8,16,64,128]{3,2,1,0:T(8,128)S(1)} %copy-done.3), custom_call_target="tpu_custom_call" | custom-call | tf_op jit(solution)/shard_map/pallas_call | solution.py:24
  34.4 0.0 copy-start
  34.4 1.6 %shard_map.43 = (f32[8,16,32,128]{3,2,1,0:T(8,128)S(1)}, f32[16,32,128]{2,1,0:T(8,128)S(1)}, f32[16,32,128]{2,1,0:T(8,128)S(1)}, f32[8,32,128]{2,1,0:T(8,128)S(1...) custom-call(s32[4]{0:T(128)S(1)} %pad_add_fusion.place, f32[8,16,32,128]{3,2,1,0:T(8,128)S(1)} %get-tuple-element.52.f, ...), custom_call_target="tpu_custom_call" | custom-call | tf_op jit(solution)/shard_map/pallas_call | solution.py:24
  36.0 0.6 collective-permute-start.5
  36.6 1.1 collective-permute-start.7
  37.7 1.5 %collective-permute-done.12.c1 = f32[8,32,128]{2,1,0:T(8,128)S(1)} collective-permute-done((f32[8,32,128]{2,1,0:T(8,128)S(1)}, f32[8,32,128]{2,1,0:T(8,128)S(1)}, u32[]{:S(2)}, u32[]{:S(2)}) %collective-permute-start.12) | collective-permute-done | bytes 131104 | tf_op jit(solution)/shard_map/ppermute | solution.py:348
  39.2 0.0 collective-permute-done.9.r0
  39.2 0.0 collective-permute-done.10.r1
  39.2 1.7 %shard_map.44 = (f32[8,16,32,128]{3,2,1,0:T(8,128)S(1)}, f32[16,32,128]{2,1,0:T(8,128)S(1)}, f32[16,32,128]{2,1,0:T(8,128)S(1)}, f32[8,32,128]{2,1,0:T(8,128)S(1...) custom-call(s32[4]{0:T(128)S(1)} %pad_add_fusion.place, f32[8,16,32,128]{3,2,1,0:T(8,128)S(1)} %get-tuple-element.64.f, ...), custom_call_target="tpu_custom_call" | custom-call | tf_op jit(solution)/shard_map/pallas_call | solution.py:24
  40.9 1.5 %collective-permute-start.13 = (f32[8,16,128]{2,1,0:T(8,128)S(1)}, f32[8,16,128]{2,1,0:T(8,128)S(1)}, u32[]{:S(2)}, u32[]{:S(2)}) collective-permute-start(f32[8,16,128]{2,1,0:T(8,128)S(1)} %get-tuple-element.71), channel_id=1, source_target_pairs={{0,2},{2,0},{1,3},{3,1},{4,6},{6,4},{5,7},{7,5},{8,10},{10,8},{9,1... | collective-permute-start | bytes 196616 | tf_op jit(solution)/shard_map/ppermute | solution.py:348
  42.4 0.7 collective-permute-start.6
  43.1 4.0 %collective-permute-start.8 = (f32[8,32,128]{2,1,0:T(8,128)S(1)}, f32[8,32,128]{2,1,0:T(8,128)S(1)}, u32[]{:S(2)}, u32[]{:S(2)}) collective-permute-start(f32[8,32,128]{2,1,0:T(8,128)S(1)} %get-tuple-element.63), channel_id=1, source_target_pairs={{4,8},{8,4},{5,9},{9,5},{6,10},{10,6},{7,11},{11,7},{20,24},{24,20... | collective-permute-start | bytes 393224 | tf_op jit(solution)/shard_map/ppermute | solution.py:348
  47.1 2.0 %collective-permute-done.13.ks = f32[8,16,128]{2,1,0:T(8,128)S(1)} collective-permute-done((f32[8,16,128]{2,1,0:T(8,128)S(1)}, f32[8,16,128]{2,1,0:T(8,128)S(1)}, u32[]{:S(2)}, u32[]{:S(2)}) %collective-permute-start.13) | collective-permute-done | bytes 65568 | tf_op jit(solution)/shard_map/ppermute | solution.py:348
  49.1 0.6 collective-permute-start.14
  49.7 0.0 collective-permute-done.7.c0
  49.8 0.7 collective-permute-start.15
  50.4 5.6 %collective-permute-done.8.c1 = f32[8,32,128]{2,1,0:T(8,128)S(1)} collective-permute-done((f32[8,32,128]{2,1,0:T(8,128)S(1)}, f32[8,32,128]{2,1,0:T(8,128)S(1)}, u32[]{:S(2)}, u32[]{:S(2)}) %collective-permute-start.8) | collective-permute-done | bytes 131104 | tf_op jit(solution)/shard_map/ppermute | solution.py:348
  56.1 0.0 collective-permute-start.16
  56.1 0.0 collective-permute-done.5.r0
  56.1 2.2 %collective-permute-start.17 = (f32[8,32,128]{2,1,0:T(8,128)S(1)}, f32[8,32,128]{2,1,0:T(8,128)S(1)}, u32[]{:S(2)}, u32[]{:S(2)}) collective-permute-start(f32[8,32,128]{2,1,0:T(8,128)S(1)} %get-tuple-element.78), channel_id=1, source_target_pairs={{4,8},{8,4},{5,9},{9,5},{6,10},{10,6},{7,11},{11,7},{20,24},{24,20... | collective-permute-start | bytes 393224 | tf_op jit(solution)/shard_map/ppermute | solution.py:348
  58.3 0.0 collective-permute-done.6.r1
  58.3 2.8 %shard_map.45 = (f32[8,16,32,128]{3,2,1,0:T(8,128)S(1)}, f32[16,32,128]{2,1,0:T(8,128)}, f32[16,32,128]{2,1,0:T(8,128)}, f32[8,32,128]{2,1,0:T(8,128)S(1)}, f32[...) custom-call(s32[4]{0:T(128)S(1)} %pad_add_fusion.place, ...), custom_call_target="tpu_custom_call" | custom-call | tf_op jit(solution)/shard_map/pallas_call | solution.py:24
  61.1 2.0 %collective-permute-start.18 = (f32[8,32,128]{2,1,0:T(8,128)S(1)}, f32[8,32,128]{2,1,0:T(8,128)S(1)}, u32[]{:S(2)}, u32[]{:S(2)}) collective-permute-start(f32[8,32,128]{2,1,0:T(8,128)S(1)} %get-tuple-element.82), channel_id=1, source_target_pairs={{0,4},{4,0},{8,12},{12,8},{1,5},{5,1},{9,13},{13,9},{2,6},{6,2},{1... | collective-permute-start | bytes 393224 | tf_op jit(solution)/shard_map/ppermute | solution.py:348
  63.1 5.0 %collective-permute-start.19 = (f32[8,32,128]{2,1,0:T(8,128)S(1)}, f32[8,32,128]{2,1,0:T(8,128)S(1)}, u32[]{:S(2)}, u32[]{:S(2)}) collective-permute-start(f32[8,32,128]{2,1,0:T(8,128)S(1)} %get-tuple-element.83), channel_id=1, source_target_pairs={{4,8},{8,4},{5,9},{9,5},{6,10},{10,6},{7,11},{11,7},{20,24},{24,20... | collective-permute-start | bytes 393224 | tf_op jit(solution)/shard_map/ppermute | solution.py:348
  68.1 2.0 %collective-permute-done.17.c1 = f32[8,32,128]{2,1,0:T(8,128)S(1)} collective-permute-done((f32[8,32,128]{2,1,0:T(8,128)S(1)}, f32[8,32,128]{2,1,0:T(8,128)S(1)}, u32[]{:S(2)}, u32[]{:S(2)}) %collective-permute-start.17) | collective-permute-done | bytes 131104 | tf_op jit(solution)/shard_map/ppermute | solution.py:348
  70.1 0.0 collective-permute-done.14.r0
  70.1 0.0 collective-permute-done.15.r1
  70.1 2.1 %shard_map.46 = (f32[8,16,32,128]{3,2,1,0:T(8,128)S(1)}, f32[16,32,128]{2,1,0:T(8,128)S(1)}, f32[16,32,128]{2,1,0:T(8,128)S(1)}, f32[8,32,128]{2,1,0:T(8,128)S(1...) custom-call(s32[4]{0:T(128)S(1)} %pad_add_fusion.place, ...), custom_call_target="tpu_custom_call" | custom-call | tf_op jit(solution)/shard_map/pallas_call | solution.py:24
  72.2 1.3 copy-done.6
  73.5 0.7 copy-done.8
  74.2 0.7 copy-done.9
  74.9 2.2 %collective-permute-start.21 = (f32[8,32,128]{2,1,0:T(8,128)S(1)}, f32[8,32,128]{2,1,0:T(8,128)S(1)}, u32[]{:S(2)}, u32[]{:S(2)}) collective-permute-start(f32[8,32,128]{2,1,0:T(8,128)S(1)} %get-tuple-element.85), channel_id=1, source_target_pairs={{4,8},{8,4},{5,9},{9,5},{6,10},{10,6},{7,11},{11,7},{20,24},{24,20... | collective-permute-start | bytes 393224 | tf_op jit(solution)/shard_map/ppermute | solution.py:348
  77.1 3.2 %collective-permute-start.22 = (f32[8,16,128]{2,1,0:T(8,128)S(1)}, f32[8,16,128]{2,1,0:T(8,128)S(1)}, u32[]{:S(2)}, u32[]{:S(2)}) collective-permute-start(f32[8,16,128]{2,1,0:T(8,128)S(1)} %get-tuple-element.86), channel_id=1, source_target_pairs={{0,2},{2,0},{1,3},{3,1},{4,6},{6,4},{5,7},{7,5},{8,10},{10,8},{9,1... | collective-permute-start | bytes 196616 | tf_op jit(solution)/shard_map/ppermute | solution.py:348
  80.3 6.8 %collective-permute-done.22.ks = f32[8,16,128]{2,1,0:T(8,128)S(1)} collective-permute-done((f32[8,16,128]{2,1,0:T(8,128)S(1)}, f32[8,16,128]{2,1,0:T(8,128)S(1)}, u32[]{:S(2)}, u32[]{:S(2)}) %collective-permute-start.22) | collective-permute-done | bytes 65568 | tf_op jit(solution)/shard_map/ppermute | solution.py:348
  87.1 3.4 %collective-permute-done.21.c1_b.c1 = f32[8,32,128]{2,1,0:T(8,128)S(1)} collective-permute-done((f32[8,32,128]{2,1,0:T(8,128)S(1)}, f32[8,32,128]{2,1,0:T(8,128)S(1)}, u32[]{:S(2)}, u32[]{:S(2)}) %collective-permute-start.21) | collective-permute-done | bytes 131104 | tf_op jit(solution)/shard_map/ppermute | solution.py:348
  90.5 1.6 %shard_map.47 = f32[16,64,128]{2,1,0:T(8,128)} custom-call(s32[4]{0:T(128)S(1)} %pad_add_fusion.place, f32[16,32,128]{2,1,0:T(8,128)S(1)} %get-tuple-element.72.g_a, f32[16,32,128]{2,1,0:T(8,128)S(1)} %get-tuple-element.73.s_a, f32[16,32,128]{2,1,0:T(8,128)S(1)} %get-tuple-element.80.g_b, f32[16,32,128]{2,1,0:T(8,128)S(1)} %get-tuple-element.81.s_b, ...), custom_call_target="tpu_custom_call" | custom-call | tf_op jit(solution)/shard_map/pallas_call | solution.py:24
  92.1 9.3 %all-to-all-start = ((f32[16,64,128]{2,1,0:T(8,128)}), f32[16,64,128]{2,1,0:T(8,128)S(1)}, u32[]{:S(2)}, u32[]{:S(2)}) async-start(f32[16,64,128]{2,1,0:T(8,128)} %shard_map.47), calls=%async_computation | async-start | bytes 1048576 | tf_op jit(solution)/shard_map/all_to_all | solution.py:390
  101.4 0.4 collective-permute-start.23
  101.8 1.4 collective-permute-start.24
  103.2 2.4 %collective-permute-start.25 = (f32[16,32,128]{2,1,0:T(8,128)}, f32[16,32,128]{2,1,0:T(8,128)S(1)}, u32[]{:S(2)}, u32[]{:S(2)}) collective-permute-start(f32[16,32,128]{2,1,0:T(8,128)} %copy-done.9), channel_id=1, source_target_pairs={{0,16},{16,0},{32,48},{48,32},{64,80},{80,64},{96,112},{112,96},{1... | collective-permute-start | bytes 786440 | tf_op jit(solution)/shard_map/ppermute | solution.py:348
  105.5 1.4 collective-permute-start.26
  106.9 5.3 %all-to-all-done.g = f32[16,64,128]{2,1,0:T(8,128)S(1)} async-done(((f32[16,64,128]{2,1,0:T(8,128)}), f32[16,64,128]{2,1,0:T(8,128)S(1)}, u32[]{:S(2)}, u32[]{:S(2)}) %all-to-all-start) | async-done | bytes 524320 | tf_op jit(solution)/shard_map/all_to_all | solution.py:390
  112.3 0.0 copy-start.1
  112.3 1.6 %copy-done.1 = f32[8,16,32,128]{3,2,1,0:T(8,128)S(1)} copy-done((f32[8,16,32,128]{3,2,1,0:T(8,128)S(1)}, f32[8,16,32,128]{3,2,1,0:T(8,128)}, u32[]{:S(2)}) %copy-start.1) | copy-done | bytes 2097176
  113.9 1.6 %copy-done.5 = f32[8,16,32,128]{3,2,1,0:T(8,128)S(1)} copy-done((f32[8,16,32,128]{3,2,1,0:T(8,128)S(1)}, f32[8,16,32,128]{3,2,1,0:T(8,128)}, u32[]{:S(2)}) %copy-start.5) | copy-done | bytes 2097176
  115.5 2.2 %shard_map.49 = (f32[8,16,32,128]{3,2,1,0:T(8,128)S(1)}, f32[16,32,128]{2,1,0:T(8,128)S(1)}) custom-call(s32[4]{0:T(128)S(1)} %pad_add_fusion.place, f32[8,16,32,128]{3,2,1,0:T(8,128)S(1)} %copy-done.5, f32[8,16,32,128]{3,2,1,0:T(8,128)S(1)} %copy-done.1, f32[16,32,128]{2,1,0:T(8,128)} %collective-permute-done.23.r0, ...), custom_call_target="tpu_custom_call" | custom-call | tf_op jit(solution)/shard_map/pallas_call | solution.py:24
  117.7 2.0 %shard_map.50 = (f32[8,16,32,128]{3,2,1,0:T(8,128)S(1)}, f32[16,32,128]{2,1,0:T(8,128)S(1)}) custom-call(s32[4]{0:T(128)S(1)} %pad_add_fusion.place, f32[8,16,32,128]{3,2,1,0:T(8,128)S(1)} %copy-done.7, f32[8,16,32,128]{3,2,1,0:T(8,128)S(1)} %get-tuple-element.65.c, f32[16,32,128]{2,1,0:T(8,128)S(1)} %collective-permute-done.25.r0, ...), custom_call_target="tpu_custom_call" | custom-call | tf_op jit(solution)/shard_map/pallas_call | solution.py:24
  119.7 19.1 %all_to_all.10.base = f32[16,64,128]{2,1,0:T(8,128)S(1)} all-to-all(f32[16,64,128]{2,1,0:T(8,128)S(1)} %shard_map.48), channel_id=1, replica_groups=mesh['rows'=16,'cols'=4,'slabs'=2,'trial'=2] {'rows'}, dimensions={0} | all-to-all | bytes 1048576 | tf_op jit(solution)/shard_map/all_to_all | solution.py:414
  138.9 3.6 %shard_map.51 = (f32[8,16,64,128]{3,2,1,0:T(8,128)}, f32[8,16,64,128]{3,2,1,0:T(8,128)}) custom-call(f32[8,16,32,128]{3,2,1,0:T(8,128)S(1)} %get-tuple-element.97.fa, f32[8,16,32,128]{3,2,1,0:T(8,128)S(1)} %get-tuple-element.98.fb, f32[16,64,128]{2,1,0:T(8,128)S(1)} %all_to_all.10.base, f32[16,32,128]{2,1,0:T(8,128)S(1)} %get-tuple-element.100.fix_a, ...), custom_call_target="tpu_custom_call" | custom-call | tf_op jit(solution)/shard_map/pallas_call | solution.py:415
  (25 shorter events, 0.1 us)
Async XLA Ops:
  0.7 28.1 %copy-start.2 = (f32[8,16,64,128]{3,2,1,0:T(8,128)S(1)}, f32[8,16,64,128]{3,2,1,0:T(8,128)}, u32[]{:S(2)}) copy-start(f32[8,16,64,128]{3,2,1,0:T(8,128)} %f.3) | copy-start | bytes 12582916
  3.7 22.0 %collective-permute-start = (f32[16,32,128]{2,1,0:T(8,128)S(1)}, f32[16,32,128]{2,1,0:T(8,128)S(1)}, u32[]{:S(2)}, u32[]{:S(2)}) collective-permute-start(f32[16,32,128]{2,1,0:T(8,128)S(1)} %get-tuple-element.54), channel_id=1, source_target_pairs={{0,16},{16,0},{32,48},{48,32},{64,80},{80,64},{96,112},{112,96},{1... | collective-permute-start | bytes 786440 | tf_op jit(solution)/shard_map/ppermute | solution.py:348
  3.8 16.1 %collective-permute-start.2 = (f32[8,32,128]{2,1,0:T(8,128)S(1)}, f32[8,32,128]{2,1,0:T(8,128)S(1)}, u32[]{:S(2)}, u32[]{:S(2)}) collective-permute-start(f32[8,32,128]{2,1,0:T(8,128)S(1)} %get-tuple-element.56), channel_id=1, source_target_pairs={{0,4},{4,0},{8,12},{12,8},{1,5},{5,1},{9,13},{13,9},{2,6},{6,2},{1... | collective-permute-start | bytes 393224 | tf_op jit(solution)/shard_map/ppermute | solution.py:348
  6.1 12.0 %collective-permute-start.4 = (f32[8,16,128]{2,1,0:T(8,128)S(1)}, f32[8,16,128]{2,1,0:T(8,128)S(1)}, u32[]{:S(2)}, u32[]{:S(2)}) collective-permute-start(f32[8,16,128]{2,1,0:T(8,128)S(1)} %get-tuple-element.58), channel_id=1, source_target_pairs={{0,2},{2,0},{1,3},{3,1},{4,6},{6,4},{5,7},{7,5},{8,10},{10,8},{9,1... | collective-permute-start | bytes 196616 | tf_op jit(solution)/shard_map/ppermute | solution.py:348
  11.5 22.9 %collective-permute-start.1 = (f32[16,32,128]{2,1,0:T(8,128)S(1)}, f32[16,32,128]{2,1,0:T(8,128)S(1)}, u32[]{:S(2)}, u32[]{:S(2)}) collective-permute-start(f32[16,32,128]{2,1,0:T(8,128)S(1)} %get-tuple-element.55), channel_id=1, source_target_pairs={{16,32},{32,16},{48,64},{64,48},{80,96},{96,80},{112,128},{128,112... | collective-permute-start | bytes 786440 | tf_op jit(solution)/shard_map/ppermute | solution.py:348
  12.2 13.4 %collective-permute-start.3 = (f32[8,32,128]{2,1,0:T(8,128)S(1)}, f32[8,32,128]{2,1,0:T(8,128)S(1)}, u32[]{:S(2)}, u32[]{:S(2)}) collective-permute-start(f32[8,32,128]{2,1,0:T(8,128)S(1)} %get-tuple-element.57), channel_id=1, source_target_pairs={{4,8},{8,4},{5,9},{9,5},{6,10},{10,6},{7,11},{11,7},{20,24},{24,20... | collective-permute-start | bytes 393224 | tf_op jit(solution)/shard_map/ppermute | solution.py:348
  18.1 21.1 %collective-permute-start.9 = (f32[16,32,128]{2,1,0:T(8,128)S(1)}, f32[16,32,128]{2,1,0:T(8,128)S(1)}, u32[]{:S(2)}, u32[]{:S(2)}) collective-permute-start(f32[16,32,128]{2,1,0:T(8,128)S(1)} %get-tuple-element.66), channel_id=1, source_target_pairs={{0,16},{16,0},{32,48},{48,32},{64,80},{80,64},{96,112},{112,96},{1... | collective-permute-start | bytes 786440 | tf_op jit(solution)/shard_map/ppermute | solution.py:348
  19.8 19.3 %collective-permute-start.10 = (f32[16,32,128]{2,1,0:T(8,128)S(1)}, f32[16,32,128]{2,1,0:T(8,128)S(1)}, u32[]{:S(2)}, u32[]{:S(2)}) collective-permute-start(f32[16,32,128]{2,1,0:T(8,128)S(1)} %get-tuple-element.67), channel_id=1, source_target_pairs={{16,32},{32,16},{48,64},{64,48},{80,96},{96,80},{112,128},{128,112... | collective-permute-start | bytes 786440 | tf_op jit(solution)/shard_map/ppermute | solution.py:348
  25.6 11.0 %collective-permute-start.11 = (f32[8,32,128]{2,1,0:T(8,128)S(1)}, f32[8,32,128]{2,1,0:T(8,128)S(1)}, u32[]{:S(2)}, u32[]{:S(2)}) collective-permute-start(f32[8,32,128]{2,1,0:T(8,128)S(1)} %get-tuple-element.68), channel_id=1, source_target_pairs={{0,4},{4,0},{8,12},{12,8},{1,5},{5,1},{9,13},{13,9},{2,6},{6,2},{1... | collective-permute-start | bytes 393224 | tf_op jit(solution)/shard_map/ppermute | solution.py:348
  25.6 13.5 %collective-permute-start.12 = (f32[8,32,128]{2,1,0:T(8,128)S(1)}, f32[8,32,128]{2,1,0:T(8,128)S(1)}, u32[]{:S(2)}, u32[]{:S(2)}) collective-permute-start(f32[8,32,128]{2,1,0:T(8,128)S(1)} %get-tuple-element.69), channel_id=1, source_target_pairs={{4,8},{8,4},{5,9},{9,5},{6,10},{10,6},{7,11},{11,7},{20,24},{24,20... | collective-permute-start | bytes 393224 | tf_op jit(solution)/shard_map/ppermute | solution.py:348
  28.9 2.2 %copy-start.3 = (f32[8,16,64,128]{3,2,1,0:T(8,128)S(1)}, f32[8,16,64,128]{3,2,1,0:T(8,128)}, u32[]{:S(2)}) copy-start(f32[8,16,64,128]{3,2,1,0:T(8,128)} %c.1) | copy-start | bytes 12582916
  34.4 23.9 %copy-start = (f32[8,16,32,128]{3,2,1,0:T(8,128)}, f32[8,16,32,128]{3,2,1,0:T(8,128)S(1)}, u32[]{:S(2)}) copy-start(f32[8,16,32,128]{3,2,1,0:T(8,128)S(1)} %get-tuple-element.53.c) | copy-start | bytes 6291460
  36.0 20.0 %collective-permute-start.5 = (f32[16,32,128]{2,1,0:T(8,128)S(1)}, f32[16,32,128]{2,1,0:T(8,128)S(1)}, u32[]{:S(2)}, u32[]{:S(2)}) collective-permute-start(f32[16,32,128]{2,1,0:T(8,128)S(1)} %get-tuple-element.60), channel_id=1, source_target_pairs={{0,16},{16,0},{32,48},{48,32},{64,80},{80,64},{96,112},{112,96},{1... | collective-permute-start | bytes 786440 | tf_op jit(solution)/shard_map/ppermute | solution.py:348
  36.6 13.1 %collective-permute-start.7 = (f32[8,32,128]{2,1,0:T(8,128)S(1)}, f32[8,32,128]{2,1,0:T(8,128)S(1)}, u32[]{:S(2)}, u32[]{:S(2)}) collective-permute-start(f32[8,32,128]{2,1,0:T(8,128)S(1)} %get-tuple-element.62), channel_id=1, source_target_pairs={{0,4},{4,0},{8,12},{12,8},{1,5},{5,1},{9,13},{13,9},{2,6},{6,2},{1... | collective-permute-start | bytes 393224 | tf_op jit(solution)/shard_map/ppermute | solution.py:348
  40.9 8.3 %collective-permute-start.13 = (f32[8,16,128]{2,1,0:T(8,128)S(1)}, f32[8,16,128]{2,1,0:T(8,128)S(1)}, u32[]{:S(2)}, u32[]{:S(2)}) collective-permute-start(f32[8,16,128]{2,1,0:T(8,128)S(1)} %get-tuple-element.71), channel_id=1, source_target_pairs={{0,2},{2,0},{1,3},{3,1},{4,6},{6,4},{5,7},{7,5},{8,10},{10,8},{9,1... | collective-permute-start | bytes 196616 | tf_op jit(solution)/shard_map/ppermute | solution.py:348
  42.4 15.9 %collective-permute-start.6 = (f32[16,32,128]{2,1,0:T(8,128)S(1)}, f32[16,32,128]{2,1,0:T(8,128)S(1)}, u32[]{:S(2)}, u32[]{:S(2)}) collective-permute-start(f32[16,32,128]{2,1,0:T(8,128)S(1)} %get-tuple-element.61), channel_id=1, source_target_pairs={{16,32},{32,16},{48,64},{64,48},{80,96},{96,80},{112,128},{128,112... | collective-permute-start | bytes 786440 | tf_op jit(solution)/shard_map/ppermute | solution.py:348
  43.1 13.0 %collective-permute-start.8 = (f32[8,32,128]{2,1,0:T(8,128)S(1)}, f32[8,32,128]{2,1,0:T(8,128)S(1)}, u32[]{:S(2)}, u32[]{:S(2)}) collective-permute-start(f32[8,32,128]{2,1,0:T(8,128)S(1)} %get-tuple-element.63), channel_id=1, source_target_pairs={{4,8},{8,4},{5,9},{9,5},{6,10},{10,6},{7,11},{11,7},{20,24},{24,20... | collective-permute-start | bytes 393224 | tf_op jit(solution)/shard_map/ppermute | solution.py:348
  49.1 20.9 %collective-permute-start.14 = (f32[16,32,128]{2,1,0:T(8,128)S(1)}, f32[16,32,128]{2,1,0:T(8,128)S(1)}, u32[]{:S(2)}, u32[]{:S(2)}) collective-permute-start(f32[16,32,128]{2,1,0:T(8,128)S(1)} %get-tuple-element.75), channel_id=1, source_target_pairs={{0,16},{16,0},{32,48},{48,32},{64,80},{80,64},{96,112},{112,96},{1... | collective-permute-start | bytes 786440 | tf_op jit(solution)/shard_map/ppermute | solution.py:348
  49.8 20.3 %collective-permute-start.15 = (f32[16,32,128]{2,1,0:T(8,128)S(1)}, f32[16,32,128]{2,1,0:T(8,128)S(1)}, u32[]{:S(2)}, u32[]{:S(2)}) collective-permute-start(f32[16,32,128]{2,1,0:T(8,128)S(1)} %get-tuple-element.76), channel_id=1, source_target_pairs={{16,32},{32,16},{48,64},{64,48},{80,96},{96,80},{112,128},{128,112... | collective-permute-start | bytes 786440 | tf_op jit(solution)/shard_map/ppermute | solution.py:348
  56.1 7.0 %collective-permute-start.16 = (f32[8,32,128]{2,1,0:T(8,128)S(1)}, f32[8,32,128]{2,1,0:T(8,128)S(1)}, u32[]{:S(2)}, u32[]{:S(2)}) collective-permute-start(f32[8,32,128]{2,1,0:T(8,128)S(1)} %get-tuple-element.77), channel_id=1, source_target_pairs={{0,4},{4,0},{8,12},{12,8},{1,5},{5,1},{9,13},{13,9},{2,6},{6,2},{1... | collective-permute-start | bytes 393224 | tf_op jit(solution)/shard_map/ppermute | solution.py:348
  56.1 14.0 %collective-permute-start.17 = (f32[8,32,128]{2,1,0:T(8,128)S(1)}, f32[8,32,128]{2,1,0:T(8,128)S(1)}, u32[]{:S(2)}, u32[]{:S(2)}) collective-permute-start(f32[8,32,128]{2,1,0:T(8,128)S(1)} %get-tuple-element.78), channel_id=1, source_target_pairs={{4,8},{8,4},{5,9},{9,5},{6,10},{10,6},{7,11},{11,7},{20,24},{24,20... | collective-permute-start | bytes 393224 | tf_op jit(solution)/shard_map/ppermute | solution.py:348
  61.1 11.0 %copy-start.4 = (f32[8,16,32,128]{3,2,1,0:T(8,128)}, f32[8,16,32,128]{3,2,1,0:T(8,128)S(1)}, u32[]{:S(2)}) copy-start(f32[8,16,32,128]{3,2,1,0:T(8,128)S(1)} %get-tuple-element.89.f) | copy-start | bytes 6291460
  61.1 26.0 %collective-permute-start.18 = (f32[8,32,128]{2,1,0:T(8,128)S(1)}, f32[8,32,128]{2,1,0:T(8,128)S(1)}, u32[]{:S(2)}, u32[]{:S(2)}) collective-permute-start(f32[8,32,128]{2,1,0:T(8,128)S(1)} %get-tuple-element.82), channel_id=1, source_target_pairs={{0,4},{4,0},{8,12},{12,8},{1,5},{5,1},{9,13},{13,9},{2,6},{6,2},{1... | collective-permute-start | bytes 393224 | tf_op jit(solution)/shard_map/ppermute | solution.py:348
  63.1 24.0 %collective-permute-start.19 = (f32[8,32,128]{2,1,0:T(8,128)S(1)}, f32[8,32,128]{2,1,0:T(8,128)S(1)}, u32[]{:S(2)}, u32[]{:S(2)}) collective-permute-start(f32[8,32,128]{2,1,0:T(8,128)S(1)} %get-tuple-element.83), channel_id=1, source_target_pairs={{4,8},{8,4},{5,9},{9,5},{6,10},{10,6},{7,11},{11,7},{20,24},{24,20... | collective-permute-start | bytes 393224 | tf_op jit(solution)/shard_map/ppermute | solution.py:348
  72.2 1.3 copy-start.6
  73.5 0.7 copy-start.8
  74.2 0.7 copy-start.9
  74.9 12.2 %collective-permute-start.20 = (f32[8,32,128]{2,1,0:T(8,128)S(1)}, f32[8,32,128]{2,1,0:T(8,128)S(1)}, u32[]{:S(2)}, u32[]{:S(2)}) collective-permute-start(f32[8,32,128]{2,1,0:T(8,128)S(1)} %get-tuple-element.84), channel_id=1, source_target_pairs={{0,4},{4,0},{8,12},{12,8},{1,5},{5,1},{9,13},{13,9},{2,6},{6,2},{1... | collective-permute-start | bytes 393224 | tf_op jit(solution)/shard_map/ppermute | solution.py:348
  74.9 15.6 %collective-permute-start.21 = (f32[8,32,128]{2,1,0:T(8,128)S(1)}, f32[8,32,128]{2,1,0:T(8,128)S(1)}, u32[]{:S(2)}, u32[]{:S(2)}) collective-permute-start(f32[8,32,128]{2,1,0:T(8,128)S(1)} %get-tuple-element.85), channel_id=1, source_target_pairs={{4,8},{8,4},{5,9},{9,5},{6,10},{10,6},{7,11},{11,7},{20,24},{24,20... | collective-permute-start | bytes 393224 | tf_op jit(solution)/shard_map/ppermute | solution.py:348
  77.1 10.0 %collective-permute-start.22 = (f32[8,16,128]{2,1,0:T(8,128)S(1)}, f32[8,16,128]{2,1,0:T(8,128)S(1)}, u32[]{:S(2)}, u32[]{:S(2)}) collective-permute-start(f32[8,16,128]{2,1,0:T(8,128)S(1)} %get-tuple-element.86), channel_id=1, source_target_pairs={{0,2},{2,0},{1,3},{3,1},{4,6},{6,4},{5,7},{7,5},{8,10},{10,8},{9,1... | collective-permute-start | bytes 196616 | tf_op jit(solution)/shard_map/ppermute | solution.py:348
  92.1 20.2 %all-to-all-start = ((f32[16,64,128]{2,1,0:T(8,128)}), f32[16,64,128]{2,1,0:T(8,128)S(1)}, u32[]{:S(2)}, u32[]{:S(2)}) async-start(f32[16,64,128]{2,1,0:T(8,128)} %shard_map.47), calls=%async_computation | async-start | bytes 1048576 | tf_op jit(solution)/shard_map/all_to_all | solution.py:390
  101.4 10.9 %collective-permute-start.23 = (f32[16,32,128]{2,1,0:T(8,128)}, f32[16,32,128]{2,1,0:T(8,128)}, u32[]{:S(2)}, u32[]{:S(2)}) collective-permute-start(f32[16,32,128]{2,1,0:T(8,128)} %get-tuple-element.90), channel_id=1, source_target_pairs={{0,16},{16,0},{32,48},{48,32},{64,80},{80,64},{96,112},{112,96},{1... | collective-permute-start | bytes 786440 | tf_op jit(solution)/shard_map/ppermute | solution.py:348
  101.8 10.5 %collective-permute-start.24 = (f32[16,32,128]{2,1,0:T(8,128)}, f32[16,32,128]{2,1,0:T(8,128)}, u32[]{:S(2)}, u32[]{:S(2)}) collective-permute-start(f32[16,32,128]{2,1,0:T(8,128)} %get-tuple-element.91), channel_id=1, source_target_pairs={{16,32},{32,16},{48,64},{64,48},{80,96},{96,80},{112,128},{128,112... | collective-permute-start | bytes 786440 | tf_op jit(solution)/shard_map/ppermute | solution.py:348
  103.2 14.5 %collective-permute-start.25 = (f32[16,32,128]{2,1,0:T(8,128)}, f32[16,32,128]{2,1,0:T(8,128)S(1)}, u32[]{:S(2)}, u32[]{:S(2)}) collective-permute-start(f32[16,32,128]{2,1,0:T(8,128)} %copy-done.9), channel_id=1, source_target_pairs={{0,16},{16,0},{32,48},{48,32},{64,80},{80,64},{96,112},{112,96},{1... | collective-permute-start | bytes 786440 | tf_op jit(solution)/shard_map/ppermute | solution.py:348
  105.5 12.2 %collective-permute-start.26 = (f32[16,32,128]{2,1,0:T(8,128)}, f32[16,32,128]{2,1,0:T(8,128)}, u32[]{:S(2)}, u32[]{:S(2)}) collective-permute-start(f32[16,32,128]{2,1,0:T(8,128)} %copy-done.8), channel_id=1, source_target_pairs={{16,32},{32,16},{48,64},{64,48},{80,96},{96,80},{112,128},{128,112... | collective-permute-start | bytes 786440 | tf_op jit(solution)/shard_map/ppermute | solution.py:348
  112.3 1.6 %copy-start.1 = (f32[8,16,32,128]{3,2,1,0:T(8,128)S(1)}, f32[8,16,32,128]{3,2,1,0:T(8,128)}, u32[]{:S(2)}) copy-start(f32[8,16,32,128]{3,2,1,0:T(8,128)} %copy-done) | copy-start | bytes 6291460
  113.9 1.6 %copy-start.5 = (f32[8,16,32,128]{3,2,1,0:T(8,128)S(1)}, f32[8,16,32,128]{3,2,1,0:T(8,128)}, u32[]{:S(2)}) copy-start(f32[8,16,32,128]{3,2,1,0:T(8,128)} %copy-done.4) | copy-start | bytes 6291460
  115.5 2.3 %copy-start.7 = (f32[8,16,32,128]{3,2,1,0:T(8,128)S(1)}, f32[8,16,32,128]{3,2,1,0:T(8,128)}, u32[]{:S(2)}) copy-start(f32[8,16,32,128]{3,2,1,0:T(8,128)} %copy-done.6) | copy-start | bytes 6291460
